TPU v7x, 32 devices: a whole 2x2x4 slice. The times are simulated.
32 devices in a mesh: group: 4 (over z), expert: 8 (over y, x, core).
Axes of the slice: x: 2, y: 2, z: 4, core: 2. Of those that a mesh axis runs over, the one named last changes fastest.
Arguments:
- tokens_in: bfloat16 [16384, 1024], P(('group', 'expert')), may hold values from -6 to 6
- cotangent: bfloat16 [16384, 1024], P(('group', 'expert')), may hold values from -6 to 6
- hash_ids: int32 [16384, 1], P(('group', 'expert')), may hold values from 0 to 7; in each aligned block of 512 rows (0 to 511, 512 to 1023, ...) at most 128 rows name the same one
- norm1_gain: float32 [1024], replicated, may hold values from 0.5 to 1.5
- norm1_bias: float32 [1024], replicated, may hold values from -1 to 1
- w_query: bfloat16 [1024, 1024], replicated, may hold values from -0.25 to 0.25
- w_key: bfloat16 [1024, 1024], replicated, may hold values from -0.1875 to 0.1875
- w_value: bfloat16 [1024, 1024], replicated, may hold values from -0.1875 to 0.1875
- w_output: bfloat16 [1024, 1024], replicated, may hold values from -1.5 to 1.5
- norm2_gain: float32 [1024], replicated, may hold values from 0.5 to 1.5
- norm2_bias: float32 [1024], replicated, may hold values from -1 to 1
- expert_in: bfloat16 [8, 1024, 4096], P('expert'), may hold values from -0.1875 to 0.1875
- expert_out: bfloat16 [8, 4096, 1024], P('expert'), may hold values from -0.125 to 0.125
Outputs:
- result: bfloat16 [16384, 1024], P(('group', 'expert'))
- grad_tokens: bfloat16 [16384, 1024], P(('group', 'expert'))
- grad_norm1_gain: float32 [1024], P(('group', 'expert'))
- grad_norm1_bias: float32 [1024], P(('group', 'expert'))
- grad_w_query: float32 [1024, 1024], P(('group', 'expert'))
- grad_w_key: float32 [1024, 1024], P(('group', 'expert'))
- grad_w_value: float32 [1024, 1024], P(('group', 'expert'))
- grad_w_output: float32 [1024, 1024], P(('group', 'expert'))
- grad_norm2_gain: float32 [1024], P(('group', 'expert'))
- grad_norm2_bias: float32 [1024], P(('group', 'expert'))
- grad_expert_in: float32 [8, 1024, 4096], P('expert', 'group')
- grad_expert_out: float32 [8, 4096, 1024], P('expert', 'group')
Inputs may be any that keep to these rules, and one draw needn't show every extreme that they name: `hash_ids`: each token's expert; among the 512 rows of one device at most 128 name one expert, a bound that some block reaches.
All inputs are finite; a program needn't handle non-finite values.
Results may differ from a plain program's by a relative error of at most 0.028.
Values may be sent and summed in bfloat16 or wider, within the bound.
No kernel may reach another device: no remote copies, remote signals or barrier semaphores. Data moves between devices by JAX's collectives and lax.ppermute only.
A program may use at most 320 MiB of HBM per device.

v0:
```python
import functools
import math

import jax
import jax.numpy as jnp
from jax import lax
from jax.experimental import pallas as pl
from jax.experimental.pallas import tpu as pltpu
from jax.sharding import PartitionSpec as P

HEADS = 16
PROMPT_DEV = 128
CONT_DEV = 384


norm_eps = 1e-05
masked_score = -1e30
bf16 = jnp.bfloat16
f32 = jnp.float32
MIB = 1 << 20
share = 0.05


def swapped(block, axis, mask):
    return lax.ppermute(block, axis, [(i, i ^ mask) for i in range(lax.axis_size(axis))])


def rounded(values):
    return values.astype(bf16)


def normalize(values, gain, shift):
    average = jnp.mean(values, axis=-1, keepdims=True)
    centered = values - average
    variance = jnp.mean(centered * centered, axis=-1, keepdims=True)
    inverse = lax.rsqrt(variance + norm_eps)
    normed = centered * inverse
    return (normed * gain + shift, normed, inverse)


def norm_back(grad_out, gain, normed, inverse):
    scaled = grad_out * gain
    first_mean = jnp.mean(scaled, axis=-1, keepdims=True)
    second = jnp.mean(scaled * normed, axis=-1, keepdims=True)
    return inverse * (scaled - first_mean - normed * second)


def matmul(a, b, kind=f32):
    return jnp.dot(a, b, preferred_element_type=f32).astype(kind)


def matmul_nt(a, b, kind=f32):
    return lax.dot_general(a, b, (((1,), (1,)), ((), ())), preferred_element_type=f32).astype(kind)


def matmul_tn(a, b, kind=f32):
    return lax.dot_general(a, b, (((0,), (0,)), ((), ())), preferred_element_type=f32).astype(kind)


def outer_bits(size):
    return range(size.bit_length() - 2, 0, -1)


def gather_relative(block, axis, more):
    size = lax.axis_size(axis)
    pieces = {0: block}
    ready, last = [0], []
    while ready:
        fresh = {}
        for r in ready:
            for bit in outer_bits(size):
                if r ^ (1 << bit) not in pieces and r ^ (1 << bit) not in fresh:
                    fresh[r ^ (1 << bit)] = swapped(pieces[r], axis, 1 << bit)
        fresh, more = lax.optimization_barrier((fresh, more))
        pieces.update(fresh)
        ready, last = list(fresh), list(fresh.values()) or last
    near = sorted(pieces)
    for r in near:
        pieces[r ^ 1] = swapped(pieces[r], axis, 1)
    order = near + [r ^ 1 for r in near]
    return [pieces[r] for r in order], order, more, last


def scatter_relative(near, far, axis):
    size = lax.axis_size(axis)
    got = yield swapped(far, axis, 1)
    both = added(near, got)
    count = size // 2
    rows = both.shape[1] // count
    pieces = {2 * i: rounded(both[:, i * rows : (i + 1) * rows]) for i in range(count)}
    bits = list(outer_bits(size))
    for level in range(len(bits), 0, -1):
        sent, spans = [], []
        for r in [r for r in sorted(pieces) if bin(r).count("1") == level]:
            ways = [bit for bit in bits if r >> bit & 1]
            if rows % (16 * len(ways)):
                ways = ways[:1]
            part = rows // len(ways)
            piece = pieces.pop(r)
            for i, bit in enumerate(ways):
                span = (i * part, (i + 1) * part)
                sent.append(swapped(piece[:, span[0] : span[1]], axis, 1 << bit))
                spans.append((r ^ (1 << bit), span))
        gots = yield sent
        for r in sorted(pieces):
            total = pieces[r].astype(f32)
            for got, (target, span) in zip(gots, spans):
                if target == r:
                    outside = ((0, 0), (span[0], rows - span[1]), (0, 0))
                    total = total + jnp.pad(got.astype(f32), outside)
            pieces[r] = rounded(total)
    return pieces[0]


def halved(blocks, place, axis, bit):
    own = (lax.axis_index(axis) >> bit) & 1
    return (
        lax.dynamic_index_in_dim(blocks, own, place, keepdims=False),
        lax.dynamic_index_in_dim(blocks, 1 - own, place, keepdims=False),
    )


def added(keep, got):
    return keep.astype(f32) + got.astype(f32)


def places_of(bits, bit, value):
    rest = [other for other in bits if other != bit]
    weight = {other: 1 << (len(bits) - 1 - i) for i, other in enumerate(bits)}
    places = []
    for number in range(1 << len(rest)):
        place = value * weight[bit]
        for i, other in enumerate(rest):
            place = place + (number >> (len(rest) - 1 - i) & 1) * weight[other]
        places.append(place)
    return places


def halve_kernel(lefts, bits, own_ref, *refs):
    sets = len(lefts)
    for k, (left, bit) in enumerate(zip(lefts, bits)):
        keep_ref, got_ref = refs[2 * k : 2 * k + 2]
        outs = refs[2 * sets + 2 * k : 2 * sets + 2 * k + 2]
        own = (own_ref[0] >> bit) & 1
        for ref, value in zip(outs, (own, 1 - own)):
            for i, place in enumerate(places_of(left, bit, value)):
                for j in range(ref.shape[1]):
                    ref[0, j, i] = rounded(added(keep_ref[0, j, place], got_ref[0, j, place]))


def halve(number, states, bits):
    _, groups, count, rows, width = states[0][0].shape
    shape = (2, groups, count // 2, rows, width)
    came = lambda first: pl.BlockSpec(
        (1, groups, count, rows, width), lambda i: (first + i if first else i, 0, 0, 0, 0)
    )
    out = pl.BlockSpec((1, groups, count // 2, rows, width), lambda i: (i, 0, 0, 0, 0))
    size = 2 * math.prod(shape)
    outs = pl.pallas_call(
        functools.partial(halve_kernel, [state[3] for state in states], bits),
        grid=(2,),
        in_specs=[pl.BlockSpec(memory_space=pltpu.SMEM)]
        + [came(state[2]) for state in states for _ in range(2)],
        out_specs=[out] * (2 * len(states)),
        out_shape=[jax.ShapeDtypeStruct(shape, bf16)] * (2 * len(states)),
        compiler_params=params("arbitrary"),
        cost_estimate=cost(2 * size, 12 * size),
        name="halve",
    )(number, *[value for state in states for value in state[:2]])
    return list(zip(outs[::2], outs[1::2]))


def turn_kernel(own_ref, *refs):
    (*sets, own_out_ref, send_ref) = refs
    own = own_ref[0] & 1
    start = 0
    for keep_ref, got_ref in zip(sets[::2], sets[1::2]):
        for i in range(keep_ref.shape[0]):
            for j in range(keep_ref.shape[1] // 2):
                for ref, value in ((own_out_ref, own), (send_ref, 1 - own)):
                    place = 2 * j + value
                    ref[start + i, j] = rounded(added(keep_ref[i, place, 0], got_ref[i, place, 0]))
        start += keep_ref.shape[0]


def turn(number, sets):
    _, groups, _, rows, width = sets[0].shape
    shape = (4, groups // 2, rows, width)
    return pl.pallas_call(
        turn_kernel,
        in_specs=[pl.BlockSpec(memory_space=pltpu.SMEM)]
        + [pl.BlockSpec(memory_space=pltpu.VMEM)] * len(sets),
        out_specs=[pl.BlockSpec(memory_space=pltpu.VMEM)] * 2,
        out_shape=[jax.ShapeDtypeStruct(shape, bf16)] * 2,
        compiler_params=params(),
        cost_estimate=cost(8 * sets[0].size, 8 * sets[0].size),
        name="turn",
    )(number, *sets)


def weight_chain(keep, send, marks):
    bits = list(range(1, lax.axis_size("expert").bit_length() - 1))
    number = lax.axis_index("expert")[None]
    got = yield swapped(send, "expert", 1)
    states = [(keep, got, 0, bits[::-1]), (keep, got, 2, bits[::-1])]
    for pair in zip(bits, bits[::-1]):
        halves = halve(number, states, pair)
        marks.append(halves[0][0])
        gots = yield [swapped(send, "expert", 1 << bit) for bit, (_, send) in zip(pair, halves)]
        states = [
            (keep, got, 0, [other for other in state[3] if other != bit])
            for state, bit, (keep, _), got in zip(states, pair, halves, gots)
        ]
    keep, send = turn(
        lax.axis_index("group")[None], [value for state in states for value in state[:2]]
    )
    marks.append(keep)
    got = yield swapped(send, "group", 1)
    both = added(keep, got)
    bits = list(range(1, lax.axis_size("group").bit_length() - 1))
    both = both.reshape((4,) + (2,) * len(bits) + both.shape[-2:])
    left = bits[::-1]
    for bit in bits:
        keep, send = halved(rounded(both), 1 + left.index(bit), "group", bit)
        left.remove(bit)
        got = yield swapped(send, "group", 1 << bit)
        both = added(keep, got)
    return [both[i] for i in range(both.shape[0])]


def moved_on(chain, came):
    try:
        return chain.send(came), None
    except StopIteration as stop:
        return None, stop.value


def vector_sums(vectors):
    for axis in ("expert", "group"):
        for bit in range(lax.axis_size(axis).bit_length() - 1):
            got = yield swapped(vectors, axis, 1 << bit)
            vectors = vectors + got
    part = vectors.shape[1] // (lax.axis_size("group") * lax.axis_size("expert"))
    place = lax.axis_index("group") * lax.axis_size("expert") + lax.axis_index("expert")
    return lax.dynamic_slice_in_dim(vectors, place * part, part, axis=1)


def params(*semantics):
    return pltpu.CompilerParams(dimension_semantics=semantics, vmem_limit_bytes=60 * MIB)


def cost(flops, total_bytes, exps=0):
    return pl.CostEstimate(
        flops=int(flops * share), bytes_accessed=int(total_bytes * share), transcendentals=int(exps * share)
    )


def logistic(values):
    return 0.5 * jnp.tanh(0.5 * values) + 0.5


def back_kernel(cot_ref, wout_ref, out_ref):
    out_ref[...] = matmul_nt(cot_ref[...], wout_ref[0], bf16)


def expert_back(cot, expert_out):
    count, width = cot.shape
    ff = expert_out.shape[1]
    block = 1024
    return pl.pallas_call(
        back_kernel,
        grid=(ff // block,),
        in_specs=[
            pl.BlockSpec((count, width), lambda j: (0, 0)),
            pl.BlockSpec((1, block, width), lambda j: (0, j, 0)),
        ],
        out_specs=pl.BlockSpec((count, block), lambda j: (0, j)),
        out_shape=jax.ShapeDtypeStruct((count, ff), bf16),
        compiler_params=params("arbitrary"),
        cost_estimate=cost(2 * count * width * ff, 2 * count * ff + 2 * width * ff),
        name="expert_back",
    )(cot, expert_out)


def front_kernel(parts, rows_ref, gh_ref, win_ref, hidden_ref, pre_ref, out_ref, acc_ref):
    step = pl.program_id(0)
    count = rows_ref.shape[0] // parts

    @pl.when(step == 0)
    def _():
        acc_ref[...] = jnp.zeros_like(acc_ref)

    first = lambda i: matmul(rows_ref[i * count : (i + 1) * count, :], win_ref[0])
    pre = first(0)
    for i in range(parts):
        later = first(i + 1) if i + 1 < parts else None
        here = pl.ds(i * count, count)
        sig = logistic(pre)
        hidden = pre * sig
        hidden_ref[here, :] = rounded(hidden)
        grad_pre = rounded(gh_ref[here, :].astype(f32) * sig * (1.0 + pre - hidden))
        pre_ref[here, :] = grad_pre
        acc_ref[here, :] += matmul_nt(grad_pre, win_ref[0])
        pre = later

    @pl.when(step == pl.num_programs(0) - 1)
    def _():
        out_ref[...] = rounded(acc_ref[...])


def expert_front(rows, grad_hidden, expert_in):
    count, width = rows.shape
    ff = expert_in.shape[2]
    block = 1024
    whole = pl.BlockSpec((count, width), lambda j: (0, 0))
    part = pl.BlockSpec((count, block), lambda j: (0, j))
    return pl.pallas_call(
        functools.partial(front_kernel, 4),
        grid=(ff // block,),
        in_specs=[whole, part, pl.BlockSpec((1, width, block), lambda j: (0, 0, j))],
        out_specs=[part, part, whole],
        out_shape=[
            jax.ShapeDtypeStruct((count, ff), bf16),
            jax.ShapeDtypeStruct((count, ff), bf16),
            jax.ShapeDtypeStruct((count, width), bf16),
        ],
        scratch_shapes=[pltpu.VMEM((count, width), f32)],
        compiler_params=params("arbitrary"),
        cost_estimate=cost(4 * count * width * ff, 6 * count * ff + 2 * width * ff, count * ff),
        name="expert_front",
    )(rows, grad_hidden, expert_in)


def produce_kernel(hidden_ref, wout_ref, out_ref, acc_ref):
    step = pl.program_id(0)
    part = matmul(hidden_ref[...], wout_ref[0])

    @pl.when(step == 0)
    def _():
        acc_ref[...] = part

    @pl.when(step > 0)
    def _():
        acc_ref[...] += part

    @pl.when(step == pl.num_programs(0) - 1)
    def _():
        out_ref[...] = rounded(acc_ref[...])


def expert_produce(hidden, expert_out):
    count, ff = hidden.shape
    width = expert_out.shape[2]
    block = 1024
    return pl.pallas_call(
        produce_kernel,
        grid=(ff // block,),
        in_specs=[
            pl.BlockSpec((count, block), lambda j: (0, j)),
            pl.BlockSpec((1, block, width), lambda j: (0, j, 0)),
        ],
        out_specs=pl.BlockSpec((count, width), lambda j: (0, 0)),
        out_shape=jax.ShapeDtypeStruct((count, width), bf16),
        scratch_shapes=[pltpu.VMEM((count, width), f32)],
        compiler_params=params("arbitrary"),
        cost_estimate=cost(2 * count * width * ff, 2 * count * ff + 2 * width * ff),
        name="expert_produce",
    )(hidden, expert_out)


def in_kernel(
    _, win_ref, wout_ref, own_rows_ref, own_pre_ref, near_rows_ref, near_ref, rows_ref, far_ref,
    in_ref, near_hidden_ref, hidden_ref, in_sum,
):
    step = pl.program_id(0)

    def shard(rows, cot):
        pre = matmul(rows, win_ref[0])
        grad_hidden = matmul_nt(cot, wout_ref[0])
        sig = logistic(pre)
        hidden = pre * sig
        grad_pre = rounded(grad_hidden * sig * (1.0 + pre - hidden))
        return rounded(hidden), matmul_tn(rows, grad_pre)

    @pl.when(step == 0)
    def _():
        rows = near_rows_ref[0]
        near_hidden_ref[...], inner = shard(rows, near_ref[...].reshape(rows.shape))
        in_sum[...] = matmul_tn(own_rows_ref[...], own_pre_ref[...]) + inner

    rows = rows_ref[0]
    hidden_ref[0], inner = shard(rows, far_ref[...].reshape(rows.shape))
    in_sum[...] += inner

    @pl.when(step == pl.num_programs(0) - 1)
    def _():
        in_ref[...] = rounded(in_sum[...]).reshape(in_ref.shape)


def in_sums(number, half, expert_in, expert_out, own, rows, near, far):
    groups, count, width = rows.shape
    sources, _, slots, _ = near.shape
    part = expert_in.shape[2] // groups
    block = part // 2
    column = lambda j, w: 2 * w[0] + half
    return pl.pallas_call(
        in_kernel,
        grid_spec=pltpu.PrefetchScalarGridSpec(
            num_scalar_prefetch=1,
            grid=(groups - 2,),
            in_specs=[
                pl.BlockSpec((1, width, block), lambda j, w: (0, 0, column(j, w))),
                pl.BlockSpec((1, block, width), lambda j, w: (0, column(j, w), 0)),
                pl.BlockSpec((count, width), lambda j, w: (0, 0)),
                pl.BlockSpec((count, block), lambda j, w: (0, column(j, w))),
                pl.BlockSpec((1, count, width), lambda j, w: (w[1], 0, 0)),
                pl.BlockSpec((sources, 1, slots, width), lambda j, w: (0, 0, 0, 0)),
                pl.BlockSpec((1, count, width), lambda j, w: (w[2 + j], 0, 0)),
                pl.BlockSpec((sources, 1, slots, width), lambda j, w: (0, 1 + j, 0, 0)),
            ],
            out_specs=[
                pl.BlockSpec((groups, width // groups, block), lambda j, w: (0, 0, 0)),
                pl.BlockSpec((count, block), lambda j, w: (0, 0)),
                pl.BlockSpec((1, count, block), lambda j, w: (j, 0, 0)),
            ],
            scratch_shapes=[pltpu.VMEM((width, block), f32)],
        ),
        out_shape=[
            jax.ShapeDtypeStruct((groups, width // groups, block), bf16),
            jax.ShapeDtypeStruct((count, block), bf16),
            jax.ShapeDtypeStruct((groups - 2, count, block), bf16),
        ],
        compiler_params=params("arbitrary"),
        cost_estimate=cost(6 * count * width * block * groups, 16e6, count * block * groups),
        name="in_sums",
    )(number, expert_in, expert_out, *own, rows, near, rows, far)


def out_kernel(_, hidden_ref, cot_ref, near_ref, far_ref, *refs):
    out_ref, total = refs[-2:]
    hiddens = refs[:-2]
    block = total.shape[0] // 2
    step = pl.program_id(0)
    cot = cot_ref[...]

    @pl.when(step == 0)
    def _():
        total[...] = matmul_tn(hidden_ref[...], cot)
        near = near_ref[...].reshape(cot.shape)
        for half in range(2):
            here = pl.ds(half * block, block)
            total[here, :] += matmul_tn(hiddens[2 * half][...], near)

    far = far_ref[...].reshape(cot.shape)
    for half in range(2):
        here = pl.ds(half * block, block)
        total[here, :] += matmul_tn(hiddens[2 * half + 1][0], far)

    @pl.when(step == pl.num_programs(0) - 1)
    def _():
        out_ref[0] = total[...]


def out_sums(number, own, near, far, hiddens):
    hidden, cot = own
    count, width = cot.shape
    sources, _, slots, _ = near.shape
    groups = number.shape[0]
    part = hidden.shape[1] // groups
    near_hidden = pl.BlockSpec((count, part // 2), lambda j, w: (0, 0))
    far_hidden = pl.BlockSpec((1, count, part // 2), lambda j, w: (j, 0, 0))
    return pl.pallas_call(
        out_kernel,
        grid_spec=pltpu.PrefetchScalarGridSpec(
            num_scalar_prefetch=1,
            grid=(groups - 2,),
            in_specs=[
                pl.BlockSpec((count, part), lambda j, w: (0, w[0])),
                pl.BlockSpec((count, width), lambda j, w: (0, 0)),
                pl.BlockSpec((sources, 1, slots, width), lambda j, w: (0, 0, 0, 0)),
                pl.BlockSpec((sources, 1, slots, width), lambda j, w: (0, 1 + j, 0, 0)),
            ]
            + [near_hidden, far_hidden] * 2,
            out_specs=pl.BlockSpec((1, part, width), lambda j, w: (0, 0, 0)),
            scratch_shapes=[pltpu.VMEM((part, width), f32)],
        ),
        out_shape=jax.ShapeDtypeStruct((1, part, width), f32),
        compiler_params=params("arbitrary"),
        cost_estimate=cost(2 * count * width * part * groups, 16e6),
        name="out_sums",
    )(number, hidden, cot, near, far, *hiddens)


def lay_kernel(*refs):
    gots, out_ref = refs[:-1], refs[-1]
    block = gots[0].shape[2]
    for i in range(gots[0].shape[0]):
        for j, ref in enumerate(gots):
            start = (i * len(gots) + j) * block
            out_ref[0, :, start : start + block] = ref[i].astype(f32)


def lay_out(gots):
    groups, rows, block = gots[0].shape
    tall = 64
    width = groups * block * len(gots)
    return pl.pallas_call(
        lay_kernel,
        grid=(rows // tall,),
        in_specs=[pl.BlockSpec((groups, tall, block), lambda j: (0, j, 0))] * len(gots),
        out_specs=pl.BlockSpec((1, tall, width), lambda j: (0, j, 0)),
        out_shape=jax.ShapeDtypeStruct((1, rows, width), f32),
        compiler_params=params("arbitrary"),
        cost_estimate=cost(rows * width, 6 * rows * width),
        name="lay_out",
    )(*gots)


def spread_kernel(first, _, ids_ref, values_ref, *refs):
    out_ref = refs[-1]
    experts, _, capacity, width = out_ref.shape

    def spread():
        rows = ids_ref.shape[2]
        ids = ids_ref[0]
        number = lax.broadcasted_iota(jnp.int32, (experts, rows), 0)
        routed = jnp.where(number == ids, f32(1.0), f32(0.0))
        square = (rows, rows)
        before = lax.broadcasted_iota(jnp.int32, square, 0) <= lax.broadcasted_iota(
            jnp.int32, square, 1
        )
        running = matmul(rounded(routed), rounded(jnp.where(before, f32(1.0), f32(0.0))))
        rank = jnp.sum(running * routed, axis=0, keepdims=True).astype(jnp.int32) - 1
        slot = ids * capacity + rank
        places = lax.broadcasted_iota(jnp.int32, (experts * capacity, rows), 0)
        onehot = rounded(jnp.where(places == slot, f32(1.0), f32(0.0)))
        out = matmul(onehot, values_ref[0, :, :width], bf16)
        out_ref[...] = out.reshape(out_ref.shape)

    if first:
        step = pl.program_id(0)

        @pl.when(step == 0)
        def _():
            out_ref[...] = refs[0][...].reshape(out_ref.shape)

        pl.when(step > 0)(spread)
    else:
        spread()


def spread_rows(numbers, ids, values, experts, first=None):
    _, rows, columns = values.shape
    width = columns - 128
    capacity = 2 * rows // experts
    start = 0 if first is None else 1
    count = numbers.shape[0] + start
    which = lambda j, w: w[jnp.maximum(j - start, 0)]
    specs = [
        pl.BlockSpec((1, 1, rows), lambda j, w: (which(j, w), 0, 0)),
        pl.BlockSpec((1, rows, columns), lambda j, w: (which(j, w), 0, 0)),
    ]
    operands = [ids, values]
    if start:
        specs.append(pl.BlockSpec(first.shape, lambda j, w: (0, 0)))
        operands.append(first)
    return pl.pallas_call(
        functools.partial(spread_kernel, start),
        grid_spec=pltpu.PrefetchScalarGridSpec(
            num_scalar_prefetch=1,
            grid=(count,),
            in_specs=specs,
            out_specs=pl.BlockSpec((experts, 1, capacity, width), lambda j, w: (0, j, 0, 0)),
        ),
        out_shape=jax.ShapeDtypeStruct((experts, count, capacity, width), bf16),
        compiler_params=params("arbitrary"),
        cost_estimate=cost(2 * count * experts * capacity * rows * width, 8e6),
        name="spread_rows",
    )(numbers, *operands)


def project_kernel(count, gain_ref, bias_ref, wq_ref, wk_ref, wv_ref, *refs):
    pieces, (in_ref, q_ref, k_ref, v_ref, scratch) = refs[:count], refs[count:]

    @pl.when(pl.program_id(0) == 0)
    def _():
        start = 0
        for ref in pieces:
            end = start + ref.shape[0]
            values = normalize(ref[...].astype(f32), gain_ref[...], bias_ref[...])[0]
            scratch[start:end, :] = rounded(values)
            start = end
        in_ref[...] = scratch[...]

    first, last = pieces[0].shape[0], pieces[-1].shape[0]
    size = scratch.shape[0]
    q_ref[:first, :] = matmul(scratch[:first, :], wq_ref[...], bf16)
    q_ref[first:, :] = matmul(scratch[size - last :, :], wq_ref[...], bf16)
    k_ref[...] = matmul(scratch[...], wk_ref[...], bf16)
    v_ref[...] = matmul(scratch[...], wv_ref[...], bf16)


def project(pieces, gain, shift, w_query, w_key, w_value):
    width = gain.shape[0]
    size = sum(p.shape[0] for p in pieces)
    own = pieces[0].shape[0] + pieces[-1].shape[0]
    block = 512
    whole = lambda rows: pl.BlockSpec((rows, width), lambda j: (0, 0))
    weights = pl.BlockSpec((width, block), lambda j: (0, j))
    columns = lambda rows: pl.BlockSpec((rows, block), lambda j: (0, j))
    return pl.pallas_call(
        functools.partial(project_kernel, len(pieces)),
        grid=(width // block,),
        in_specs=[whole(1), whole(1)] + [weights] * 3 + [whole(p.shape[0]) for p in pieces],
        out_specs=[whole(size), columns(own), columns(size), columns(size)],
        out_shape=[jax.ShapeDtypeStruct((rows, width), bf16) for rows in (size, own, size, size)],
        scratch_shapes=[pltpu.VMEM((size, width), bf16)],
        compiler_params=params("arbitrary"),
        cost_estimate=cost(4 * size * width * width, 8 * size * width + 4 * width * width),
        name="project",
    )(gain[None], shift[None], w_query, w_key, w_value, *pieces)


def weights_kernel(odd_ref, *refs):
    attended_ref, others_ref, grad_ref, dq_ref, *backs = refs[:-2]
    keep_ref, send_ref = refs[-2:]
    size = others_ref.shape[0]
    totals = [
        matmul_tn(attended_ref[...], grad_ref[...]),
        matmul_tn(others_ref[:PROMPT_DEV, :], dq_ref[:PROMPT_DEV, :])
        + matmul_tn(others_ref[size - CONT_DEV :, :], dq_ref[PROMPT_DEV:, :]),
    ]
    for i in range(2):
        total, start = None, 0
        for ref in backs:
            count = ref.shape[1]
            part = matmul_tn(others_ref[start : start + count, :], ref[i])
            total = part if total is None else total + part
            start += count
        totals.append(total)
    half, rows = keep_ref.shape[2:4]

    def put(even_ref, odd_ref):
        for i, total in enumerate(totals):
            for j in range(half):
                start = 2 * j * rows
                even_ref[i, 0, j] = rounded(total[start : start + rows])
                odd_ref[i, 0, j] = rounded(total[start + rows : start + 2 * rows])

    @pl.when(odd_ref[0] == 0)
    def _():
        put(keep_ref, send_ref)

    @pl.when(odd_ref[0] != 0)
    def _():
        put(send_ref, keep_ref)


def weight_parts(odd, attended, others_in, grad_attn, grad_queries, backs, groups, experts):
    width = attended.shape[1]
    part = width // groups
    rows = part // experts
    left = lambda m: pl.BlockSpec((m.shape[0], part), lambda j: (0, j))
    whole = lambda m: pl.BlockSpec(m.shape, lambda j: (0,) * m.ndim)
    lefts, rights = [attended, others_in], [grad_attn, grad_queries, *backs]
    shape = (4, groups, experts // 2, rows, width)
    out = pl.BlockSpec((4, 1) + shape[2:], lambda j: (0, j, 0, 0, 0))
    return pl.pallas_call(
        weights_kernel,
        grid=(groups,),
        in_specs=[pl.BlockSpec(memory_space=pltpu.SMEM)]
        + [left(m) for m in lefts]
        + [whole(m) for m in rights],
        out_specs=[out, out],
        out_shape=[jax.ShapeDtypeStruct(shape, bf16)] * 2,
        compiler_params=params("arbitrary"),
        cost_estimate=cost(10e9, 30e6),
        name="weight_parts",
    )(odd, *lefts, *rights)


def resid_back_kernel(
    got_ref, spread_ref, resid_ref, gain_ref, cot_ref, wo_ref, grad_ref, attn_ref, attended_ref, sums_ref
):
    grad = matmul_tn(spread_ref[...], got_ref[...])
    _, normed, inverse = normalize(resid_ref[...], 1.0, 0.0)
    sums = jnp.concatenate(
        [jnp.sum(grad * normed, axis=0, keepdims=True), jnp.sum(grad, axis=0, keepdims=True)]
    )

    @pl.when(pl.program_id(0) == 0)
    def _():
        sums_ref[...] = sums

    @pl.when(pl.program_id(0) > 0)
    def _():
        sums_ref[...] += sums

    total = cot_ref[...].astype(f32) + norm_back(grad, gain_ref[...], normed, inverse)
    grad_ref[...] = total
    attn_ref[...] = rounded(total)
    attended_ref[...] = matmul_nt(rounded(total), wo_ref[...], bf16)


def resid_back(got, spread, residual, gain, cotangent, w_output):
    rows, width = residual.shape
    slots = got.shape[0]
    block = 256
    whole = lambda count: pl.BlockSpec((count, width), lambda j: (0, 0))
    part = pl.BlockSpec((block, width), lambda j: (j, 0))
    return pl.pallas_call(
        resid_back_kernel,
        grid=(rows // block,),
        in_specs=[
            whole(slots),
            pl.BlockSpec((slots, block), lambda j: (0, j)),
            part,
            whole(1),
            part,
            whole(width),
        ],
        out_specs=[part, part, part, whole(2)],
        out_shape=[
            jax.ShapeDtypeStruct((rows, width), f32),
            jax.ShapeDtypeStruct((rows, width), bf16),
            jax.ShapeDtypeStruct((rows, width), bf16),
            jax.ShapeDtypeStruct((2, width), f32),
        ],
        compiler_params=params("arbitrary"),
        cost_estimate=cost(2 * rows * width * (slots + width), 16 * rows * width),
        name="resid_back",
    )(got, spread, residual, gain[None], cotangent, w_output)


def input_back_kernel(
    prompt_ref, own_ref, near_ref, dq_ref, wq_ref, wk_ref, wv_ref, x_ref, gain_ref, resid_ref,
    out_ref, sums_ref, dk_ref, dv_ref,
):
    step = pl.program_id(0)
    block = dk_ref.shape[0]
    count = prompt_ref.shape[1]

    def put(first):
        for i, ref in enumerate((dk_ref, dv_ref)):
            start, size = (0, block - count) if first else (block - count, block)
            if first:
                ref[:count, :] = prompt_ref[i]
            here = pl.ds(start, size)
            ref[block - size :, :] = rounded(added(own_ref[i, here, :], near_ref[i, here, :]))

    pl.when(step == 0)(lambda: put(True))
    pl.when(step > 0)(lambda: put(False))
    grad = matmul_nt(dq_ref[...], wq_ref[...])
    grad = grad + matmul_nt(dk_ref[...], wk_ref[...])
    grad = grad + matmul_nt(dv_ref[...], wv_ref[...])
    _, normed, inverse = normalize(x_ref[...].astype(f32), 1.0, 0.0)
    sums = jnp.concatenate(
        [jnp.sum(grad * normed, axis=0, keepdims=True), jnp.sum(grad, axis=0, keepdims=True)]
    )

    @pl.when(step == 0)
    def _():
        sums_ref[...] = sums

    @pl.when(step > 0)
    def _():
        sums_ref[...] += sums

    out_ref[...] = rounded(resid_ref[...] + norm_back(grad, gain_ref[...], normed, inverse))


def input_back(prompt, own, near, grad_queries, w_query, w_key, w_value, tokens, gain, grad_resid):
    rows, width = tokens.shape
    block = rows // 2
    whole = lambda count: pl.BlockSpec((count, width), lambda j: (0, 0))
    part = pl.BlockSpec((block, width), lambda j: (j, 0))
    pair = lambda count: pl.BlockSpec((2, count, width), lambda j: (0, 0, 0))
    return pl.pallas_call(
        input_back_kernel,
        grid=(rows // block,),
        in_specs=[
            pair(PROMPT_DEV),
            pair(CONT_DEV),
            pair(CONT_DEV),
            part,
            whole(width),
            whole(width),
            whole(width),
            part,
            whole(1),
            part,
        ],
        out_specs=[part, whole(2)],
        out_shape=[
            jax.ShapeDtypeStruct((rows, width), bf16),
            jax.ShapeDtypeStruct((2, width), f32),
        ],
        scratch_shapes=[pltpu.VMEM((block, width), bf16)] * 2,
        compiler_params=params("arbitrary"),
        cost_estimate=cost(6 * rows * width * width, 20 * rows * width),
        name="input_back",
    )(prompt, own, near, grad_queries, w_query, w_key, w_value, tokens, gain[None], grad_resid)


def head_stack(block):
    first = lax.broadcasted_iota(jnp.int32, block.shape, 1) < block.shape[1] // 2
    zero = jnp.zeros_like(block)
    return jnp.concatenate([jnp.where(first, block, zero), jnp.where(first, zero, block)])


def head_merge(turned):
    half, rows = turned.shape[0] // 2, turned.shape[1] // 2
    return jnp.concatenate([turned[:half, :rows], turned[half:, rows:]]).T


def chunk_scores(chunk, keys, stack, near_bias, bias_ref, prompt_len):
    scores = matmul_nt(keys, stack)
    if chunk == 0:
        bias = bias_ref[...]
        return scores + jnp.concatenate([bias, bias], axis=1)
    tri = (PROMPT_DEV, PROMPT_DEV)
    after = lax.broadcasted_iota(jnp.int32, tri, 0) > lax.broadcasted_iota(jnp.int32, tri, 1)
    diag = jnp.where(after, f32(masked_score), f32(0.0))
    last = keys.shape[0] - PROMPT_DEV
    near_end = prompt_len + CONT_DEV
    pieces = [scores[:prompt_len], scores[prompt_len:near_end] + near_bias]
    if last > near_end:
        pieces.append(scores[near_end:last])
    pieces.append(scores[last:] + jnp.concatenate([diag, diag], axis=1))
    return jnp.concatenate(pieces)


def chunk_keys(chunk, prompt_len):
    return prompt_len if chunk == 0 else prompt_len + CONT_DEV + PROMPT_DEV * chunk


def attend_kernel(prompt_len, near_ref, q_ref, k_ref, v_ref, bias_ref, out_ref, log_ref):
    scale = bf16(1.0 / math.sqrt(q_ref.shape[1] // 2))
    chunks = q_ref.shape[0] // PROMPT_DEV

    def scores_of(chunk):
        stack = head_stack(q_ref[pl.ds(chunk * PROMPT_DEV, PROMPT_DEV), :] * scale)
        keys = k_ref[: chunk_keys(chunk, prompt_len), :]
        return chunk_scores(chunk, keys, stack, near_ref[0], bias_ref, prompt_len)

    scores = scores_of(0)
    for chunk in range(chunks):
        rows = pl.ds(chunk * PROMPT_DEV, PROMPT_DEV)
        size = chunk_keys(chunk, prompt_len)
        later = scores_of(chunk + 1) if chunk + 1 < chunks else None
        top = jnp.max(scores, axis=0, keepdims=True)
        weights = jnp.exp(scores - top)
        total = jnp.sum(weights, axis=0, keepdims=True)
        mixed = matmul_tn(v_ref[:size, :], rounded(weights)) / total
        out_ref[rows, :] = rounded(head_merge(mixed))
        log_ref[0, chunk : chunk + 1, :] = top + jnp.log(total)
        scores = later


def attend_back_kernel(
    prompt_len,
    near_ref,
    q_ref,
    k_ref,
    v_ref,
    bias_ref,
    log_ref,
    out_ref,
    grad_ref,
    dq_ref,
    first_ref,
    second_ref,
    near_out_ref,
    own_ref,
    dk_ref,
    dv_ref,
):
    scale = 1.0 / math.sqrt(q_ref.shape[1] // 2)
    half = q_ref.shape[1] // 2
    dk_ref[...] = jnp.zeros_like(dk_ref)
    dv_ref[...] = jnp.zeros_like(dv_ref)
    for chunk in range(q_ref.shape[0] // PROMPT_DEV):
        rows = pl.ds(chunk * PROMPT_DEV, PROMPT_DEV)
        size = chunk_keys(chunk, prompt_len)
        stack = head_stack(q_ref[rows, :] * bf16(scale))
        grad = grad_ref[rows, :]
        grad_stack = head_stack(grad)
        product = (grad.astype(f32) * out_ref[rows, :].astype(f32)).T
        inner = jnp.concatenate(
            [
                jnp.sum(product[:half], axis=0, keepdims=True),
                jnp.sum(product[half:], axis=0, keepdims=True),
            ],
            axis=1,
        )
        keys = k_ref[:size, :]
        scores = chunk_scores(chunk, keys, stack, near_ref[0], bias_ref, prompt_len)
        weights = jnp.exp(scores - log_ref[0, chunk : chunk + 1, :])
        dv_ref[:size, :] += matmul(rounded(weights), grad_stack)
        grad_prob = matmul_nt(v_ref[:size, :], grad_stack)
        grad_score = rounded(weights * (grad_prob - inner))
        dk_ref[:size, :] += matmul(grad_score, stack)
        dq_ref[rows, :] = rounded(head_merge(matmul_tn(keys, grad_score)) * scale)
    start = 0
    for ref in (first_ref, second_ref, near_out_ref, own_ref):
        count = ref.shape[1]
        ref[0] = rounded(dk_ref[start : start + count, :])
        ref[1] = rounded(dv_ref[start : start + count, :])
        start += count


def attend(near_bias, queries, keys, values, bias):
    rows, width = queries.shape
    size = keys.shape[0]
    prompt_len = bias.shape[0]
    lanes = 2 * width // HEADS
    pairs = HEADS // 2
    chunks = rows // PROMPT_DEV
    block = lambda count: pl.BlockSpec((count, lanes), lambda j: (0, j))
    return pl.pallas_call(
        functools.partial(attend_kernel, prompt_len),
        grid=(pairs,),
        in_specs=[
            pl.BlockSpec(memory_space=pltpu.SMEM),
            block(rows),
            block(size),
            block(size),
            pl.BlockSpec((prompt_len, PROMPT_DEV), lambda j: (0, 0)),
        ],
        out_specs=[
            block(rows),
            pl.BlockSpec((1, chunks, 2 * PROMPT_DEV), lambda j: (j, 0, 0)),
        ],
        out_shape=[
            jax.ShapeDtypeStruct((rows, width), bf16),
            jax.ShapeDtypeStruct((pairs, chunks, 2 * PROMPT_DEV), f32),
        ],
        compiler_params=params("arbitrary"),
        cost_estimate=cost(16 * rows * size * width, 4 * (rows + size) * width, rows * size * HEADS),
        name="attend",
    )(near_bias, queries, keys, values, bias)


def attend_back(near_bias, queries, keys, values, bias, log_total, attended, grad):
    rows, width = queries.shape
    size = keys.shape[0]
    prompt_len = bias.shape[0]
    lanes = 2 * width // HEADS
    pairs = HEADS // 2
    chunks = rows // PROMPT_DEV
    block = lambda count: pl.BlockSpec((count, lanes), lambda j: (0, j))
    counts = (prompt_len // 2, prompt_len // 2, CONT_DEV, CONT_DEV)
    return pl.pallas_call(
        functools.partial(attend_back_kernel, prompt_len),
        grid=(pairs,),
        in_specs=[
            pl.BlockSpec(memory_space=pltpu.SMEM),
            block(rows),
            block(size),
            block(size),
            pl.BlockSpec((prompt_len, PROMPT_DEV), lambda j: (0, 0)),
            pl.BlockSpec((1, chunks, 2 * PROMPT_DEV), lambda j: (j, 0, 0)),
            block(rows),
            block(rows),
        ],
        out_specs=[block(rows)]
        + [pl.BlockSpec((2, count, lanes), lambda j: (0, 0, j)) for count in counts],
        out_shape=[jax.ShapeDtypeStruct((rows, width), bf16)]
        + [jax.ShapeDtypeStruct((2, count, width), bf16) for count in counts],
        scratch_shapes=[pltpu.VMEM((size, lanes), f32), pltpu.VMEM((size, lanes), f32)],
        compiler_params=params("arbitrary"),
        cost_estimate=cost(40 * rows * size * width, 8 * (rows + size) * width, rows * size * HEADS),
        name="attend_back",
    )(near_bias, queries, keys, values, bias, log_total, attended, grad)


def local(
    tokens_in,
    cotangent,
    hash_ids,
    norm1_gain,
    norm1_bias,
    w_query,
    w_key,
    w_value,
    w_output,
    norm2_gain,
    norm2_bias,
    expert_in,
    expert_out,
):
    row_count, width = tokens_in.shape
    experts = lax.axis_size("expert")
    groups = lax.axis_size("group")
    position = lax.axis_index("expert")
    group = lax.axis_index("group")
    capacity = 2 * row_count // experts
    slots = experts * capacity
    tied = lax.optimization_barrier

    def all_exchanged(values):
        return lax.all_to_all(values, "expert", split_axis=0, concat_axis=0, tiled=True)

    def exchanged(values):
        got = all_exchanged(values.reshape(experts, capacity, width))
        return got.reshape(slots, width)

    near_tokens = lax.ppermute(
        tokens_in[PROMPT_DEV:], "expert", [(i, i + 1) for i in range(0, experts, 2)]
    )
    prompts, prompt_ids, near_tokens, last_tokens = gather_relative(
        tokens_in[:PROMPT_DEV], "expert", near_tokens
    )
    ids = jnp.broadcast_to(rounded(hash_ids), (row_count, 128))
    all_cot = lax.all_gather(jnp.concatenate([cotangent, ids], axis=1), "group")

    row_index = jnp.arange(row_count, dtype=jnp.int32)
    lower = rounded(row_index[:, None] >= row_index[None, :])

    routed = rounded(hash_ids == jnp.arange(experts, dtype=jnp.int32)[None, :])
    running = matmul(lower, routed)
    rank = (jnp.sum(running * routed.astype(f32), axis=-1) - 1.0).astype(jnp.int32)
    slot = hash_ids[:, 0] * capacity + rank
    spread = rounded(slot[None, :] == jnp.arange(slots, dtype=jnp.int32)[:, None])

    cot_sent, _ = tied((matmul(spread, cotangent, bf16), last_tokens))
    cot = {0: exchanged(cot_sent)}
    others_in, queries, keys, values = project(
        prompts + [near_tokens, tokens_in[PROMPT_DEV:]],
        norm1_gain,
        norm1_bias,
        w_query,
        w_key,
        w_value,
    )
    block_pos = jnp.stack([(position ^ r) * PROMPT_DEV for r in prompt_ids])
    prompt_pos = jnp.arange(PROMPT_DEV, dtype=jnp.int32)
    key_pos = (block_pos[:, None] + prompt_pos[None, :]).reshape(-1)
    query_pos = position * PROMPT_DEV + row_index[:PROMPT_DEV]
    bias = jnp.where(key_pos[:, None] <= query_pos[None, :], f32(0.0), f32(masked_score))
    near_bias = jnp.where(position % 2 == 1, f32(0.0), f32(masked_score))[None]
    attended, log_total = attend(near_bias, queries, keys, values, bias)

    residual = tokens_in.astype(f32) + matmul(attended, w_output)
    ffn_in = rounded(normalize(residual, norm2_gain, norm2_bias)[0])
    rows = exchanged(matmul(spread, ffn_in, bf16))
    all_numbers = all_cot[:, :, width].astype(jnp.int32)[:, None]
    numbers = lambda masks: jnp.stack([group ^ mask for mask in masks])
    near_sent = spread_rows(numbers([1]), all_numbers, all_cot, experts)
    grad_hidden = expert_back(cot[0], expert_out)
    rows, grad_hidden, near_sent = tied((rows, grad_hidden, near_sent))
    all_rows = lax.all_gather(rows, "group")
    cot[1] = all_exchanged(near_sent)
    hidden, grad_pre, grad_rows = expert_front(rows, grad_hidden, expert_in)
    grad_rows, hidden, cot[1] = tied((grad_rows, hidden, cot[1]))
    grad_got = exchanged(grad_rows)
    produced = expert_produce(hidden, expert_out)
    far_sent = spread_rows(numbers(range(2, groups)), all_numbers, all_cot, experts, produced)
    far_sent, grad_got = tied((far_sent, grad_got))
    far_got = all_exchanged(far_sent)

    grad_resid, grad_attn, grad_attended, sums2 = resid_back(
        grad_got, spread, residual, norm2_gain, cotangent, w_output
    )
    grad_queries, back_first, back_second, back_near, back_own = attend_back(
        near_bias, queries, keys, values, bias, log_total, attended, grad_attended
    )
    backs = (back_first, back_second, back_near, back_own, grad_queries)
    prompt_sums = scatter_relative(back_first, back_second, "expert")
    prompt_sent = next(prompt_sums)
    near_back = lax.ppermute(
        back_near, "expert", [(i + 1, i) for i in range(0, experts, 2)]
    )
    weights = weight_parts(
        (position & 1)[None],
        attended,
        others_in,
        grad_attn,
        grad_queries,
        (back_first, back_second, back_near, back_own),
        groups,
        experts,
    )
    weights, prompt_sent, near_back, far_got = tied((weights, prompt_sent, near_back, far_got))
    marks = []
    weight_sums = weight_chain(*weights, marks)
    weight_sent = next(weight_sums)
    prompt_sent, prompt_back = moved_on(prompt_sums, prompt_sent)
    weight_sent, prompt_sent = tied((weight_sent, prompt_sent))
    weight_sent, _ = moved_on(weight_sums, weight_sent)
    prompt_sent, prompt_back = moved_on(prompt_sums, prompt_sent)
    number, _ = tied((numbers(range(groups)), marks[-1]))
    operands = (expert_in, expert_out, (rows, grad_pre), all_rows, cot[1], far_got)
    in_first, *hidden_first = in_sums(number, 0, *operands)
    over_group = lambda values: lax.all_to_all(
        values, "group", split_axis=0, concat_axis=0, tiled=True
    )
    weight_sent, in_first = tied((weight_sent, in_first))
    got_first = over_group(in_first)
    weight_sent, _ = moved_on(weight_sums, weight_sent)
    number, _ = tied((number, marks[-1]))
    in_second, *hidden_second = in_sums(number, 1, *operands)
    got_first, in_second = tied((got_first, in_second))
    got_second = over_group(in_second)
    prompt_sent, weight_sent, number, _ = tied((prompt_sent, weight_sent, number, in_second))
    while prompt_sent is not None:
        prompt_sent, prompt_back = moved_on(prompt_sums, prompt_sent)
    grad_tokens, sums1 = input_back(
        prompt_back,
        back_own,
        near_back,
        grad_queries,
        w_query,
        w_key,
        w_value,
        tokens_in,
        norm1_gain,
        grad_resid,
    )
    number, _ = tied((number, sums1))
    grad_expert_out = out_sums(
        number, (hidden, cot[0]), cot[1], far_got, hidden_first + hidden_second
    )
    vector_steps = vector_sums(jnp.concatenate([sums1, sums2]))
    vectors = next(vector_steps)
    vectors = vector_steps.send(vectors)
    vectors, got_second, grad_expert_out = tied((vectors, got_second, grad_expert_out))
    vectors, _ = moved_on(vector_steps, vectors)
    while vectors is not None:
        vectors, vector_parts = moved_on(vector_steps, vectors)
    vectors = vector_parts
    while weight_sent is not None:
        weight_sent, weight_grads = moved_on(weight_sums, weight_sent)
    far_late, _ = tied((far_got, in_second))
    result_got = far_late[:, 0].reshape(slots, width)
    result = rounded(residual + matmul_tn(spread, result_got))
    grad_expert_in = lay_out([got_first, got_second])
    grad_w_output, grad_w_query, grad_w_key, grad_w_value = weight_grads
    return (
        result,
        grad_tokens,
        vectors[0],
        vectors[1],
        grad_w_query,
        grad_w_key,
        grad_w_value,
        grad_w_output,
        vectors[2],
        vectors[3],
        grad_expert_in,
        grad_expert_out,
    )


def solution(mesh):
    both = ("group", "expert")
    return jax.shard_map(
        local,
        mesh=mesh,
        in_specs=(
            P(both, None),
            P(both, None),
            P(both, None),
            P(),
            P(),
            P(),
            P(),
            P(),
            P(),
            P(),
            P(),
            P("expert", None, None),
            P("expert", None, None),
        ),
        out_specs=(
            P(both, None),
            P(both, None),
            P(both),
            P(both),
            P(both, None),
            P(both, None),
            P(both, None),
            P(both, None),
            P(both),
            P(both),
            P("expert", "group", None),
            P("expert", "group", None),
        ),
        check_vma=False,
    )
```

profile of v0, /device:TPU:0, one launch (start us, length us, event | category | flops | bytes accessed | tf_op | source)
XLA Modules:
  0.0 407.7 jit_solution(10167622899644909499)
XLA Ops:
  8.2 2.4 pad_maximum_fusion
  10.7 2.5 collective-permute-start.2
  13.2 2.4 collective-permute-start
  15.6 1.5 collective-permute-start.1
  17.4 4.1 %collective-permute-done.refs_1_ = bf16[128,1024]{1,0:T(8,128)(2,1)} collective-permute-done((bf16[128,1024]{1,0:T(8,128)(2,1)S(1)}, bf16[128,1024]{1,0:T(8,128)(2,1)}, u32[]{:S(2)}, u32[]{:S(2)}) %collective-permute-start) | collective-permute-done | bytes 262176 | tf_op jit(solution)/shard_map/ppermute | solution.py:25
  23.9 1.5 collective-permute-start.3
  25.4 2.6 fusion.5
  28.7 1.9 collective-permute-done.3.refs_3_
  30.6 3.8 all-to-all-start.1
  36.3 16.9 %project.1 = (bf16[1792,1024]{1,0:T(8,128)(2,1)}, bf16[512,1024]{1,0:T(8,128)(2,1)}, bf16[1792,1024]{1,0:T(8,128)(2,1)}, bf16[1792,1024]{1,0:T(8,128)(2,1)}) custom-call(f32[1,1024]{1,0:T(1,128)} %bitcast.73, f32[1,1024]{1,0:T(1,128)} %bitcast.77, bf16[1024,1024]{1,0:T(8,128)(2,1)} %wq_ref.3, bf16[1024,1024]{1,0:T(8,128)(2,1)} %wk_ref.3, ...), custom_call_target="tpu_custom_call" | custom-call | flops 375809632 | bytes 943718 | tf_op jit(solution)/shard_map/project/pallas_call | solution.py:611
  53.2 23.3 %attend.1 = (bf16[512,1024]{1,0:T(8,128)(2,1)}, f32[8,4,256]{2,1,0:T(4,128)}) custom-call(f32[1]{0:T(128)} %bitcast.near_ref, bf16[512,1024]{1,0:T(8,128)(2,1)} %get-tuple-element.94.q_ref, bf16[1792,1024]{1,0:T(8,128)(2,1)} %get-tuple-element.95.k_ref, bf16[1792,1024]{1,0:T(8,128)(2,1)} %get-tuple-element.96.v_ref, f32[1024,128]{1,0:T(8,128)} %compare_select_fusion.bias_ref), custom_call_target="tpu_custom_call" | custom-call | flops 751619264 | bytes 471859 | tf_op jit(solution)/shard_map/attend/pallas_call | solution.py:920
  76.5 3.3 fusion.18
  81.1 2.9 fusion.4
  85.3 4.7 %all-to-all-start = ((bf16[8,128,1024]{2,1,0:T(8,128)(2,1)}), bf16[8,128,1024]{2,1,0:T(8,128)(2,1)S(1)}, u32[]{:S(2)}, u32[]{:S(2)}) async-start(bf16[8,128,1024]{2,1,0:T(8,128)(2,1)} %bitcast.71), calls=%async_computation | async-start | bytes 4194304 | tf_op jit(solution)/shard_map/all_to_all | solution.py:1002
  90.0 13.1 %expert_back.1.gh_ref = bf16[1024,4096]{1,0:T(8,128)(2,1)} custom-call(bf16[1024,1024]{1,0:T(8,128)(2,1)} %bitcast.66, bf16[1,4096,1024]{2,1,0:T(8,128)(2,1)} %wout_ref.7), custom_call_target="tpu_custom_call" | custom-call | flops 429496736 | bytes 838860 | tf_op jit(solution)/shard_map/expert_back/pallas_call | solution.py:270
  105.1 4.0 spread_rows.2
  109.2 7.4 %all-to-all-done = bf16[8,128,1024]{2,1,0:T(8,128)(2,1)S(1)} async-done(((bf16[8,128,1024]{2,1,0:T(8,128)(2,1)}), bf16[8,128,1024]{2,1,0:T(8,128)(2,1)S(1)}, u32[]{:S(2)}, u32[]{:S(2)}) %all-to-all-start) | async-done | bytes 2097184 | tf_op jit(solution)/shard_map/all_to_all | solution.py:1002
  117.9 4.4 %all-to-all-start.2 = ((bf16[8,1,128,1024]{3,2,1,0:T(8,128)(2,1)}), bf16[8,1,128,1024]{3,2,1,0:T(8,128)(2,1)}, u32[]{:S(2)}, u32[]{:S(2)}) async-start(bf16[8,1,128,1024]{3,2,1,0:T(8,128)(2,1)} %spread_rows.2), calls=%async_computation.2 | async-start | bytes 4194304 | tf_op jit(solution)/shard_map/all_to_all | solution.py:1002
  123.1 25.4 %expert_front.1 = (bf16[1024,4096]{1,0:T(8,128)(2,1)}, bf16[1024,4096]{1,0:T(8,128)(2,1)}, bf16[1024,1024]{1,0:T(8,128)(2,1)}) custom-call(bf16[1024,1024]{1,0:T(8,128)(2,1)} %bitcast.60, bf16[1024,4096]{1,0:T(8,128)(2,1)} %expert_back.1.gh_ref, bf16[1,1024,4096]{2,1,0:T(8,128)(2,1)} %win_ref.5), custom_call_target="tpu_custom_call" | custom-call | flops 858993472 | bytes 1677721 | tf_op jit(solution)/shard_map/expert_front/pallas_call | solution.py:317
  149.0 3.7 all-to-all-start.3
  153.2 14.6 %expert_produce.1.refs_0_ = bf16[1024,1024]{1,0:T(8,128)(2,1)} custom-call(bf16[1024,4096]{1,0:T(8,128)(2,1)} %get-tuple-element.105.hidden_ref, bf16[1,4096,1024]{2,1,0:T(8,128)(2,1)} %wout_ref.7), custom_call_target="tpu_custom_call" | custom-call | flops 429496736 | bytes 838860 | tf_op jit(solution)/shard_map/expert_produce/pallas_call | solution.py:355
  167.8 7.6 %spread_rows.3 = bf16[8,3,128,1024]{3,2,1,0:T(8,128)(2,1)} custom-call(s32[2]{0:T(128)} %pad_add_fusion._, s32[4,1,512]{2,1,0:T(1,128)} %reshape.106.ids_ref, bf16[4,512,1152]{2,1,0:T(8,128)(2,1)} %bitcast.65, bf16[1024,1024]{1,0:T(8,128)(2,1)} %expert_produce.1.refs_0_), custom_call_target="tpu_custom_call" | custom-call | flops 161061280 | bytes 400000 | tf_op jit(solution)/shard_map/spread_rows/pallas_call | solution.py:567
  175.5 3.8 all-to-all-done.3
  180.7 4.9 %all-to-all-start.4 = ((bf16[8,3,128,1024]{3,2,1,0:T(8,128)(2,1)}), bf16[8,3,128,1024]{3,2,1,0:T(8,128)(2,1)}, u32[]{:S(2)}, u32[]{:S(2)}) async-start(bf16[8,3,128,1024]{3,2,1,0:T(8,128)(2,1)} %spread_rows.3), calls=%async_computation.4 | async-start | bytes 12582912 | tf_op jit(solution)/shard_map/all_to_all | solution.py:1002
  187.1 8.0 %resid_back.1 = (f32[512,1024]{1,0:T(8,128)}, bf16[512,1024]{1,0:T(8,128)(2,1)}, bf16[512,1024]{1,0:T(8,128)(2,1)}, f32[2,1024]{1,0:T(2,128)}) custom-call(bf16[1024,1024]{1,0:T(8,128)(2,1)} %bitcast.68, bf16[1024,512]{1,0:T(8,128)(2,1)} %fusion.1.spread_ref, f32[512,1024]{1,0:T(8,128)} %copy-done.2, f32[1,1024]{1,0:T(1,128)} %bitcast.78, ...), custom_call_target="tpu_custom_call" | custom-call | flops 107374184 | bytes 419430 | tf_op jit(solution)/shard_map/resid_back/pallas_call | solution.py:711
  195.0 34.1 %attend_back.1 = (bf16[512,1024]{1,0:T(8,128)(2,1)}, bf16[2,512,1024]{2,1,0:T(8,128)(2,1)}, bf16[2,512,1024]{2,1,0:T(8,128)(2,1)}, bf16[2,384,1024]{2,1,0:T(8,128)(2,1)}, bf16[2,384,1024]{2,1,0:T(8,128)(2,1)}) custom-call(f32[1]{0:T(128)} %bitcast.near_ref, bf16[512,1024]{1,0:T(8,128)(2,1)} %get-tuple-element.94.q_ref, ...), custom_call_target="tpu_custom_call" | custom-call | flops 1879048192 | bytes 943718 | tf_op jit(solution)/shard_map/attend_back/pallas_call | solution.py:953
  230.8 18.6 %weight_parts.1 = (bf16[4,4,4,32,1024]{4,3,2,1,0:T(8,128)(2,1)}, bf16[4,4,4,32,1024]{4,3,2,1,0:T(8,128)(2,1)}) custom-call(s32[1]{0:T(128)} %bitcast.13.odd_ref, bf16[512,1024]{1,0:T(8,128)(2,1)} %get-tuple-element.97.out_ref.refs_0_, bf16[1792,1024]{1,0:T(8,128)(2,1)} %get-tuple-element.98.refs_1_, bf16[512,1024]{1,0:T(8,128)(2,1)} %get-tuple-element.108.refs_2_, ...), custom_call_target="tpu_custom_call" | custom-call | flops 500000000 | bytes 1500000 | tf_op jit(solution)/shard_map/weight_parts/pallas_call | solution.py:668
  249.4 7.7 %all-to-all-done.4.far_ref = bf16[8,3,128,1024]{3,2,1,0:T(8,128)(2,1)} async-done(((bf16[8,3,128,1024]{3,2,1,0:T(8,128)(2,1)}), bf16[8,3,128,1024]{3,2,1,0:T(8,128)(2,1)}, u32[]{:S(2)}, u32[]{:S(2)}) %all-to-all-start.4) | async-done | bytes 6291488 | tf_op jit(solution)/shard_map/all_to_all | solution.py:1002
  257.2 3.2 add_convert_fusion
  261.7 7.6 %collective-permute-done.11 = bf16[2,64,1024]{2,1,0:T(8,128)(2,1)S(1)} collective-permute-done((bf16[2,64,1024]{2,1,0:T(8,128)(2,1)S(1)}, bf16[2,64,1024]{2,1,0:T(8,128)(2,1)S(1)}, u32[]{:S(2)}, u32[]{:S(2)}) %collective-permute-start.11) | collective-permute-done | bytes 262176 | tf_op jit(solution)/shard_map/ppermute | solution.py:25
  269.5 5.2 %halve.2 = (bf16[2,4,2,32,1024]{4,3,2,1,0:T(8,128)(2,1)}, bf16[2,4,2,32,1024]{4,3,2,1,0:T(8,128)(2,1)}, bf16[2,4,2,32,1024]{4,3,2,1,0:T(8,128)(2,1)}, bf16[2,4,2,32,1024]{4,3,2,1,0:T(8,128)(2,1)}) custom-call(s32[1]{0:T(128)} %bitcast.25.own_ref, bf16[4,4,4,32,1024]{4,3,2,1,0:T(8,128)(2,1)} %get-tuple-element.120.refs_0_.refs_2_, ...), custom_call_target="tpu_custom_call" | custom-call | flops 104857 | bytes 629145 | tf_op jit(solution)/shard_map/halve/pallas_call | solution.py:159
  277.4 19.4 %in_sums.2 = (bf16[4,256,512]{2,1,0:T(8,128)(2,1)}, bf16[1024,512]{1,0:T(8,128)(2,1)}, bf16[2,1024,512]{2,1,0:T(8,128)(2,1)}) custom-call(s32[4]{0:T(128)} %pad_add_fusion.1._, bf16[1,1024,4096]{2,1,0:T(8,128)(2,1)} %win_ref.5, bf16[1,4096,1024]{2,1,0:T(8,128)(2,1)} %wout_ref.7, bf16[1024,1024]{1,0:T(8,128)(2,1)} %bitcast.61, ...), custom_call_target="tpu_custom_call" | custom-call | flops 644245120 | bytes 800000 | tf_op jit(solution)/shard_map/in_sums/pallas_call | solution.py:406
  296.7 2.9 collective-permute-done.13.refs_1_
  300.6 5.1 %all-to-all-start.5 = ((bf16[4,256,512]{2,1,0:T(8,128)(2,1)}), bf16[4,256,512]{2,1,0:T(8,128)(2,1)S(1)}, u32[]{:S(2)}, u32[]{:S(2)}) async-start(bf16[4,256,512]{2,1,0:T(8,128)(2,1)} %get-tuple-element.131), calls=%async_computation.5 | async-start | bytes 2097152 | tf_op jit(solution)/shard_map/all_to_all | solution.py:1095
  305.7 2.2 add_convert_fusion.6
  310.2 3.3 halve.3
  315.3 19.1 %in_sums.3 = (bf16[4,256,512]{2,1,0:T(8,128)(2,1)}, bf16[1024,512]{1,0:T(8,128)(2,1)}, bf16[2,1024,512]{2,1,0:T(8,128)(2,1)}) custom-call(s32[4]{0:T(128)} %pad_add_fusion.1._, bf16[1,1024,4096]{2,1,0:T(8,128)(2,1)} %win_ref.5, bf16[1,4096,1024]{2,1,0:T(8,128)(2,1)} %wout_ref.7, bf16[1024,1024]{1,0:T(8,128)(2,1)} %bitcast.62, ...), custom_call_target="tpu_custom_call" | custom-call | flops 644245120 | bytes 800000 | tf_op jit(solution)/shard_map/in_sums/pallas_call | solution.py:406
  334.4 5.3 %all-to-all-start.6 = ((bf16[4,256,512]{2,1,0:T(8,128)(2,1)}), bf16[4,256,512]{2,1,0:T(8,128)(2,1)}, u32[]{:S(2)}, u32[]{:S(2)}) async-start(bf16[4,256,512]{2,1,0:T(8,128)(2,1)} %get-tuple-element.138), calls=%async_computation.6 | async-start | bytes 2097152 | tf_op jit(solution)/shard_map/all_to_all | solution.py:1095
  339.8 2.7 turn.1
  342.5 2.0 collective-permute-start.24
  344.5 2.3 add_convert_fusion.5.prompt_ref
  346.8 10.6 %input_back.1 = (bf16[512,1024]{1,0:T(8,128)(2,1)}, f32[2,1024]{1,0:T(2,128)}) custom-call(bf16[2,128,1024]{2,1,0:T(8,128)(2,1)} %add_convert_fusion.5.prompt_ref, bf16[2,384,1024]{2,1,0:T(8,128)(2,1)} %get-tuple-element.115.refs_7_.own_ref, bf16[2,384,1024]{2,1,0:T(8,128)(2,1)} %collective-permute-done.9.near_ref, ...), custom_call_target="tpu_custom_call" | custom-call | flops 161061280 | bytes 524288 | tf_op jit(solution)/shard_map/input_back/pallas_call | solution.py:778
  358.2 17.1 %out_sums.1 = f32[1,1024,1024]{2,1,0:T(8,128)} custom-call(s32[4]{0:T(128)} %pad_add_fusion.1._, bf16[1024,4096]{1,0:T(8,128)(2,1)} %get-tuple-element.105.hidden_ref, bf16[1024,1024]{1,0:T(8,128)(2,1)} %bitcast.67, bf16[8,1,128,1024]{3,2,1,0:T(8,128)(2,1)} %all-to-all-done.2.near_ref, bf16[8,3,128,1024]{3,2,1,0:T(8,128)(2,1)} %all-to-all-done.4.far_ref, ...), custom_call_target="tpu_custom_call" | custom-call | flops 429496736 | bytes 800000 | tf_op jit(solution)/shard_map/out_sums/pallas_call | solution.py:472
  375.4 3.1 slice.68
  379.7 2.4 collective-permute-start.25
  383.8 3.9 add_convert_fusion.1
  388.2 6.4 %collective-permute-done.25 = bf16[4,32,1024]{2,1,0:T(8,128)(2,1)S(1)} collective-permute-done((bf16[4,32,1024]{2,1,0:T(8,128)(2,1)S(1)}, bf16[4,32,1024]{2,1,0:T(8,128)(2,1)S(1)}, u32[]{:S(2)}, u32[]{:S(2)}) %collective-permute-start.25) | collective-permute-done | bytes 262176 | tf_op jit(solution)/shard_map/ppermute | solution.py:25
  395.6 4.2 %lay_out.1 = f32[1,256,4096]{2,1,0:T(8,128)} custom-call(bf16[4,256,512]{2,1,0:T(8,128)(2,1)} %copy-done.5, bf16[4,256,512]{2,1,0:T(8,128)(2,1)} %all-to-all-done.6.refs_1_), custom_call_target="tpu_custom_call" | custom-call | flops 52428 | bytes 314572 | tf_op jit(solution)/shard_map/lay_out/pallas_call | solution.py:507
  (130 shorter events, 33.5 us)
Async XLA Ops:
  7.2 3.4 copy-start.7
  7.2 95.9 %all-gather.5.cloned.1.call-start = ((), (), s32[]{:S(2)}) async-start(), calls=%async_computation.7 | async-start | bytes 5898240 | tf_op jit(solution)/shard_map/all_gather | solution.py:1015
  10.5 6.6 %copy-start.21 = (s32[512,1]{0,1:T(1,128)S(1)}, s32[512,1]{0,1:T(1,128)}, u32[]{:S(2)}) copy-start(s32[512,1]{0,1:T(1,128)} %param.15) | copy-start | bytes 6148
  10.5 14.9 %copy-start.6 = (bf16[512,1024]{1,0:T(8,128)(2,1)S(1)}, bf16[512,1024]{1,0:T(8,128)(2,1)}, u32[]{:S(2)}) copy-start(bf16[512,1024]{1,0:T(8,128)(2,1)} %cot_ref.1) | copy-start | bytes 3145732
  10.6 17.4 %copy-start.9 = (bf16[384,1024]{1,0:T(8,128)(2,1)}, bf16[384,1024]{1,0:T(8,128)(2,1)S(1)}, u32[]{:S(2)}) copy-start(bf16[384,1024]{1,0:T(8,128)(2,1)S(1)} %slice.63.refs_9_) | copy-start | bytes 2359300
  10.7 12.3 %collective-permute-start.2 = (bf16[384,1024]{1,0:T(8,128)(2,1)S(1)}, bf16[384,1024]{1,0:T(8,128)(2,1)S(1)}, u32[]{:S(2)}, u32[]{:S(2)}) collective-permute-start(bf16[384,1024]{1,0:T(8,128)(2,1)S(1)} %slice.63.refs_9_), channel_id=1, source_target_pairs={{0,1},{2,3},{4,5},{6,7},{8,9},{10,11},{12,13},{14,15},{16,17},{18,... | collective-permute-start | bytes 2359304 | tf_op jit(solution)/shard_map/ppermute | solution.py:1008
  13.2 14.8 %copy-start.12 = (bf16[128,1024]{1,0:T(8,128)(2,1)}, bf16[128,1024]{1,0:T(8,128)(2,1)S(1)}, u32[]{:S(2)}) copy-start(bf16[128,1024]{1,0:T(8,128)(2,1)S(1)} %slice.62.refs_0_) | copy-start | bytes 786436
  13.2 8.3 %collective-permute-start = (bf16[128,1024]{1,0:T(8,128)(2,1)S(1)}, bf16[128,1024]{1,0:T(8,128)(2,1)}, u32[]{:S(2)}, u32[]{:S(2)}) collective-permute-start(bf16[128,1024]{1,0:T(8,128)(2,1)S(1)} %slice.62.refs_0_), channel_id=1, source_target_pairs={{0,2},{1,3},{2,0},{3,1},{4,6},{5,7},{6,4},{7,5},{8,10},{9,11},{10,... | collective-permute-start | bytes 786440 | tf_op jit(solution)/shard_map/ppermute | solution.py:25
  15.6 7.4 %collective-permute-start.1 = (bf16[128,1024]{1,0:T(8,128)(2,1)S(1)}, bf16[128,1024]{1,0:T(8,128)(2,1)}, u32[]{:S(2)}, u32[]{:S(2)}) collective-permute-start(bf16[128,1024]{1,0:T(8,128)(2,1)S(1)} %slice.62.refs_0_), channel_id=1, source_target_pairs={{0,4},{1,5},{2,6},{3,7},{4,0},{5,1},{6,2},{7,3},{8,12},{9,13},{10,... | collective-permute-start | bytes 786440 | tf_op jit(solution)/shard_map/ppermute | solution.py:25
  17.1 18.3 %collective-permute-start.4 = (bf16[128,1024]{1,0:T(8,128)(2,1)S(1)}, bf16[128,1024]{1,0:T(8,128)(2,1)}, u32[]{:S(2)}, u32[]{:S(2)}) collective-permute-start(bf16[128,1024]{1,0:T(8,128)(2,1)S(1)} %slice.62.refs_0_), channel_id=1, source_target_pairs={{0,1},{1,0},{2,3},{3,2},{4,5},{5,4},{6,7},{7,6},{8,9},{9,8},{10,11... | collective-permute-start | bytes 786440 | tf_op jit(solution)/shard_map/ppermute | solution.py:25
  23.9 6.7 %collective-permute-start.3 = (bf16[128,1024]{1,0:T(8,128)(2,1)}, bf16[128,1024]{1,0:T(8,128)(2,1)}, u32[]{:S(2)}, u32[]{:S(2)}) collective-permute-start(bf16[128,1024]{1,0:T(8,128)(2,1)} %collective-permute-done.refs_1_), channel_id=1, source_target_pairs={{0,4},{1,5},{2,6},{3,7},{4,0},{5,1},{6,2},{7,3},{8,12},{9,13},{10,... | collective-permute-start | bytes 786440 | tf_op jit(solution)/shard_map/ppermute | solution.py:25
  28.2 7.3 %collective-permute-start.5 = (bf16[128,1024]{1,0:T(8,128)(2,1)}, bf16[128,1024]{1,0:T(8,128)(2,1)S(1)}, u32[]{:S(2)}, u32[]{:S(2)}) collective-permute-start(bf16[128,1024]{1,0:T(8,128)(2,1)} %collective-permute-done.refs_1_), channel_id=1, source_target_pairs={{0,1},{1,0},{2,3},{3,2},{4,5},{5,4},{6,7},{7,6},{8,9},{9,8},{10,11... | collective-permute-start | bytes 786440 | tf_op jit(solution)/shard_map/ppermute | solution.py:25
  28.2 7.3 %collective-permute-start.6 = (bf16[128,1024]{1,0:T(8,128)(2,1)}, bf16[128,1024]{1,0:T(8,128)(2,1)S(1)}, u32[]{:S(2)}, u32[]{:S(2)}) collective-permute-start(bf16[128,1024]{1,0:T(8,128)(2,1)} %collective-permute-done.1.refs_2_), channel_id=1, source_target_pairs={{0,1},{1,0},{2,3},{3,2},{4,5},{5,4},{6,7},{7,6},{8,9},{9,8},{10,11... | collective-permute-start | bytes 786440 | tf_op jit(solution)/shard_map/ppermute | solution.py:25
  30.6 4.9 %collective-permute-start.7 = (bf16[128,1024]{1,0:T(8,128)(2,1)}, bf16[128,1024]{1,0:T(8,128)(2,1)S(1)}, u32[]{:S(2)}, u32[]{:S(2)}) collective-permute-start(bf16[128,1024]{1,0:T(8,128)(2,1)} %collective-permute-done.3.refs_3_), channel_id=1, source_target_pairs={{0,1},{1,0},{2,3},{3,2},{4,5},{5,4},{6,7},{7,6},{8,9},{9,8},{10,11... | collective-permute-start | bytes 786440 | tf_op jit(solution)/shard_map/ppermute | solution.py:25
  30.6 53.4 %all-to-all-start.1 = ((bf16[8,128,1024]{2,1,0:T(8,128)(2,1)}), bf16[8,128,1024]{2,1,0:T(8,128)(2,1)S(1)}, u32[]{:S(2)}, u32[]{:S(2)}) async-start(bf16[8,128,1024]{2,1,0:T(8,128)(2,1)} %bitcast.69), calls=%async_computation.1 | async-start | bytes 4194304 | tf_op jit(solution)/shard_map/all_to_all | solution.py:1002
  53.2 23.3 %copy-start.8 = (bf16[512,1024]{1,0:T(8,128)(2,1)S(1)}, bf16[512,1024]{1,0:T(8,128)(2,1)}, u32[]{:S(2)}) copy-start(bf16[512,1024]{1,0:T(8,128)(2,1)} %x_ref.1) | copy-start | bytes 3145732
  85.3 31.3 %all-to-all-start = ((bf16[8,128,1024]{2,1,0:T(8,128)(2,1)}), bf16[8,128,1024]{2,1,0:T(8,128)(2,1)S(1)}, u32[]{:S(2)}, u32[]{:S(2)}) async-start(bf16[8,128,1024]{2,1,0:T(8,128)(2,1)} %bitcast.71), calls=%async_computation | async-start | bytes 4194304 | tf_op jit(solution)/shard_map/all_to_all | solution.py:1002
  117.9 31.0 %all-to-all-start.2 = ((bf16[8,1,128,1024]{3,2,1,0:T(8,128)(2,1)}), bf16[8,1,128,1024]{3,2,1,0:T(8,128)(2,1)}, u32[]{:S(2)}, u32[]{:S(2)}) async-start(bf16[8,1,128,1024]{3,2,1,0:T(8,128)(2,1)} %spread_rows.2), calls=%async_computation.2 | async-start | bytes 4194304 | tf_op jit(solution)/shard_map/all_to_all | solution.py:1002
  122.3 155.0 %all-gather.7.cloned.1.call-start = ((), (), s32[]{:S(2)}) async-start(), calls=%async_computation.8 | async-start | bytes 10485760 | tf_op jit(solution)/shard_map/all_gather | solution.py:1052
  149.0 30.3 %all-to-all-start.3 = ((bf16[8,128,1024]{2,1,0:T(8,128)(2,1)}), bf16[8,128,1024]{2,1,0:T(8,128)(2,1)S(1)}, u32[]{:S(2)}, u32[]{:S(2)}) async-start(bf16[8,128,1024]{2,1,0:T(8,128)(2,1)} %bitcast.72), calls=%async_computation.3 | async-start | bytes 4194304 | tf_op jit(solution)/shard_map/all_to_all | solution.py:1002
  180.7 76.5 %all-to-all-start.4 = ((bf16[8,3,128,1024]{3,2,1,0:T(8,128)(2,1)}), bf16[8,3,128,1024]{3,2,1,0:T(8,128)(2,1)}, u32[]{:S(2)}, u32[]{:S(2)}) async-start(bf16[8,3,128,1024]{3,2,1,0:T(8,128)(2,1)} %spread_rows.3), calls=%async_computation.4 | async-start | bytes 12582912 | tf_op jit(solution)/shard_map/all_to_all | solution.py:1002
  229.1 20.3 %collective-permute-start.8 = (bf16[2,512,1024]{2,1,0:T(8,128)(2,1)}, bf16[2,512,1024]{2,1,0:T(8,128)(2,1)S(1)}, u32[]{:S(2)}, u32[]{:S(2)}) collective-permute-start(bf16[2,512,1024]{2,1,0:T(8,128)(2,1)} %get-tuple-element.113.refs_5_), channel_id=1, source_target_pairs={{0,1},{1,0},{2,3},{3,2},{4,5},{5,4},{6,7},{7,6},{8,9},{9,8},{10,11... | collective-permute-start | bytes 6291464 | tf_op jit(solution)/shard_map/ppermute | solution.py:25
  229.5 19.9 %collective-permute-start.9 = (bf16[2,384,1024]{2,1,0:T(8,128)(2,1)}, bf16[2,384,1024]{2,1,0:T(8,128)(2,1)}, u32[]{:S(2)}, u32[]{:S(2)}) collective-permute-start(bf16[2,384,1024]{2,1,0:T(8,128)(2,1)} %get-tuple-element.114.refs_6_), channel_id=1, source_target_pairs={{1,0},{3,2},{5,4},{7,6},{9,8},{11,10},{13,12},{15,14},{17,16},{19,... | collective-permute-start | bytes 4718600 | tf_op jit(solution)/shard_map/ppermute | solution.py:1071
  249.4 7.8 %copy-start.10 = (bf16[2,512,1024]{2,1,0:T(8,128)(2,1)}, bf16[2,512,1024]{2,1,0:T(8,128)(2,1)S(1)}, u32[]{:S(2)}) copy-start(bf16[2,512,1024]{2,1,0:T(8,128)(2,1)S(1)} %collective-permute-done.8) | copy-start | bytes 6291460
  257.2 12.3 %collective-permute-start.10 = (bf16[4,4,4,32,1024]{4,3,2,1,0:T(8,128)(2,1)}, bf16[4,4,4,32,1024]{4,3,2,1,0:T(8,128)(2,1)}, u32[]{:S(2)}, u32[]{:S(2)}) collective-permute-start(bf16[4,4,4,32,1024]{4,3,2,1,0:T(8,128)(2,1)} %get-tuple-element.121), channel_id=1, source_target_pairs={{0,1},{1,0},{2,3},{3,2},{4,5},{5,4},{6,7},{7,6},{8,9},{9,8},{10,11... | collective-permute-start | bytes 12582920 | tf_op jit(solution)/shard_map/ppermute | solution.py:25
  260.4 8.8 %collective-permute-start.11 = (bf16[2,64,1024]{2,1,0:T(8,128)(2,1)S(1)}, bf16[2,64,1024]{2,1,0:T(8,128)(2,1)S(1)}, u32[]{:S(2)}, u32[]{:S(2)}) collective-permute-start(bf16[2,64,1024]{2,1,0:T(8,128)(2,1)S(1)} %get-tuple-element.169), channel_id=1, source_target_pairs={{0,4},{1,5},{2,6},{3,7},{4,0},{5,1},{6,2},{7,3},{8,12},{9,13},{10,... | collective-permute-start | bytes 786440 | tf_op jit(solution)/shard_map/ppermute | solution.py:25
  261.0 8.4 %collective-permute-start.12 = (bf16[2,64,1024]{2,1,0:T(8,128)(2,1)S(1)}, bf16[2,64,1024]{2,1,0:T(8,128)(2,1)S(1)}, u32[]{:S(2)}, u32[]{:S(2)}) collective-permute-start(bf16[2,64,1024]{2,1,0:T(8,128)(2,1)S(1)} %get-tuple-element.168), channel_id=1, source_target_pairs={{0,2},{1,3},{2,0},{3,1},{4,6},{5,7},{6,4},{7,5},{8,10},{9,11},{10,... | collective-permute-start | bytes 786440 | tf_op jit(solution)/shard_map/ppermute | solution.py:25
  269.5 5.2 %copy-start.18 = (bf16[2,64,1024]{2,1,0:T(8,128)(2,1)}, bf16[2,64,1024]{2,1,0:T(8,128)(2,1)S(1)}, u32[]{:S(2)}) copy-start(bf16[2,64,1024]{2,1,0:T(8,128)(2,1)S(1)} %collective-permute-done.12) | copy-start | bytes 786436
  274.7 24.9 %collective-permute-start.13 = (bf16[2,4,2,32,1024]{4,3,2,1,0:T(8,128)(2,1)}, bf16[2,4,2,32,1024]{4,3,2,1,0:T(8,128)(2,1)S(1)}, u32[]{:S(2)}, u32[]{:S(2)}) collective-permute-start(bf16[2,4,2,32,1024]{4,3,2,1,0:T(8,128)(2,1)} %get-tuple-element.124), channel_id=1, source_target_pairs={{0,2},{1,3},{2,0},{3,1},{4,6},{5,7},{6,4},{7,5},{8,10},{9,11},{10,... | collective-permute-start | bytes 3145736 | tf_op jit(solution)/shard_map/ppermute | solution.py:25
  275.4 24.6 %collective-permute-start.14 = (bf16[2,4,2,32,1024]{4,3,2,1,0:T(8,128)(2,1)}, bf16[2,4,2,32,1024]{4,3,2,1,0:T(8,128)(2,1)}, u32[]{:S(2)}, u32[]{:S(2)}) collective-permute-start(bf16[2,4,2,32,1024]{4,3,2,1,0:T(8,128)(2,1)} %get-tuple-element.125), channel_id=1, source_target_pairs={{0,4},{1,5},{2,6},{3,7},{4,0},{5,1},{6,2},{7,3},{8,12},{9,13},{10,... | collective-permute-start | bytes 3145736 | tf_op jit(solution)/shard_map/ppermute | solution.py:25
  300.6 33.8 %all-to-all-start.5 = ((bf16[4,256,512]{2,1,0:T(8,128)(2,1)}), bf16[4,256,512]{2,1,0:T(8,128)(2,1)S(1)}, u32[]{:S(2)}, u32[]{:S(2)}) async-start(bf16[4,256,512]{2,1,0:T(8,128)(2,1)} %get-tuple-element.131), calls=%async_computation.5 | async-start | bytes 2097152 | tf_op jit(solution)/shard_map/all_to_all | solution.py:1095
  307.9 31.9 %collective-permute-start.15 = (bf16[2,128,1024]{2,1,0:T(8,128)(2,1)}, bf16[2,128,1024]{2,1,0:T(8,128)(2,1)}, u32[]{:S(2)}, u32[]{:S(2)}) collective-permute-start(bf16[2,128,1024]{2,1,0:T(8,128)(2,1)} %get-tuple-element.167), channel_id=1, source_target_pairs={{0,2},{1,3},{2,0},{3,1},{4,6},{5,7},{6,4},{7,5},{8,10},{9,11},{10,... | collective-permute-start | bytes 1572872 | tf_op jit(solution)/shard_map/ppermute | solution.py:25
  308.8 31.0 %collective-permute-start.16 = (bf16[2,128,1024]{2,1,0:T(8,128)(2,1)}, bf16[2,128,1024]{2,1,0:T(8,128)(2,1)}, u32[]{:S(2)}, u32[]{:S(2)}) collective-permute-start(bf16[2,128,1024]{2,1,0:T(8,128)(2,1)} %get-tuple-element.166), channel_id=1, source_target_pairs={{0,4},{1,5},{2,6},{3,7},{4,0},{5,1},{6,2},{7,3},{8,12},{9,13},{10,... | collective-permute-start | bytes 1572872 | tf_op jit(solution)/shard_map/ppermute | solution.py:25
  313.5 26.3 %collective-permute-start.17 = (bf16[2,4,1,32,1024]{4,3,2,1,0:T(8,128)(2,1)}, bf16[2,4,1,32,1024]{4,3,2,1,0:T(8,128)(2,1)}, u32[]{:S(2)}, u32[]{:S(2)}) collective-permute-start(bf16[2,4,1,32,1024]{4,3,2,1,0:T(8,128)(2,1)} %get-tuple-element.142), channel_id=1, source_target_pairs={{0,4},{1,5},{2,6},{3,7},{4,0},{5,1},{6,2},{7,3},{8,12},{9,13},{10,... | collective-permute-start | bytes 1572872 | tf_op jit(solution)/shard_map/ppermute | solution.py:25
  314.1 25.7 %collective-permute-start.18 = (bf16[2,4,1,32,1024]{4,3,2,1,0:T(8,128)(2,1)}, bf16[2,4,1,32,1024]{4,3,2,1,0:T(8,128)(2,1)}, u32[]{:S(2)}, u32[]{:S(2)}) collective-permute-start(bf16[2,4,1,32,1024]{4,3,2,1,0:T(8,128)(2,1)} %get-tuple-element.143), channel_id=1, source_target_pairs={{0,2},{1,3},{2,0},{3,1},{4,6},{5,7},{6,4},{7,5},{8,10},{9,11},{10,... | collective-permute-start | bytes 1572872 | tf_op jit(solution)/shard_map/ppermute | solution.py:25
  334.4 8.1 %copy-start.5 = (bf16[4,256,512]{2,1,0:T(8,128)(2,1)}, bf16[4,256,512]{2,1,0:T(8,128)(2,1)S(1)}, u32[]{:S(2)}) copy-start(bf16[4,256,512]{2,1,0:T(8,128)(2,1)S(1)} %all-to-all-done.5.refs_0_) | copy-start | bytes 3145732
  334.4 48.0 %all-to-all-start.6 = ((bf16[4,256,512]{2,1,0:T(8,128)(2,1)}), bf16[4,256,512]{2,1,0:T(8,128)(2,1)}, u32[]{:S(2)}, u32[]{:S(2)}) async-start(bf16[4,256,512]{2,1,0:T(8,128)(2,1)} %get-tuple-element.138), calls=%async_computation.6 | async-start | bytes 2097152 | tf_op jit(solution)/shard_map/all_to_all | solution.py:1095
  342.5 37.0 %collective-permute-start.24 = (bf16[4,2,32,1024]{3,2,1,0:T(8,128)(2,1)}, bf16[4,2,32,1024]{3,2,1,0:T(8,128)(2,1)S(1)}, u32[]{:S(2)}, u32[]{:S(2)}) collective-permute-start(bf16[4,2,32,1024]{3,2,1,0:T(8,128)(2,1)} %get-tuple-element.162), channel_id=1, source_target_pairs={{0,8},{8,0},{16,24},{24,16},{1,9},{9,1},{17,25},{25,17},{2,10},{10... | collective-permute-start | bytes 1572872 | tf_op jit(solution)/shard_map/ppermute | solution.py:25
  346.8 10.6 %copy-start.19 = (f32[2,1024]{1,0:T(2,128)S(1)}, f32[2,1024]{1,0:T(2,128)}, u32[]{:S(2)}) copy-start(f32[2,1024]{1,0:T(2,128)} %get-tuple-element.150) | copy-start | bytes 24580
  358.1 20.4 %collective-permute-start.19 = (f32[4,1024]{1,0:T(4,128)S(1)}, f32[4,1024]{1,0:T(4,128)S(1)}, u32[]{:S(2)}, u32[]{:S(2)}) collective-permute-start(f32[4,1024]{1,0:T(4,128)S(1)} %pad_maximum_fusion.1), channel_id=1, source_target_pairs={{0,1},{1,0},{2,3},{3,2},{4,5},{5,4},{6,7},{7,6},{8,9},{9,8},{10,11... | collective-permute-start | bytes 49160 | tf_op jit(solution)/shard_map/ppermute | solution.py:25
  375.4 3.2 copy-start.20
  375.4 4.1 %copy-start.14 = (bf16[4,2,32,1024]{3,2,1,0:T(8,128)(2,1)S(1)}, bf16[4,2,32,1024]{3,2,1,0:T(8,128)(2,1)}, u32[]{:S(2)}) copy-start(bf16[4,2,32,1024]{3,2,1,0:T(8,128)(2,1)} %get-tuple-element.161) | copy-start | bytes 1572868
  378.5 5.3 %copy-start.3 = (f32[512,1024]{1,0:T(8,128)S(1)}, f32[512,1024]{1,0:T(8,128)}, u32[]{:S(2)}) copy-start(f32[512,1024]{1,0:T(8,128)} %copy-done.2) | copy-start | bytes 6291460
  378.5 3.8 collective-permute-start.20
  379.7 14.8 %collective-permute-start.25 = (bf16[4,32,1024]{2,1,0:T(8,128)(2,1)S(1)}, bf16[4,32,1024]{2,1,0:T(8,128)(2,1)S(1)}, u32[]{:S(2)}, u32[]{:S(2)}) collective-permute-start(bf16[4,32,1024]{2,1,0:T(8,128)(2,1)S(1)} %dynamic-slice_bitcast_fusion), channel_id=1, source_target_pairs={{0,16},{8,24},{16,0},{24,8},{1,17},{9,25},{17,1},{25,9},{2,18},{10... | collective-permute-start | bytes 786440 | tf_op jit(solution)/shard_map/ppermute | solution.py:25
  382.4 5.4 %collective-permute-start.21 = (f32[4,1024]{1,0:T(4,128)S(1)}, f32[4,1024]{1,0:T(4,128)S(1)}, u32[]{:S(2)}, u32[]{:S(2)}) collective-permute-start(f32[4,1024]{1,0:T(4,128)S(1)} %add.141), channel_id=1, source_target_pairs={{0,4},{1,5},{2,6},{3,7},{4,0},{5,1},{6,2},{7,3},{8,12},{9,13},{10,... | collective-permute-start | bytes 49160 | tf_op jit(solution)/shard_map/ppermute | solution.py:25
  387.7 7.1 %collective-permute-start.22 = (f32[4,1024]{1,0:T(4,128)S(1)}, f32[4,1024]{1,0:T(4,128)S(1)}, u32[]{:S(2)}, u32[]{:S(2)}) collective-permute-start(f32[4,1024]{1,0:T(4,128)S(1)} %add.142), channel_id=1, source_target_pairs={{0,8},{8,0},{16,24},{24,16},{1,9},{9,1},{17,25},{25,17},{2,10},{10... | collective-permute-start | bytes 49160 | tf_op jit(solution)/shard_map/ppermute | solution.py:25
  394.8 5.0 %collective-permute-start.23 = (f32[4,1024]{1,0:T(4,128)S(1)}, f32[4,1024]{1,0:T(4,128)S(1)}, u32[]{:S(2)}, u32[]{:S(2)}) collective-permute-start(f32[4,1024]{1,0:T(4,128)S(1)} %add.143), channel_id=1, source_target_pairs={{0,16},{8,24},{16,0},{24,8},{1,17},{9,25},{17,1},{25,9},{2,18},{10... | collective-permute-start | bytes 49160 | tf_op jit(solution)/shard_map/ppermute | solution.py:25
  (11 other events, 12.3 us)
Sparse Core Ops, SparseCore 0:
  10.7 92.0 all-gather.4
  124.7 151.2 all-gather.6
where the time goes:
time: 412 us; the launch traced here: 408 us
  Pallas kernels  247 us (60%)
  starting transfers between devices  56.9 us (14%)
  waiting for transfers between devices  45.5 us (11%)
  other arithmetic  17.3 us (4%)
  between operations  14.9 us (4%)
  local copies, waits for them, and re-layouts  12.8 us (3%)
  matrix products  12.8 us (3%)
    pallas_call x2, Pallas kernels, in_sums(): pl.pallas_call(in_kernel, grid_spec=pltpu.PrefetchScalarGridSpec(num_scal...  38.5 us
    pallas_call x1, Pallas kernels, attend_back(): pl.pallas_call(functools.partial(attend_back_kernel, prompt_len), grid=(p...  34.1 us
    pallas_call x1, Pallas kernels, expert_front(): pl.pallas_call(functools.partial(front_kernel, 4), grid=(ff // block,), i...  25.4 us
    ppermute x24, waiting for transfers between devices, swapped(): lax.ppermute(block, axis, [(i, i ^ mask) for i in range(lax.axis_size(axi...  25.3 us
    pallas_call x1, Pallas kernels, attend(): pl.pallas_call(functools.partial(attend_kernel, prompt_len), grid=(pairs,...  23.3 us
    all_to_all x5, starting transfers between devices, all_exchanged(): lax.all_to_all(values, 'expert', split_axis=0, concat_axis=0, tiled=True)  21.4 us
    ppermute x24, starting transfers between devices, swapped(): lax.ppermute(block, axis, [(i, i ^ mask) for i in range(lax.axis_size(axi...  21.1 us
    all_to_all x5, waiting for transfers between devices, all_exchanged(): lax.all_to_all(values, 'expert', split_axis=0, concat_axis=0, tiled=True)  19.4 us
  transfers between devices with their start and end apart: 35, of which 14 were waited for; matrix products, arithmetic and copies ran while one was open for 8% of the time, Pallas kernels for 61%

commit v1 on v0

--- a/solution.py
+++ b/solution.py
@@ -236,13 +236,12 @@
 
 
 def vector_sums(vectors):
-    for axis in ("expert", "group"):
-        for bit in range(lax.axis_size(axis).bit_length() - 1):
-            got = yield swapped(vectors, axis, 1 << bit)
-            vectors = vectors + got
-    part = vectors.shape[1] // (lax.axis_size("group") * lax.axis_size("expert"))
-    place = lax.axis_index("group") * lax.axis_size("expert") + lax.axis_index("expert")
-    return lax.dynamic_slice_in_dim(vectors, place * part, part, axis=1)
+    axes = ("group", "expert")
+    devices = lax.axis_size("group") * lax.axis_size("expert")
+    count, width = vectors.shape
+    pieces = vectors.reshape(count, devices, width // devices).swapaxes(0, 1)
+    got = lax.all_to_all(pieces, axes, split_axis=0, concat_axis=0, tiled=True)
+    return jnp.sum(got, axis=0)
 
 
 def params(*semantics):
@@ -1086,7 +1085,9 @@
     weight_sums = weight_chain(*weights, marks)
     weight_sent = next(weight_sums)
     prompt_sent, prompt_back = moved_on(prompt_sums, prompt_sent)
-    weight_sent, prompt_sent = tied((weight_sent, prompt_sent))
+    result_got = far_got[:, 0].reshape(slots, width)
+    result = rounded(residual + matmul_tn(spread, result_got))
+    weight_sent, prompt_sent, result = tied((weight_sent, prompt_sent, result))
     weight_sent, _ = moved_on(weight_sums, weight_sent)
     prompt_sent, prompt_back = moved_on(prompt_sums, prompt_sent)
     number, _ = tied((numbers(range(groups)), marks[-1]))
@@ -1100,7 +1101,9 @@
     weight_sent, _ = moved_on(weight_sums, weight_sent)
     number, _ = tied((number, marks[-1]))
     in_second, *hidden_second = in_sums(number, 1, *operands)
-    got_first, in_second = tied((got_first, in_second))
+    got_first, in_second, prompt_sent, weight_sent = tied(
+        (got_first, in_second, prompt_sent, weight_sent)
+    )
     got_second = over_group(in_second)
     prompt_sent, weight_sent, number, _ = tied((prompt_sent, weight_sent, number, in_second))
     while prompt_sent is not None:
@@ -1117,23 +1120,18 @@
         norm1_gain,
         grad_resid,
     )
-    number, _ = tied((number, sums1))
+    weight_sent, number, sums1 = tied((weight_sent, number, sums1))
+    weight_sent, weight_grads = moved_on(weight_sums, weight_sent)
     grad_expert_out = out_sums(
         number, (hidden, cot[0]), cot[1], far_got, hidden_first + hidden_second
     )
-    vector_steps = vector_sums(jnp.concatenate([sums1, sums2]))
-    vectors = next(vector_steps)
-    vectors = vector_steps.send(vectors)
-    vectors, got_second, grad_expert_out = tied((vectors, got_second, grad_expert_out))
-    vectors, _ = moved_on(vector_steps, vectors)
-    while vectors is not None:
-        vectors, vector_parts = moved_on(vector_steps, vectors)
-    vectors = vector_parts
+    vectors = jnp.concatenate([sums1, sums2])
+    vectors, got_second, grad_expert_out, weight_sent = tied(
+        (vectors, got_second, grad_expert_out, weight_sent)
+    )
+    vectors = vector_sums(vectors)
     while weight_sent is not None:
         weight_sent, weight_grads = moved_on(weight_sums, weight_sent)
-    far_late, _ = tied((far_got, in_second))
-    result_got = far_late[:, 0].reshape(slots, width)
-    result = rounded(residual + matmul_tn(spread, result_got))
     grad_expert_in = lay_out([got_first, got_second])
     grad_w_output, grad_w_query, grad_w_key, grad_w_value = weight_grads
     return (

time: 412 us -> 402 us (0.976)
  waiting for transfers between devices: 45.5 us -> 37 us
    ppermute x24 -> x19, waiting for transfers between devices: 25.3 us -> 14.3 us  [swapped(): lax.ppermute(block, axis, [(i, i ^ mask) for i in range(lax.axis_size(axi...]
    ppermute x24 -> x19, starting transfers between devices: 21.1 us -> 18.2 us  [swapped(): lax.ppermute(block, axis, [(i, i ^ mask) for i in range(lax.axis_size(axi...]
  transfers between devices with their start and end apart: 35 -> 31, of which waited for: 14 -> 13; matrix products, arithmetic and copies ran while one was open for 8% -> 7% of each run, Pallas kernels for 61% -> 62%
where the time goes in v1:
time: 402 us; the launch traced here: 398 us
  Pallas kernels  248 us (62%)
  starting transfers between devices  56.8 us (14%)
  waiting for transfers between devices  37 us (9%)
  other arithmetic  17.2 us (4%)
  between operations  14.8 us (4%)
  local copies, waits for them, and re-layouts  12.9 us (3%)
  matrix products  11.2 us (3%)
    pallas_call x2, Pallas kernels, in_sums(): pl.pallas_call(in_kernel, grid_spec=pltpu.PrefetchScalarGridSpec(num_scal...  38.8 us
    pallas_call x1, Pallas kernels, attend_back(): pl.pallas_call(functools.partial(attend_back_kernel, prompt_len), grid=(p...  34.1 us
    pallas_call x1, Pallas kernels, expert_front(): pl.pallas_call(functools.partial(front_kernel, 4), grid=(ff // block,), i...  25.4 us
    pallas_call x1, Pallas kernels, attend(): pl.pallas_call(functools.partial(attend_kernel, prompt_len), grid=(pairs,...  23.2 us
    all_to_all x5, starting transfers between devices, all_exchanged(): lax.all_to_all(values, 'expert', split_axis=0, concat_axis=0, tiled=True)  21.2 us
    pallas_call x1, Pallas kernels, weight_parts(): pl.pallas_call(weights_kernel, grid=(groups,), in_specs=[pl.BlockSpec(mem...  18.6 us
    ppermute x19, starting transfers between devices, swapped(): lax.ppermute(block, axis, [(i, i ^ mask) for i in range(lax.axis_size(axi...  18.2 us
    all_to_all x5, waiting for transfers between devices, all_exchanged(): lax.all_to_all(values, 'expert', split_axis=0, concat_axis=0, tiled=True)  18.1 us
  transfers between devices with their start and end apart: 31, of which 13 were waited for; matrix products, arithmetic and copies ran while one was open for 7% of the time, Pallas kernels for 62%

profile of v1, /device:TPU:0, one launch (start us, length us, event | category | flops | bytes accessed | tf_op | source)
XLA Modules:
  0.0 397.7 jit_solution(16580827707788646871)
XLA Ops:
  8.2 2.3 pad_maximum_fusion
  10.6 2.5 collective-permute-start.2
  13.2 2.4 collective-permute-start
  17.4 4.1 %collective-permute-done.refs_1_ = bf16[128,1024]{1,0:T(8,128)(2,1)} collective-permute-done((bf16[128,1024]{1,0:T(8,128)(2,1)S(1)}, bf16[128,1024]{1,0:T(8,128)(2,1)}, u32[]{:S(2)}, u32[]{:S(2)}) %collective-permute-start) | collective-permute-done | bytes 262176 | tf_op jit(solution)/shard_map/ppermute | solution.py:25
  25.4 2.6 fusion.5
  28.6 1.9 collective-permute-done.3.refs_3_
  30.5 3.8 all-to-all-start.1
  35.4 16.9 %project.1 = (bf16[1792,1024]{1,0:T(8,128)(2,1)}, bf16[512,1024]{1,0:T(8,128)(2,1)}, bf16[1792,1024]{1,0:T(8,128)(2,1)}, bf16[1792,1024]{1,0:T(8,128)(2,1)}) custom-call(f32[1,1024]{1,0:T(1,128)} %bitcast.77, f32[1,1024]{1,0:T(1,128)} %bitcast.81, bf16[1024,1024]{1,0:T(8,128)(2,1)} %wq_ref.3, bf16[1024,1024]{1,0:T(8,128)(2,1)} %wk_ref.3, ...), custom_call_target="tpu_custom_call" | custom-call | flops 375809632 | bytes 943718 | tf_op jit(solution)/shard_map/project/pallas_call | solution.py:610
  52.3 23.2 %attend.1 = (bf16[512,1024]{1,0:T(8,128)(2,1)}, f32[8,4,256]{2,1,0:T(4,128)}) custom-call(f32[1]{0:T(128)} %bitcast.1.near_ref, bf16[512,1024]{1,0:T(8,128)(2,1)} %get-tuple-element.102.q_ref, bf16[1792,1024]{1,0:T(8,128)(2,1)} %get-tuple-element.103.k_ref, bf16[1792,1024]{1,0:T(8,128)(2,1)} %get-tuple-element.104.v_ref, f32[1024,128]{1,0:T(8,128)} %compare_select_fusion.bias_ref), custom_call_target="tpu_custom_call" | custom-call | flops 751619264 | bytes 471859 | tf_op jit(solution)/shard_map/attend/pallas_call | solution.py:919
  75.5 3.3 fusion.17
  80.1 2.8 fusion.4
  84.3 4.4 %all-to-all-start = ((bf16[8,128,1024]{2,1,0:T(8,128)(2,1)}), bf16[8,128,1024]{2,1,0:T(8,128)(2,1)S(1)}, u32[]{:S(2)}, u32[]{:S(2)}) async-start(bf16[8,128,1024]{2,1,0:T(8,128)(2,1)} %bitcast.73), calls=%async_computation | async-start | bytes 4194304 | tf_op jit(solution)/shard_map/all_to_all | solution.py:1001
  88.7 13.2 %expert_back.1.gh_ref = bf16[1024,4096]{1,0:T(8,128)(2,1)} custom-call(bf16[1024,1024]{1,0:T(8,128)(2,1)} %bitcast.69, bf16[1,4096,1024]{2,1,0:T(8,128)(2,1)} %wout_ref.7), custom_call_target="tpu_custom_call" | custom-call | flops 429496736 | bytes 838860 | tf_op jit(solution)/shard_map/expert_back/pallas_call | solution.py:269
  104.8 4.0 %spread_rows.2 = bf16[8,1,128,1024]{3,2,1,0:T(8,128)(2,1)} custom-call(s32[1]{0:T(128)} %bitcast.21._, s32[4,1,512]{2,1,0:T(1,128)} %reshape.110.ids_ref, bf16[4,512,1152]{2,1,0:T(8,128)(2,1)} %bitcast.67), custom_call_target="tpu_custom_call" | custom-call | flops 53687092 | bytes 400000 | tf_op jit(solution)/shard_map/spread_rows/pallas_call | solution.py:566
  108.8 6.5 %all-to-all-done = bf16[8,128,1024]{2,1,0:T(8,128)(2,1)S(1)} async-done(((bf16[8,128,1024]{2,1,0:T(8,128)(2,1)}), bf16[8,128,1024]{2,1,0:T(8,128)(2,1)S(1)}, u32[]{:S(2)}, u32[]{:S(2)}) %all-to-all-start) | async-done | bytes 2097184 | tf_op jit(solution)/shard_map/all_to_all | solution.py:1001
  116.7 4.4 %all-to-all-start.2 = ((bf16[8,1,128,1024]{3,2,1,0:T(8,128)(2,1)}), bf16[8,1,128,1024]{3,2,1,0:T(8,128)(2,1)}, u32[]{:S(2)}, u32[]{:S(2)}) async-start(bf16[8,1,128,1024]{3,2,1,0:T(8,128)(2,1)} %spread_rows.2), calls=%async_computation.2 | async-start | bytes 4194304 | tf_op jit(solution)/shard_map/all_to_all | solution.py:1001
  121.8 25.4 %expert_front.1 = (bf16[1024,4096]{1,0:T(8,128)(2,1)}, bf16[1024,4096]{1,0:T(8,128)(2,1)}, bf16[1024,1024]{1,0:T(8,128)(2,1)}) custom-call(bf16[1024,1024]{1,0:T(8,128)(2,1)} %bitcast.63, bf16[1024,4096]{1,0:T(8,128)(2,1)} %expert_back.1.gh_ref, bf16[1,1024,4096]{2,1,0:T(8,128)(2,1)} %win_ref.5), custom_call_target="tpu_custom_call" | custom-call | flops 858993472 | bytes 1677721 | tf_op jit(solution)/shard_map/expert_front/pallas_call | solution.py:316
  147.7 3.6 all-to-all-start.3
  151.9 14.6 %expert_produce.1.refs_0_ = bf16[1024,1024]{1,0:T(8,128)(2,1)} custom-call(bf16[1024,4096]{1,0:T(8,128)(2,1)} %get-tuple-element.113.hidden_ref, bf16[1,4096,1024]{2,1,0:T(8,128)(2,1)} %wout_ref.7), custom_call_target="tpu_custom_call" | custom-call | flops 429496736 | bytes 838860 | tf_op jit(solution)/shard_map/expert_produce/pallas_call | solution.py:354
  166.5 7.7 %spread_rows.3 = bf16[8,3,128,1024]{3,2,1,0:T(8,128)(2,1)} custom-call(s32[2]{0:T(128)} %pad_add_fusion._, s32[4,1,512]{2,1,0:T(1,128)} %reshape.110.ids_ref, bf16[4,512,1152]{2,1,0:T(8,128)(2,1)} %bitcast.68, bf16[1024,1024]{1,0:T(8,128)(2,1)} %expert_produce.1.refs_0_), custom_call_target="tpu_custom_call" | custom-call | flops 161061280 | bytes 400000 | tf_op jit(solution)/shard_map/spread_rows/pallas_call | solution.py:566
  174.2 3.8 all-to-all-done.3
  179.4 5.0 %all-to-all-start.4 = ((bf16[8,3,128,1024]{3,2,1,0:T(8,128)(2,1)}), bf16[8,3,128,1024]{3,2,1,0:T(8,128)(2,1)}, u32[]{:S(2)}, u32[]{:S(2)}) async-start(bf16[8,3,128,1024]{3,2,1,0:T(8,128)(2,1)} %spread_rows.3), calls=%async_computation.4 | async-start | bytes 12582912 | tf_op jit(solution)/shard_map/all_to_all | solution.py:1001
  185.8 7.9 %resid_back.1 = (f32[512,1024]{1,0:T(8,128)}, bf16[512,1024]{1,0:T(8,128)(2,1)}, bf16[512,1024]{1,0:T(8,128)(2,1)}, f32[2,1024]{1,0:T(2,128)}) custom-call(bf16[1024,1024]{1,0:T(8,128)(2,1)} %bitcast.71, bf16[1024,512]{1,0:T(8,128)(2,1)} %fusion.1.spread_ref, f32[512,1024]{1,0:T(8,128)} %copy-done.2, f32[1,1024]{1,0:T(1,128)} %bitcast.82, ...), custom_call_target="tpu_custom_call" | custom-call | flops 107374184 | bytes 419430 | tf_op jit(solution)/shard_map/resid_back/pallas_call | solution.py:710
  193.7 34.1 %attend_back.1 = (bf16[512,1024]{1,0:T(8,128)(2,1)}, bf16[2,512,1024]{2,1,0:T(8,128)(2,1)}, bf16[2,512,1024]{2,1,0:T(8,128)(2,1)}, bf16[2,384,1024]{2,1,0:T(8,128)(2,1)}, bf16[2,384,1024]{2,1,0:T(8,128)(2,1)}) custom-call(f32[1]{0:T(128)} %bitcast.1.near_ref, bf16[512,1024]{1,0:T(8,128)(2,1)} %get-tuple-element.102.q_ref, ...), custom_call_target="tpu_custom_call" | custom-call | flops 1879048192 | bytes 943718 | tf_op jit(solution)/shard_map/attend_back/pallas_call | solution.py:952
  228.2 1.7 collective-permute-start.9
  230.0 18.6 %weight_parts.1 = (bf16[4,4,4,32,1024]{4,3,2,1,0:T(8,128)(2,1)}, bf16[4,4,4,32,1024]{4,3,2,1,0:T(8,128)(2,1)}) custom-call(s32[1]{0:T(128)} %bitcast.odd_ref, bf16[512,1024]{1,0:T(8,128)(2,1)} %get-tuple-element.105.out_ref.refs_0_, bf16[1792,1024]{1,0:T(8,128)(2,1)} %get-tuple-element.106.refs_1_, bf16[512,1024]{1,0:T(8,128)(2,1)} %get-tuple-element.116.refs_2_, ...), custom_call_target="tpu_custom_call" | custom-call | flops 500000000 | bytes 1500000 | tf_op jit(solution)/shard_map/weight_parts/pallas_call | solution.py:667
  248.6 7.3 %all-to-all-done.4.far_ref = bf16[8,3,128,1024]{3,2,1,0:T(8,128)(2,1)} async-done(((bf16[8,3,128,1024]{3,2,1,0:T(8,128)(2,1)}), bf16[8,3,128,1024]{3,2,1,0:T(8,128)(2,1)}, u32[]{:S(2)}, u32[]{:S(2)}) %all-to-all-start.4) | async-done | bytes 6291488 | tf_op jit(solution)/shard_map/all_to_all | solution.py:1001
  256.0 3.2 add_convert_fusion
  260.4 1.8 slice.68
  262.3 2.3 add_convert_fusion.1
  264.6 3.5 collective-permute-done.11
  268.3 5.2 %halve.2 = (bf16[2,4,2,32,1024]{4,3,2,1,0:T(8,128)(2,1)}, bf16[2,4,2,32,1024]{4,3,2,1,0:T(8,128)(2,1)}, bf16[2,4,2,32,1024]{4,3,2,1,0:T(8,128)(2,1)}, bf16[2,4,2,32,1024]{4,3,2,1,0:T(8,128)(2,1)}) custom-call(s32[1]{0:T(128)} %bitcast.26.own_ref, bf16[4,4,4,32,1024]{4,3,2,1,0:T(8,128)(2,1)} %get-tuple-element.131.refs_0_.refs_2_, ...), custom_call_target="tpu_custom_call" | custom-call | flops 104857 | bytes 629145 | tf_op jit(solution)/shard_map/halve/pallas_call | solution.py:159
  276.1 19.5 %in_sums.2 = (bf16[4,256,512]{2,1,0:T(8,128)(2,1)}, bf16[1024,512]{1,0:T(8,128)(2,1)}, bf16[2,1024,512]{2,1,0:T(8,128)(2,1)}) custom-call(s32[4]{0:T(128)} %pad_add_fusion.1._, bf16[1,1024,4096]{2,1,0:T(8,128)(2,1)} %win_ref.5, bf16[1,4096,1024]{2,1,0:T(8,128)(2,1)} %wout_ref.7, bf16[1024,1024]{1,0:T(8,128)(2,1)} %bitcast.64, ...), custom_call_target="tpu_custom_call" | custom-call | flops 644245120 | bytes 800000 | tf_op jit(solution)/shard_map/in_sums/pallas_call | solution.py:405
  295.6 2.8 collective-permute-done.13.refs_1_
  299.4 5.1 %all-to-all-start.5 = ((bf16[4,256,512]{2,1,0:T(8,128)(2,1)}), bf16[4,256,512]{2,1,0:T(8,128)(2,1)S(1)}, u32[]{:S(2)}, u32[]{:S(2)}) async-start(bf16[4,256,512]{2,1,0:T(8,128)(2,1)} %get-tuple-element.140), calls=%async_computation.5 | async-start | bytes 2097152 | tf_op jit(solution)/shard_map/all_to_all | solution.py:1096
  304.5 2.2 add_convert_fusion.6
  309.1 3.3 halve.3
  314.1 19.3 %in_sums.3 = (bf16[4,256,512]{2,1,0:T(8,128)(2,1)}, bf16[1024,512]{1,0:T(8,128)(2,1)}, bf16[2,1024,512]{2,1,0:T(8,128)(2,1)}) custom-call(s32[4]{0:T(128)} %pad_add_fusion.1._, bf16[1,1024,4096]{2,1,0:T(8,128)(2,1)} %win_ref.5, bf16[1,4096,1024]{2,1,0:T(8,128)(2,1)} %wout_ref.7, bf16[1024,1024]{1,0:T(8,128)(2,1)} %bitcast.65, ...), custom_call_target="tpu_custom_call" | custom-call | flops 644245120 | bytes 800000 | tf_op jit(solution)/shard_map/in_sums/pallas_call | solution.py:405
  334.3 5.4 %all-to-all-start.6 = ((bf16[4,256,512]{2,1,0:T(8,128)(2,1)}), bf16[4,256,512]{2,1,0:T(8,128)(2,1)}, u32[]{:S(2)}, u32[]{:S(2)}) async-start(bf16[4,256,512]{2,1,0:T(8,128)(2,1)} %get-tuple-element.155), calls=%async_computation.6 | async-start | bytes 2097152 | tf_op jit(solution)/shard_map/all_to_all | solution.py:1096
  339.7 2.3 add_convert_fusion.5.prompt_ref
  342.0 10.6 %input_back.1 = (bf16[512,1024]{1,0:T(8,128)(2,1)}, f32[2,1024]{1,0:T(2,128)}) custom-call(bf16[2,128,1024]{2,1,0:T(8,128)(2,1)} %add_convert_fusion.5.prompt_ref, bf16[2,384,1024]{2,1,0:T(8,128)(2,1)} %get-tuple-element.123.refs_7_.own_ref, bf16[2,384,1024]{2,1,0:T(8,128)(2,1)} %collective-permute-done.9.near_ref, ...), custom_call_target="tpu_custom_call" | custom-call | flops 161061280 | bytes 524288 | tf_op jit(solution)/shard_map/input_back/pallas_call | solution.py:777
  352.6 2.7 turn.1
  355.3 2.0 collective-permute-start.19
  357.4 17.3 %out_sums.1 = f32[1,1024,1024]{2,1,0:T(8,128)} custom-call(s32[4]{0:T(128)} %pad_add_fusion.1._, bf16[1024,4096]{1,0:T(8,128)(2,1)} %get-tuple-element.113.hidden_ref, bf16[1024,1024]{1,0:T(8,128)(2,1)} %bitcast.70, bf16[8,1,128,1024]{3,2,1,0:T(8,128)(2,1)} %all-to-all-done.2.near_ref, bf16[8,3,128,1024]{3,2,1,0:T(8,128)(2,1)} %all-to-all-done.4.far_ref, ...), custom_call_target="tpu_custom_call" | custom-call | flops 429496736 | bytes 800000 | tf_op jit(solution)/shard_map/out_sums/pallas_call | solution.py:471
  374.9 2.4 collective-permute-start.20
  378.2 2.5 all-to-all-start.7
  380.8 4.2 %lay_out.1 = f32[1,256,4096]{2,1,0:T(8,128)} custom-call(bf16[4,256,512]{2,1,0:T(8,128)(2,1)} %copy-done.5, bf16[4,256,512]{2,1,0:T(8,128)(2,1)} %all-to-all-done.6.refs_1_), custom_call_target="tpu_custom_call" | custom-call | flops 52428 | bytes 314572 | tf_op jit(solution)/shard_map/lay_out/pallas_call | solution.py:506
  384.9 2.9 all-to-all-done.7
  (118 shorter events, 34.3 us)
Async XLA Ops:
  7.2 3.4 copy-start.6
  7.2 95.6 %all-gather.5.cloned.1.call-start = ((), (), s32[]{:S(2)}) async-start(), calls=%async_computation.8 | async-start | bytes 5898240 | tf_op jit(solution)/shard_map/all_gather | solution.py:1014
  10.5 6.6 %copy-start.16 = (s32[512,1]{0,1:T(1,128)S(1)}, s32[512,1]{0,1:T(1,128)}, u32[]{:S(2)}) copy-start(s32[512,1]{0,1:T(1,128)} %param.15) | copy-start | bytes 6148
  10.5 14.9 %copy-start.7 = (bf16[512,1024]{1,0:T(8,128)(2,1)S(1)}, bf16[512,1024]{1,0:T(8,128)(2,1)}, u32[]{:S(2)}) copy-start(bf16[512,1024]{1,0:T(8,128)(2,1)} %cot_ref.1) | copy-start | bytes 3145732
  10.6 17.4 %copy-start.8 = (bf16[384,1024]{1,0:T(8,128)(2,1)}, bf16[384,1024]{1,0:T(8,128)(2,1)S(1)}, u32[]{:S(2)}) copy-start(bf16[384,1024]{1,0:T(8,128)(2,1)S(1)} %slice.63.refs_9_) | copy-start | bytes 2359300
  10.6 12.3 %collective-permute-start.2 = (bf16[384,1024]{1,0:T(8,128)(2,1)S(1)}, bf16[384,1024]{1,0:T(8,128)(2,1)S(1)}, u32[]{:S(2)}, u32[]{:S(2)}) collective-permute-start(bf16[384,1024]{1,0:T(8,128)(2,1)S(1)} %slice.63.refs_9_), channel_id=1, source_target_pairs={{0,1},{2,3},{4,5},{6,7},{8,9},{10,11},{12,13},{14,15},{16,17},{18,... | collective-permute-start | bytes 2359304 | tf_op jit(solution)/shard_map/ppermute | solution.py:1007
  13.2 14.8 %copy-start.11 = (bf16[128,1024]{1,0:T(8,128)(2,1)}, bf16[128,1024]{1,0:T(8,128)(2,1)S(1)}, u32[]{:S(2)}) copy-start(bf16[128,1024]{1,0:T(8,128)(2,1)S(1)} %slice.62.refs_0_) | copy-start | bytes 786436
  13.2 8.3 %collective-permute-start = (bf16[128,1024]{1,0:T(8,128)(2,1)S(1)}, bf16[128,1024]{1,0:T(8,128)(2,1)}, u32[]{:S(2)}, u32[]{:S(2)}) collective-permute-start(bf16[128,1024]{1,0:T(8,128)(2,1)S(1)} %slice.62.refs_0_), channel_id=1, source_target_pairs={{0,2},{1,3},{2,0},{3,1},{4,6},{5,7},{6,4},{7,5},{8,10},{9,11},{10,... | collective-permute-start | bytes 786440 | tf_op jit(solution)/shard_map/ppermute | solution.py:25
  15.6 7.4 %collective-permute-start.1 = (bf16[128,1024]{1,0:T(8,128)(2,1)S(1)}, bf16[128,1024]{1,0:T(8,128)(2,1)}, u32[]{:S(2)}, u32[]{:S(2)}) collective-permute-start(bf16[128,1024]{1,0:T(8,128)(2,1)S(1)} %slice.62.refs_0_), channel_id=1, source_target_pairs={{0,4},{1,5},{2,6},{3,7},{4,0},{5,1},{6,2},{7,3},{8,12},{9,13},{10,... | collective-permute-start | bytes 786440 | tf_op jit(solution)/shard_map/ppermute | solution.py:25
  17.1 18.3 %collective-permute-start.4 = (bf16[128,1024]{1,0:T(8,128)(2,1)S(1)}, bf16[128,1024]{1,0:T(8,128)(2,1)}, u32[]{:S(2)}, u32[]{:S(2)}) collective-permute-start(bf16[128,1024]{1,0:T(8,128)(2,1)S(1)} %slice.62.refs_0_), channel_id=1, source_target_pairs={{0,1},{1,0},{2,3},{3,2},{4,5},{5,4},{6,7},{7,6},{8,9},{9,8},{10,11... | collective-permute-start | bytes 786440 | tf_op jit(solution)/shard_map/ppermute | solution.py:25
  23.8 6.7 %collective-permute-start.3 = (bf16[128,1024]{1,0:T(8,128)(2,1)}, bf16[128,1024]{1,0:T(8,128)(2,1)}, u32[]{:S(2)}, u32[]{:S(2)}) collective-permute-start(bf16[128,1024]{1,0:T(8,128)(2,1)} %collective-permute-done.refs_1_), channel_id=1, source_target_pairs={{0,4},{1,5},{2,6},{3,7},{4,0},{5,1},{6,2},{7,3},{8,12},{9,13},{10,... | collective-permute-start | bytes 786440 | tf_op jit(solution)/shard_map/ppermute | solution.py:25
  28.1 7.2 %collective-permute-start.5 = (bf16[128,1024]{1,0:T(8,128)(2,1)}, bf16[128,1024]{1,0:T(8,128)(2,1)}, u32[]{:S(2)}, u32[]{:S(2)}) collective-permute-start(bf16[128,1024]{1,0:T(8,128)(2,1)} %collective-permute-done.refs_1_), channel_id=1, source_target_pairs={{0,1},{1,0},{2,3},{3,2},{4,5},{5,4},{6,7},{7,6},{8,9},{9,8},{10,11... | collective-permute-start | bytes 786440 | tf_op jit(solution)/shard_map/ppermute | solution.py:25
  28.1 7.2 %collective-permute-start.6 = (bf16[128,1024]{1,0:T(8,128)(2,1)}, bf16[128,1024]{1,0:T(8,128)(2,1)}, u32[]{:S(2)}, u32[]{:S(2)}) collective-permute-start(bf16[128,1024]{1,0:T(8,128)(2,1)} %collective-permute-done.1.refs_2_), channel_id=1, source_target_pairs={{0,1},{1,0},{2,3},{3,2},{4,5},{5,4},{6,7},{7,6},{8,9},{9,8},{10,11... | collective-permute-start | bytes 786440 | tf_op jit(solution)/shard_map/ppermute | solution.py:25
  30.5 4.8 %collective-permute-start.7 = (bf16[128,1024]{1,0:T(8,128)(2,1)}, bf16[128,1024]{1,0:T(8,128)(2,1)}, u32[]{:S(2)}, u32[]{:S(2)}) collective-permute-start(bf16[128,1024]{1,0:T(8,128)(2,1)} %collective-permute-done.3.refs_3_), channel_id=1, source_target_pairs={{0,1},{1,0},{2,3},{3,2},{4,5},{5,4},{6,7},{7,6},{8,9},{9,8},{10,11... | collective-permute-start | bytes 786440 | tf_op jit(solution)/shard_map/ppermute | solution.py:25
  30.5 52.4 %all-to-all-start.1 = ((bf16[8,128,1024]{2,1,0:T(8,128)(2,1)}), bf16[8,128,1024]{2,1,0:T(8,128)(2,1)S(1)}, u32[]{:S(2)}, u32[]{:S(2)}) async-start(bf16[8,128,1024]{2,1,0:T(8,128)(2,1)} %bitcast.72), calls=%async_computation.1 | async-start | bytes 4194304 | tf_op jit(solution)/shard_map/all_to_all | solution.py:1001
  78.8 1.3 copy-start.2
  78.8 1.3 copy-start.19
  82.9 1.4 copy-start.1
  84.3 31.0 %all-to-all-start = ((bf16[8,128,1024]{2,1,0:T(8,128)(2,1)}), bf16[8,128,1024]{2,1,0:T(8,128)(2,1)S(1)}, u32[]{:S(2)}, u32[]{:S(2)}) async-start(bf16[8,128,1024]{2,1,0:T(8,128)(2,1)} %bitcast.73), calls=%async_computation | async-start | bytes 4194304 | tf_op jit(solution)/shard_map/all_to_all | solution.py:1001
  115.3 1.4 copy-start
  116.7 31.0 %all-to-all-start.2 = ((bf16[8,1,128,1024]{3,2,1,0:T(8,128)(2,1)}), bf16[8,1,128,1024]{3,2,1,0:T(8,128)(2,1)}, u32[]{:S(2)}, u32[]{:S(2)}) async-start(bf16[8,1,128,1024]{3,2,1,0:T(8,128)(2,1)} %spread_rows.2), calls=%async_computation.2 | async-start | bytes 4194304 | tf_op jit(solution)/shard_map/all_to_all | solution.py:1001
  121.0 155.1 %all-gather.7.cloned.1.call-start = ((), (), s32[]{:S(2)}) async-start(), calls=%async_computation.9 | async-start | bytes 10485760 | tf_op jit(solution)/shard_map/all_gather | solution.py:1051
  147.7 30.3 %all-to-all-start.3 = ((bf16[8,128,1024]{2,1,0:T(8,128)(2,1)}), bf16[8,128,1024]{2,1,0:T(8,128)(2,1)S(1)}, u32[]{:S(2)}, u32[]{:S(2)}) async-start(bf16[8,128,1024]{2,1,0:T(8,128)(2,1)} %bitcast.74), calls=%async_computation.3 | async-start | bytes 4194304 | tf_op jit(solution)/shard_map/all_to_all | solution.py:1001
  178.0 1.4 copy-start.4
  179.4 76.6 %all-to-all-start.4 = ((bf16[8,3,128,1024]{3,2,1,0:T(8,128)(2,1)}), bf16[8,3,128,1024]{3,2,1,0:T(8,128)(2,1)}, u32[]{:S(2)}, u32[]{:S(2)}) async-start(bf16[8,3,128,1024]{3,2,1,0:T(8,128)(2,1)} %spread_rows.3), calls=%async_computation.4 | async-start | bytes 12582912 | tf_op jit(solution)/shard_map/all_to_all | solution.py:1001
  227.8 20.8 %collective-permute-start.8 = (bf16[2,512,1024]{2,1,0:T(8,128)(2,1)}, bf16[2,512,1024]{2,1,0:T(8,128)(2,1)S(1)}, u32[]{:S(2)}, u32[]{:S(2)}) collective-permute-start(bf16[2,512,1024]{2,1,0:T(8,128)(2,1)} %get-tuple-element.121.refs_5_), channel_id=1, source_target_pairs={{0,1},{1,0},{2,3},{3,2},{4,5},{5,4},{6,7},{7,6},{8,9},{9,8},{10,11... | collective-permute-start | bytes 6291464 | tf_op jit(solution)/shard_map/ppermute | solution.py:25
  228.2 20.4 %collective-permute-start.9 = (bf16[2,384,1024]{2,1,0:T(8,128)(2,1)}, bf16[2,384,1024]{2,1,0:T(8,128)(2,1)}, u32[]{:S(2)}, u32[]{:S(2)}) collective-permute-start(bf16[2,384,1024]{2,1,0:T(8,128)(2,1)} %get-tuple-element.122.refs_6_), channel_id=1, source_target_pairs={{1,0},{3,2},{5,4},{7,6},{9,8},{11,10},{13,12},{15,14},{17,16},{19,... | collective-permute-start | bytes 4718600 | tf_op jit(solution)/shard_map/ppermute | solution.py:1070
  248.6 7.3 %copy-start.9 = (bf16[2,512,1024]{2,1,0:T(8,128)(2,1)}, bf16[2,512,1024]{2,1,0:T(8,128)(2,1)S(1)}, u32[]{:S(2)}) copy-start(bf16[2,512,1024]{2,1,0:T(8,128)(2,1)S(1)} %collective-permute-done.8) | copy-start | bytes 6291460
  256.0 12.3 %collective-permute-start.10 = (bf16[4,4,4,32,1024]{4,3,2,1,0:T(8,128)(2,1)}, bf16[4,4,4,32,1024]{4,3,2,1,0:T(8,128)(2,1)}, u32[]{:S(2)}, u32[]{:S(2)}) collective-permute-start(bf16[4,4,4,32,1024]{4,3,2,1,0:T(8,128)(2,1)} %get-tuple-element.127), channel_id=1, source_target_pairs={{0,1},{1,0},{2,3},{3,2},{4,5},{5,4},{6,7},{7,6},{8,9},{9,8},{10,11... | collective-permute-start | bytes 12582920 | tf_op jit(solution)/shard_map/ppermute | solution.py:25
  259.2 8.8 %collective-permute-start.11 = (bf16[2,64,1024]{2,1,0:T(8,128)(2,1)S(1)}, bf16[2,64,1024]{2,1,0:T(8,128)(2,1)S(1)}, u32[]{:S(2)}, u32[]{:S(2)}) collective-permute-start(bf16[2,64,1024]{2,1,0:T(8,128)(2,1)S(1)} %get-tuple-element.185), channel_id=1, source_target_pairs={{0,4},{1,5},{2,6},{3,7},{4,0},{5,1},{6,2},{7,3},{8,12},{9,13},{10,... | collective-permute-start | bytes 786440 | tf_op jit(solution)/shard_map/ppermute | solution.py:25
  259.8 2.4 copy-start.3
  259.8 8.4 %collective-permute-start.12 = (bf16[2,64,1024]{2,1,0:T(8,128)(2,1)S(1)}, bf16[2,64,1024]{2,1,0:T(8,128)(2,1)S(1)}, u32[]{:S(2)}, u32[]{:S(2)}) collective-permute-start(bf16[2,64,1024]{2,1,0:T(8,128)(2,1)S(1)} %get-tuple-element.184), channel_id=1, source_target_pairs={{0,2},{1,3},{2,0},{3,1},{4,6},{5,7},{6,4},{7,5},{8,10},{9,11},{10,... | collective-permute-start | bytes 786440 | tf_op jit(solution)/shard_map/ppermute | solution.py:25
  268.3 5.2 %copy-start.15 = (bf16[2,64,1024]{2,1,0:T(8,128)(2,1)}, bf16[2,64,1024]{2,1,0:T(8,128)(2,1)S(1)}, u32[]{:S(2)}) copy-start(bf16[2,64,1024]{2,1,0:T(8,128)(2,1)S(1)} %collective-permute-done.12) | copy-start | bytes 786436
  273.5 24.9 %collective-permute-start.13 = (bf16[2,4,2,32,1024]{4,3,2,1,0:T(8,128)(2,1)}, bf16[2,4,2,32,1024]{4,3,2,1,0:T(8,128)(2,1)S(1)}, u32[]{:S(2)}, u32[]{:S(2)}) collective-permute-start(bf16[2,4,2,32,1024]{4,3,2,1,0:T(8,128)(2,1)} %get-tuple-element.133), channel_id=1, source_target_pairs={{0,2},{1,3},{2,0},{3,1},{4,6},{5,7},{6,4},{7,5},{8,10},{9,11},{10,... | collective-permute-start | bytes 3145736 | tf_op jit(solution)/shard_map/ppermute | solution.py:25
  274.2 24.6 %collective-permute-start.14 = (bf16[2,4,2,32,1024]{4,3,2,1,0:T(8,128)(2,1)}, bf16[2,4,2,32,1024]{4,3,2,1,0:T(8,128)(2,1)}, u32[]{:S(2)}, u32[]{:S(2)}) collective-permute-start(bf16[2,4,2,32,1024]{4,3,2,1,0:T(8,128)(2,1)} %get-tuple-element.134), channel_id=1, source_target_pairs={{0,4},{1,5},{2,6},{3,7},{4,0},{5,1},{6,2},{7,3},{8,12},{9,13},{10,... | collective-permute-start | bytes 3145736 | tf_op jit(solution)/shard_map/ppermute | solution.py:25
  299.4 34.9 %all-to-all-start.5 = ((bf16[4,256,512]{2,1,0:T(8,128)(2,1)}), bf16[4,256,512]{2,1,0:T(8,128)(2,1)S(1)}, u32[]{:S(2)}, u32[]{:S(2)}) async-start(bf16[4,256,512]{2,1,0:T(8,128)(2,1)} %get-tuple-element.140), calls=%async_computation.5 | async-start | bytes 2097152 | tf_op jit(solution)/shard_map/all_to_all | solution.py:1096
  306.7 26.7 %collective-permute-start.15 = (bf16[2,128,1024]{2,1,0:T(8,128)(2,1)}, bf16[2,128,1024]{2,1,0:T(8,128)(2,1)}, u32[]{:S(2)}, u32[]{:S(2)}) collective-permute-start(bf16[2,128,1024]{2,1,0:T(8,128)(2,1)} %get-tuple-element.183), channel_id=1, source_target_pairs={{0,2},{1,3},{2,0},{3,1},{4,6},{5,7},{6,4},{7,5},{8,10},{9,11},{10,... | collective-permute-start | bytes 1572872 | tf_op jit(solution)/shard_map/ppermute | solution.py:25
  307.6 25.8 %collective-permute-start.16 = (bf16[2,128,1024]{2,1,0:T(8,128)(2,1)}, bf16[2,128,1024]{2,1,0:T(8,128)(2,1)}, u32[]{:S(2)}, u32[]{:S(2)}) collective-permute-start(bf16[2,128,1024]{2,1,0:T(8,128)(2,1)} %get-tuple-element.182), channel_id=1, source_target_pairs={{0,4},{1,5},{2,6},{3,7},{4,0},{5,1},{6,2},{7,3},{8,12},{9,13},{10,... | collective-permute-start | bytes 1572872 | tf_op jit(solution)/shard_map/ppermute | solution.py:25
  312.4 21.1 %collective-permute-start.17 = (bf16[2,4,1,32,1024]{4,3,2,1,0:T(8,128)(2,1)}, bf16[2,4,1,32,1024]{4,3,2,1,0:T(8,128)(2,1)S(1)}, u32[]{:S(2)}, u32[]{:S(2)}) collective-permute-start(bf16[2,4,1,32,1024]{4,3,2,1,0:T(8,128)(2,1)} %get-tuple-element.149), channel_id=1, source_target_pairs={{0,4},{1,5},{2,6},{3,7},{4,0},{5,1},{6,2},{7,3},{8,12},{9,13},{10,... | collective-permute-start | bytes 1572872 | tf_op jit(solution)/shard_map/ppermute | solution.py:25
  313.0 21.3 %collective-permute-start.18 = (bf16[2,4,1,32,1024]{4,3,2,1,0:T(8,128)(2,1)}, bf16[2,4,1,32,1024]{4,3,2,1,0:T(8,128)(2,1)}, u32[]{:S(2)}, u32[]{:S(2)}) collective-permute-start(bf16[2,4,1,32,1024]{4,3,2,1,0:T(8,128)(2,1)} %get-tuple-element.150), channel_id=1, source_target_pairs={{0,2},{1,3},{2,0},{3,1},{4,6},{5,7},{6,4},{7,5},{8,10},{9,11},{10,... | collective-permute-start | bytes 1572872 | tf_op jit(solution)/shard_map/ppermute | solution.py:25
  334.3 7.7 %copy-start.5 = (bf16[4,256,512]{2,1,0:T(8,128)(2,1)}, bf16[4,256,512]{2,1,0:T(8,128)(2,1)S(1)}, u32[]{:S(2)}) copy-start(bf16[4,256,512]{2,1,0:T(8,128)(2,1)S(1)} %all-to-all-done.5.refs_0_) | copy-start | bytes 3145732
  334.3 40.4 %all-to-all-start.6 = ((bf16[4,256,512]{2,1,0:T(8,128)(2,1)}), bf16[4,256,512]{2,1,0:T(8,128)(2,1)}, u32[]{:S(2)}, u32[]{:S(2)}) async-start(bf16[4,256,512]{2,1,0:T(8,128)(2,1)} %get-tuple-element.155), calls=%async_computation.6 | async-start | bytes 2097152 | tf_op jit(solution)/shard_map/all_to_all | solution.py:1096
  355.3 19.3 %collective-permute-start.19 = (bf16[4,2,32,1024]{3,2,1,0:T(8,128)(2,1)}, bf16[4,2,32,1024]{3,2,1,0:T(8,128)(2,1)S(1)}, u32[]{:S(2)}, u32[]{:S(2)}) collective-permute-start(bf16[4,2,32,1024]{3,2,1,0:T(8,128)(2,1)} %get-tuple-element.175), channel_id=1, source_target_pairs={{0,8},{8,0},{16,24},{24,16},{1,9},{9,1},{17,25},{25,17},{2,10},{10... | collective-permute-start | bytes 1572872 | tf_op jit(solution)/shard_map/ppermute | solution.py:25
  357.4 17.3 %copy-start.17 = (f32[2,1024]{1,0:T(2,128)S(1)}, f32[2,1024]{1,0:T(2,128)}, u32[]{:S(2)}) copy-start(f32[2,1024]{1,0:T(2,128)} %get-tuple-element.166) | copy-start | bytes 24580
  357.4 17.3 %copy-start.18 = (f32[2,1024]{1,0:T(2,128)S(1)}, f32[2,1024]{1,0:T(2,128)}, u32[]{:S(2)}) copy-start(f32[2,1024]{1,0:T(2,128)} %get-tuple-element.165) | copy-start | bytes 24580
  357.4 17.3 %copy-start.14 = (bf16[4,2,32,1024]{3,2,1,0:T(8,128)(2,1)S(1)}, bf16[4,2,32,1024]{3,2,1,0:T(8,128)(2,1)}, u32[]{:S(2)}) copy-start(bf16[4,2,32,1024]{3,2,1,0:T(8,128)(2,1)} %get-tuple-element.177) | copy-start | bytes 1572868
  374.9 14.8 %collective-permute-start.20 = (bf16[4,32,1024]{2,1,0:T(8,128)(2,1)S(1)}, bf16[4,32,1024]{2,1,0:T(8,128)(2,1)S(1)}, u32[]{:S(2)}, u32[]{:S(2)}) collective-permute-start(bf16[4,32,1024]{2,1,0:T(8,128)(2,1)S(1)} %dynamic-slice_bitcast_fusion), channel_id=1, source_target_pairs={{0,16},{8,24},{16,0},{24,8},{1,17},{9,25},{17,1},{25,9},{2,18},{10... | collective-permute-start | bytes 786440 | tf_op jit(solution)/shard_map/ppermute | solution.py:25
  378.2 9.6 %all-to-all-start.7 = ((f32[32,1,128]{2,1,0:T(1,128)}), f32[32,1,128]{2,1,0:T(1,128)S(1)}, u32[]{:S(2)}, u32[]{:S(2)}) async-start(f32[32,1,128]{2,1,0:T(1,128)} %reshape.113), calls=%async_computation.7 | async-start | bytes 32768 | tf_op jit(solution)/shard_map/all_to_all | solution.py:243
  (4 other events, 4.0 us)
Sparse Core Ops, SparseCore 0:
  10.6 92.0 all-gather.4
  123.5 151.2 all-gather.6

commit v2 on v1

--- a/solution.py
+++ b/solution.py
@@ -368,32 +368,49 @@
 
 
 def in_kernel(
-    _, win_ref, wout_ref, own_rows_ref, own_pre_ref, near_rows_ref, near_ref, rows_ref, far_ref,
-    in_ref, near_hidden_ref, hidden_ref, in_sum,
+    half, number_ref, own_rows_ref, own_pre_ref, win_hbm, wout_hbm, rows_hbm, near_hbm, far_hbm,
+    in_ref, near_out, far_out, in_sum, win_ref, wout_ref, rows_ref, cot_ref, hidden_ref,
+    weight_sems, shard_sems, out_sems,
 ):
-    step = pl.program_id(0)
-
-    def shard(rows, cot):
-        pre = matmul(rows, win_ref[0])
-        grad_hidden = matmul_nt(cot, wout_ref[0])
+    shards, count, _ = rows_ref.shape
+    block = win_ref.shape[1]
+    place = pl.multiple_of((2 * number_ref[0] + half) * block, block)
+    weights = [
+        pltpu.make_async_copy(win_hbm.at[0, :, pl.ds(place, block)], win_ref, weight_sems.at[0]),
+        pltpu.make_async_copy(wout_hbm.at[0, pl.ds(place, block), :], wout_ref, weight_sems.at[1]),
+    ]
+    copies, outs = [], []
+    for i in range(shards):
+        cot = near_hbm.at[:, 0] if i == 0 else far_hbm.at[:, i]
+        rows = rows_hbm.at[number_ref[1 + i]]
+        copies.append(
+            [
+                pltpu.make_async_copy(rows, rows_ref.at[i], shard_sems.at[i, 0]),
+                pltpu.make_async_copy(cot, cot_ref.at[i], shard_sems.at[i, 1]),
+            ]
+        )
+        out = near_out if i == 0 else far_out.at[i - 1]
+        outs.append(pltpu.make_async_copy(hidden_ref.at[i], out, out_sems.at[i]))
+    for copy in weights + [copy for pair in copies for copy in pair]:
+        copy.start()
+    in_sum[...] = matmul_tn(own_rows_ref[...], own_pre_ref[...])
+    for copy in weights:
+        copy.wait()
+    for i in range(shards):
+        for copy in copies[i]:
+            copy.wait()
+        rows = rows_ref[i]
+        pre = matmul(rows, win_ref[...])
+        grad_hidden = matmul_nt(cot_ref[i].reshape(rows.shape), wout_ref[...])
         sig = logistic(pre)
         hidden = pre * sig
+        hidden_ref[i] = rounded(hidden)
+        outs[i].start()
         grad_pre = rounded(grad_hidden * sig * (1.0 + pre - hidden))
-        return rounded(hidden), matmul_tn(rows, grad_pre)
-
-    @pl.when(step == 0)
-    def _():
-        rows = near_rows_ref[0]
-        near_hidden_ref[...], inner = shard(rows, near_ref[...].reshape(rows.shape))
-        in_sum[...] = matmul_tn(own_rows_ref[...], own_pre_ref[...]) + inner
-
-    rows = rows_ref[0]
-    hidden_ref[0], inner = shard(rows, far_ref[...].reshape(rows.shape))
-    in_sum[...] += inner
-
-    @pl.when(step == pl.num_programs(0) - 1)
-    def _():
-        in_ref[...] = rounded(in_sum[...]).reshape(in_ref.shape)
+        in_sum[...] += matmul_tn(rows, grad_pre)
+    in_ref[...] = rounded(in_sum[...]).reshape(in_ref.shape)
+    for copy in outs:
+        copy.wait()
 
 
 def in_sums(number, half, expert_in, expert_out, own, rows, near, far):
@@ -401,28 +418,34 @@
     sources, _, slots, _ = near.shape
     part = expert_in.shape[2] // groups
     block = part // 2
-    column = lambda j, w: 2 * w[0] + half
-    return pl.pallas_call(
-        in_kernel,
+    shards = groups - 1
+    there = pl.BlockSpec(memory_space=pl.ANY)
+    return pl.pallas_call(
+        functools.partial(in_kernel, half),
         grid_spec=pltpu.PrefetchScalarGridSpec(
             num_scalar_prefetch=1,
-            grid=(groups - 2,),
+            grid=(1,),
             in_specs=[
-                pl.BlockSpec((1, width, block), lambda j, w: (0, 0, column(j, w))),
-                pl.BlockSpec((1, block, width), lambda j, w: (0, column(j, w), 0)),
                 pl.BlockSpec((count, width), lambda j, w: (0, 0)),
-                pl.BlockSpec((count, block), lambda j, w: (0, column(j, w))),
-                pl.BlockSpec((1, count, width), lambda j, w: (w[1], 0, 0)),
-                pl.BlockSpec((sources, 1, slots, width), lambda j, w: (0, 0, 0, 0)),
-                pl.BlockSpec((1, count, width), lambda j, w: (w[2 + j], 0, 0)),
-                pl.BlockSpec((sources, 1, slots, width), lambda j, w: (0, 1 + j, 0, 0)),
-            ],
+                pl.BlockSpec((count, block), lambda j, w: (0, 2 * w[0] + half)),
+            ]
+            + [there] * 5,
             out_specs=[
                 pl.BlockSpec((groups, width // groups, block), lambda j, w: (0, 0, 0)),
-                pl.BlockSpec((count, block), lambda j, w: (0, 0)),
-                pl.BlockSpec((1, count, block), lambda j, w: (j, 0, 0)),
+                there,
+                there,
             ],
-            scratch_shapes=[pltpu.VMEM((width, block), f32)],
+            scratch_shapes=[
+                pltpu.VMEM((width, block), f32),
+                pltpu.VMEM((width, block), bf16),
+                pltpu.VMEM((block, width), bf16),
+                pltpu.VMEM((shards, count, width), bf16),
+                pltpu.VMEM((shards, sources, slots, width), bf16),
+                pltpu.VMEM((shards, count, block), bf16),
+                pltpu.SemaphoreType.DMA((2,)),
+                pltpu.SemaphoreType.DMA((shards, 2)),
+                pltpu.SemaphoreType.DMA((shards,)),
+            ],
         ),
         out_shape=[
             jax.ShapeDtypeStruct((groups, width // groups, block), bf16),
@@ -432,25 +455,50 @@
         compiler_params=params("arbitrary"),
         cost_estimate=cost(6 * count * width * block * groups, 16e6, count * block * groups),
         name="in_sums",
-    )(number, expert_in, expert_out, *own, rows, near, rows, far)
-
-
-def out_kernel(_, hidden_ref, cot_ref, near_ref, far_ref, *refs):
+    )(number, *own, expert_in, expert_out, rows, near, far)
+
+
+def own_kernel(_, hidden_ref, cot_ref, out_ref):
+    out_ref[...] = matmul_tn(hidden_ref[...], cot_ref[...])
+
+
+def own_out(number, groups, hidden, cot):
+    count, width = cot.shape
+    part = hidden.shape[1] // groups
+    block = part // 2
+    return pl.pallas_call(
+        own_kernel,
+        grid_spec=pltpu.PrefetchScalarGridSpec(
+            num_scalar_prefetch=1,
+            grid=(2,),
+            in_specs=[
+                pl.BlockSpec((count, block), lambda j, w: (0, 2 * w[0] + j)),
+                pl.BlockSpec((count, width), lambda j, w: (0, 0)),
+            ],
+            out_specs=pl.BlockSpec((block, width), lambda j, w: (j, 0)),
+        ),
+        out_shape=jax.ShapeDtypeStruct((part, width), f32),
+        compiler_params=params("arbitrary"),
+        cost_estimate=cost(2 * count * width * part, 8e6),
+        name="own_out",
+    )(number, hidden, cot)
+
+
+def out_kernel(own_ref, near_ref, far_ref, *refs):
     out_ref, total = refs[-2:]
     hiddens = refs[:-2]
     block = total.shape[0] // 2
+    count = hiddens[0].shape[0]
     step = pl.program_id(0)
-    cot = cot_ref[...]
 
     @pl.when(step == 0)
     def _():
-        total[...] = matmul_tn(hidden_ref[...], cot)
-        near = near_ref[...].reshape(cot.shape)
+        near = near_ref[...].reshape(count, -1)
         for half in range(2):
             here = pl.ds(half * block, block)
-            total[here, :] += matmul_tn(hiddens[2 * half][...], near)
-
-    far = far_ref[...].reshape(cot.shape)
+            total[here, :] = own_ref[here, :] + matmul_tn(hiddens[2 * half][...], near)
+
+    far = far_ref[...].reshape(count, -1)
     for half in range(2):
         here = pl.ds(half * block, block)
         total[here, :] += matmul_tn(hiddens[2 * half + 1][0], far)
@@ -460,34 +508,29 @@
         out_ref[0] = total[...]
 
 
-def out_sums(number, own, near, far, hiddens):
-    hidden, cot = own
-    count, width = cot.shape
+def out_sums(own, near, far, hiddens):
+    part, width = own.shape
+    count = hiddens[0].shape[0]
     sources, _, slots, _ = near.shape
-    groups = number.shape[0]
-    part = hidden.shape[1] // groups
-    near_hidden = pl.BlockSpec((count, part // 2), lambda j, w: (0, 0))
-    far_hidden = pl.BlockSpec((1, count, part // 2), lambda j, w: (j, 0, 0))
+    steps = hiddens[1].shape[0]
+    near_hidden = pl.BlockSpec((count, part // 2), lambda j: (0, 0))
+    far_hidden = pl.BlockSpec((1, count, part // 2), lambda j: (j, 0, 0))
     return pl.pallas_call(
         out_kernel,
-        grid_spec=pltpu.PrefetchScalarGridSpec(
-            num_scalar_prefetch=1,
-            grid=(groups - 2,),
-            in_specs=[
-                pl.BlockSpec((count, part), lambda j, w: (0, w[0])),
-                pl.BlockSpec((count, width), lambda j, w: (0, 0)),
-                pl.BlockSpec((sources, 1, slots, width), lambda j, w: (0, 0, 0, 0)),
-                pl.BlockSpec((sources, 1, slots, width), lambda j, w: (0, 1 + j, 0, 0)),
-            ]
-            + [near_hidden, far_hidden] * 2,
-            out_specs=pl.BlockSpec((1, part, width), lambda j, w: (0, 0, 0)),
-            scratch_shapes=[pltpu.VMEM((part, width), f32)],
-        ),
+        grid=(steps,),
+        in_specs=[
+            pl.BlockSpec((part, width), lambda j: (0, 0)),
+            pl.BlockSpec((sources, 1, slots, width), lambda j: (0, 0, 0, 0)),
+            pl.BlockSpec((sources, 1, slots, width), lambda j: (0, 1 + j, 0, 0)),
+        ]
+        + [near_hidden, far_hidden] * 2,
+        out_specs=pl.BlockSpec((1, part, width), lambda j: (0, 0, 0)),
         out_shape=jax.ShapeDtypeStruct((1, part, width), f32),
-        compiler_params=params("arbitrary"),
-        cost_estimate=cost(2 * count * width * part * groups, 16e6),
+        scratch_shapes=[pltpu.VMEM((part, width), f32)],
+        compiler_params=params("arbitrary"),
+        cost_estimate=cost(2 * count * width * part * (steps + 1), 16e6),
         name="out_sums",
-    )(number, hidden, cot, near, far, *hiddens)
+    )(own, near, far, *hiddens)
 
 
 def lay_kernel(*refs):
@@ -1080,7 +1123,11 @@
         groups,
         experts,
     )
-    weights, prompt_sent, near_back, far_got = tied((weights, prompt_sent, near_back, far_got))
+    place, _ = tied((group[None], weights))
+    own_part = own_out(place, groups, hidden, cot[0])
+    weights, prompt_sent, near_back, far_got, own_part = tied(
+        (weights, prompt_sent, near_back, far_got, own_part)
+    )
     marks = []
     weight_sums = weight_chain(*weights, marks)
     weight_sent = next(weight_sums)
@@ -1089,23 +1136,23 @@
     result = rounded(residual + matmul_tn(spread, result_got))
     weight_sent, prompt_sent, result = tied((weight_sent, prompt_sent, result))
     weight_sent, _ = moved_on(weight_sums, weight_sent)
-    prompt_sent, prompt_back = moved_on(prompt_sums, prompt_sent)
     number, _ = tied((numbers(range(groups)), marks[-1]))
     operands = (expert_in, expert_out, (rows, grad_pre), all_rows, cot[1], far_got)
     in_first, *hidden_first = in_sums(number, 0, *operands)
     over_group = lambda values: lax.all_to_all(
         values, "group", split_axis=0, concat_axis=0, tiled=True
     )
-    weight_sent, in_first = tied((weight_sent, in_first))
     got_first = over_group(in_first)
+    weight_sent, prompt_sent, _ = tied((weight_sent, prompt_sent, in_first))
     weight_sent, _ = moved_on(weight_sums, weight_sent)
+    prompt_sent, prompt_back = moved_on(prompt_sums, prompt_sent)
     number, _ = tied((number, marks[-1]))
     in_second, *hidden_second = in_sums(number, 1, *operands)
     got_first, in_second, prompt_sent, weight_sent = tied(
         (got_first, in_second, prompt_sent, weight_sent)
     )
     got_second = over_group(in_second)
-    prompt_sent, weight_sent, number, _ = tied((prompt_sent, weight_sent, number, in_second))
+    prompt_sent, weight_sent, _ = tied((prompt_sent, weight_sent, in_second))
     while prompt_sent is not None:
         prompt_sent, prompt_back = moved_on(prompt_sums, prompt_sent)
     grad_tokens, sums1 = input_back(
@@ -1120,11 +1167,9 @@
         norm1_gain,
         grad_resid,
     )
-    weight_sent, number, sums1 = tied((weight_sent, number, sums1))
+    weight_sent, own_part, sums1 = tied((weight_sent, own_part, sums1))
     weight_sent, weight_grads = moved_on(weight_sums, weight_sent)
-    grad_expert_out = out_sums(
-        number, (hidden, cot[0]), cot[1], far_got, hidden_first + hidden_second
-    )
+    grad_expert_out = out_sums(own_part, cot[1], far_got, hidden_first + hidden_second)
     vectors = jnp.concatenate([sums1, sums2])
     vectors, got_second, grad_expert_out, weight_sent = tied(
         (vectors, got_second, grad_expert_out, weight_sent)

time: 402 us -> 399 us (level)
  waiting for transfers between devices: 37 us -> 31.3 us
    all_to_all x5, waiting for transfers between devices: 18.1 us -> 13.2 us  [all_exchanged(): lax.all_to_all(values, 'expert', split_axis=0, concat_axis=0, tiled=True)]
    pallas_call x3 -> x4, Pallas kernels: 56.1 us -> 57.4 us  [the longest x2 37.5 us: in_sums(): pl.pallas_call(functools.partial(in_kernel, half), grid_spec=pltpu.Prefet...]
    unnamed x44 -> x42, local copies, waits for them, and re-layouts: 8.2 us -> 7.46 us
  transfers between devices with their start and end apart: 31 -> 31, of which waited for: 13 -> 13; matrix products, arithmetic and copies ran while one was open for 7% -> 8% of each run, Pallas kernels for 62% -> 63%
where the time goes in v2:
time: 399 us; the launch traced here: 395 us
  Pallas kernels  249 us (62%)
  starting transfers between devices  58.7 us (15%)
  waiting for transfers between devices  31.3 us (8%)
  other arithmetic  17.4 us (4%)
  between operations  14.7 us (4%)
  local copies, waits for them, and re-layouts  12.3 us (3%)
  matrix products  11.2 us (3%)
    pallas_call x2, Pallas kernels, in_sums(): pl.pallas_call(functools.partial(in_kernel, half), grid_spec=pltpu.Prefet...  37.5 us
    pallas_call x1, Pallas kernels, attend_back(): pl.pallas_call(functools.partial(attend_back_kernel, prompt_len), grid=(p...  34.1 us
    pallas_call x1, Pallas kernels, expert_front(): pl.pallas_call(functools.partial(front_kernel, 4), grid=(ff // block,), i...  25.4 us
    pallas_call x1, Pallas kernels, attend(): pl.pallas_call(functools.partial(attend_kernel, prompt_len), grid=(pairs,...  23.2 us
    all_to_all x5, starting transfers between devices, all_exchanged(): lax.all_to_all(values, 'expert', split_axis=0, concat_axis=0, tiled=True)  21.5 us
    ppermute x19, starting transfers between devices, swapped(): lax.ppermute(block, axis, [(i, i ^ mask) for i in range(lax.axis_size(axi...  20.1 us
    pallas_call x1, Pallas kernels, weight_parts(): pl.pallas_call(weights_kernel, grid=(groups,), in_specs=[pl.BlockSpec(mem...  18.6 us
    pallas_call x1, Pallas kernels, project(): pl.pallas_call(functools.partial(project_kernel, len(pieces)), grid=(widt...  16.9 us
  transfers between devices with their start and end apart: 31, of which 13 were waited for; matrix products, arithmetic and copies ran while one was open for 8% of the time, Pallas kernels for 63%

profile of v2, /device:TPU:0, one launch (start us, length us, event | category | flops | bytes accessed | tf_op | source)
XLA Modules:
  0.0 394.9 jit_solution(16166055293291644585)
XLA Ops:
  8.2 2.4 pad_maximum_fusion
  10.6 2.5 collective-permute-start.2
  13.2 2.4 collective-permute-start
  17.4 4.1 %collective-permute-done.refs_1_ = bf16[128,1024]{1,0:T(8,128)(2,1)} collective-permute-done((bf16[128,1024]{1,0:T(8,128)(2,1)S(1)}, bf16[128,1024]{1,0:T(8,128)(2,1)}, u32[]{:S(2)}, u32[]{:S(2)}) %collective-permute-start) | collective-permute-done | bytes 262176 | tf_op jit(solution)/shard_map/ppermute | solution.py:25
  25.4 2.6 fusion.5
  28.6 1.9 collective-permute-done.3.refs_3_
  30.6 3.9 all-to-all-start.1
  35.5 16.9 %project.1 = (bf16[1792,1024]{1,0:T(8,128)(2,1)}, bf16[512,1024]{1,0:T(8,128)(2,1)}, bf16[1792,1024]{1,0:T(8,128)(2,1)}, bf16[1792,1024]{1,0:T(8,128)(2,1)}) custom-call(f32[1,1024]{1,0:T(1,128)} %bitcast.75, f32[1,1024]{1,0:T(1,128)} %bitcast.79, bf16[1024,1024]{1,0:T(8,128)(2,1)} %wq_ref.3, bf16[1024,1024]{1,0:T(8,128)(2,1)} %wk_ref.3, ...), custom_call_target="tpu_custom_call" | custom-call | flops 375809632 | bytes 943718 | tf_op jit(solution)/shard_map/project/pallas_call | solution.py:653
  52.4 23.2 %attend.1 = (bf16[512,1024]{1,0:T(8,128)(2,1)}, f32[8,4,256]{2,1,0:T(4,128)}) custom-call(f32[1]{0:T(128)} %bitcast.1.near_ref, bf16[512,1024]{1,0:T(8,128)(2,1)} %get-tuple-element.104.q_ref, bf16[1792,1024]{1,0:T(8,128)(2,1)} %get-tuple-element.105.k_ref, bf16[1792,1024]{1,0:T(8,128)(2,1)} %get-tuple-element.106.v_ref, f32[1024,128]{1,0:T(8,128)} %compare_select_fusion.bias_ref), custom_call_target="tpu_custom_call" | custom-call | flops 751619264 | bytes 471859 | tf_op jit(solution)/shard_map/attend/pallas_call | solution.py:962
  75.6 3.3 fusion.17
  80.2 2.9 fusion.4
  84.4 4.8 %all-to-all-start = ((bf16[8,128,1024]{2,1,0:T(8,128)(2,1)}), bf16[8,128,1024]{2,1,0:T(8,128)(2,1)S(1)}, u32[]{:S(2)}, u32[]{:S(2)}) async-start(bf16[8,128,1024]{2,1,0:T(8,128)(2,1)} %bitcast.71), calls=%async_computation | async-start | bytes 4194304 | tf_op jit(solution)/shard_map/all_to_all | solution.py:1044
  89.2 13.2 %expert_back.1.gh_ref = bf16[1024,4096]{1,0:T(8,128)(2,1)} custom-call(bf16[1024,1024]{1,0:T(8,128)(2,1)} %bitcast.67, bf16[1,4096,1024]{2,1,0:T(8,128)(2,1)} %wout_hbm.3), custom_call_target="tpu_custom_call" | custom-call | flops 429496736 | bytes 838860 | tf_op jit(solution)/shard_map/expert_back/pallas_call | solution.py:269
  104.8 4.0 %spread_rows.2 = bf16[8,1,128,1024]{3,2,1,0:T(8,128)(2,1)} custom-call(s32[1]{0:T(128)} %bitcast.21._, s32[4,1,512]{2,1,0:T(1,128)} %reshape.110.ids_ref, bf16[4,512,1152]{2,1,0:T(8,128)(2,1)} %bitcast.65), custom_call_target="tpu_custom_call" | custom-call | flops 53687092 | bytes 400000 | tf_op jit(solution)/shard_map/spread_rows/pallas_call | solution.py:609
  108.9 7.0 %all-to-all-done = bf16[8,128,1024]{2,1,0:T(8,128)(2,1)S(1)} async-done(((bf16[8,128,1024]{2,1,0:T(8,128)(2,1)}), bf16[8,128,1024]{2,1,0:T(8,128)(2,1)S(1)}, u32[]{:S(2)}, u32[]{:S(2)}) %all-to-all-start) | async-done | bytes 2097184 | tf_op jit(solution)/shard_map/all_to_all | solution.py:1044
  117.1 4.3 %all-to-all-start.2 = ((bf16[8,1,128,1024]{3,2,1,0:T(8,128)(2,1)}), bf16[8,1,128,1024]{3,2,1,0:T(8,128)(2,1)}, u32[]{:S(2)}, u32[]{:S(2)}) async-start(bf16[8,1,128,1024]{3,2,1,0:T(8,128)(2,1)} %spread_rows.2), calls=%async_computation.2 | async-start | bytes 4194304 | tf_op jit(solution)/shard_map/all_to_all | solution.py:1044
  122.2 25.4 %expert_front.1 = (bf16[1024,4096]{1,0:T(8,128)(2,1)}, bf16[1024,4096]{1,0:T(8,128)(2,1)}, bf16[1024,1024]{1,0:T(8,128)(2,1)}) custom-call(bf16[1024,1024]{1,0:T(8,128)(2,1)} %bitcast.59, bf16[1024,4096]{1,0:T(8,128)(2,1)} %expert_back.1.gh_ref, bf16[1,1024,4096]{2,1,0:T(8,128)(2,1)} %win_hbm.3), custom_call_target="tpu_custom_call" | custom-call | flops 858993472 | bytes 1677721 | tf_op jit(solution)/shard_map/expert_front/pallas_call | solution.py:316
  148.1 3.6 all-to-all-start.3
  152.3 14.6 %expert_produce.1.refs_0_ = bf16[1024,1024]{1,0:T(8,128)(2,1)} custom-call(bf16[1024,4096]{1,0:T(8,128)(2,1)} %get-tuple-element.115.hidden_ref, bf16[1,4096,1024]{2,1,0:T(8,128)(2,1)} %wout_hbm.3), custom_call_target="tpu_custom_call" | custom-call | flops 429496736 | bytes 838860 | tf_op jit(solution)/shard_map/expert_produce/pallas_call | solution.py:354
  167.0 7.6 %spread_rows.3 = bf16[8,3,128,1024]{3,2,1,0:T(8,128)(2,1)} custom-call(s32[2]{0:T(128)} %pad_add_fusion._, s32[4,1,512]{2,1,0:T(1,128)} %reshape.110.ids_ref, bf16[4,512,1152]{2,1,0:T(8,128)(2,1)} %bitcast.66, bf16[1024,1024]{1,0:T(8,128)(2,1)} %expert_produce.1.refs_0_), custom_call_target="tpu_custom_call" | custom-call | flops 161061280 | bytes 400000 | tf_op jit(solution)/shard_map/spread_rows/pallas_call | solution.py:609
  174.6 3.8 all-to-all-done.3
  179.7 4.9 %all-to-all-start.4 = ((bf16[8,3,128,1024]{3,2,1,0:T(8,128)(2,1)}), bf16[8,3,128,1024]{3,2,1,0:T(8,128)(2,1)}, u32[]{:S(2)}, u32[]{:S(2)}) async-start(bf16[8,3,128,1024]{3,2,1,0:T(8,128)(2,1)} %spread_rows.3), calls=%async_computation.4 | async-start | bytes 12582912 | tf_op jit(solution)/shard_map/all_to_all | solution.py:1044
  186.0 8.0 %resid_back.1 = (f32[512,1024]{1,0:T(8,128)}, bf16[512,1024]{1,0:T(8,128)(2,1)}, bf16[512,1024]{1,0:T(8,128)(2,1)}, f32[2,1024]{1,0:T(2,128)}) custom-call(bf16[1024,1024]{1,0:T(8,128)(2,1)} %bitcast.69, bf16[1024,512]{1,0:T(8,128)(2,1)} %fusion.1.spread_ref, f32[512,1024]{1,0:T(8,128)} %copy-done.2, f32[1,1024]{1,0:T(1,128)} %bitcast.80, ...), custom_call_target="tpu_custom_call" | custom-call | flops 107374184 | bytes 419430 | tf_op jit(solution)/shard_map/resid_back/pallas_call | solution.py:753
  194.0 34.1 %attend_back.1 = (bf16[512,1024]{1,0:T(8,128)(2,1)}, bf16[2,512,1024]{2,1,0:T(8,128)(2,1)}, bf16[2,512,1024]{2,1,0:T(8,128)(2,1)}, bf16[2,384,1024]{2,1,0:T(8,128)(2,1)}, bf16[2,384,1024]{2,1,0:T(8,128)(2,1)}) custom-call(f32[1]{0:T(128)} %bitcast.1.near_ref, bf16[512,1024]{1,0:T(8,128)(2,1)} %get-tuple-element.104.q_ref, ...), custom_call_target="tpu_custom_call" | custom-call | flops 1879048192 | bytes 943718 | tf_op jit(solution)/shard_map/attend_back/pallas_call | solution.py:995
  229.8 18.6 %weight_parts.1 = (bf16[4,4,4,32,1024]{4,3,2,1,0:T(8,128)(2,1)}, bf16[4,4,4,32,1024]{4,3,2,1,0:T(8,128)(2,1)}) custom-call(s32[1]{0:T(128)} %bitcast.odd_ref, bf16[512,1024]{1,0:T(8,128)(2,1)} %get-tuple-element.107.out_ref.refs_0_, bf16[1792,1024]{1,0:T(8,128)(2,1)} %get-tuple-element.108.refs_1_, bf16[512,1024]{1,0:T(8,128)(2,1)} %get-tuple-element.118.refs_2_, ...), custom_call_target="tpu_custom_call" | custom-call | flops 500000000 | bytes 1500000 | tf_op jit(solution)/shard_map/weight_parts/pallas_call | solution.py:710
  248.4 5.8 %own_out.1.own_ref = f32[1024,1024]{1,0:T(8,128)} custom-call(s32[1]{0:T(128)} %bitcast.25._.own_ref, bf16[1024,4096]{1,0:T(8,128)(2,1)} %get-tuple-element.115.hidden_ref, bf16[1024,1024]{1,0:T(8,128)(2,1)} %bitcast.68), custom_call_target="tpu_custom_call" | custom-call | flops 107374184 | bytes 400000 | tf_op jit(solution)/shard_map/own_out/pallas_call | solution.py:469
  254.2 2.0 all-to-all-done.4.far_hbm.far_ref
  256.5 1.9 slice.68
  258.4 3.3 add_convert_fusion
  265.0 2.3 add_convert_fusion.1
  267.3 3.5 collective-permute-done.11
  270.8 1.9 collective-permute-done.12
  272.7 5.4 %halve.2 = (bf16[2,4,2,32,1024]{4,3,2,1,0:T(8,128)(2,1)}, bf16[2,4,2,32,1024]{4,3,2,1,0:T(8,128)(2,1)}, bf16[2,4,2,32,1024]{4,3,2,1,0:T(8,128)(2,1)}, bf16[2,4,2,32,1024]{4,3,2,1,0:T(8,128)(2,1)}) custom-call(s32[1]{0:T(128)} %bitcast.27.own_ref, bf16[4,4,4,32,1024]{4,3,2,1,0:T(8,128)(2,1)} %get-tuple-element.134.refs_0_.refs_2_, ...), custom_call_target="tpu_custom_call" | custom-call | flops 104857 | bytes 629145 | tf_op jit(solution)/shard_map/halve/pallas_call | solution.py:159
  280.8 18.7 %in_sums.2 = (bf16[4,256,512]{2,1,0:T(8,128)(2,1)}, bf16[1024,512]{1,0:T(8,128)(2,1)}, bf16[2,1024,512]{2,1,0:T(8,128)(2,1)}) custom-call(s32[4]{0:T(128)} %pad_add_fusion.1.number_ref, bf16[1024,1024]{1,0:T(8,128)(2,1)} %bitcast.60, bf16[1024,4096]{1,0:T(8,128)(2,1)} %get-tuple-element.138.own_pre_ref, bf16[1,1024,4096]{2,1,0:T(8,128)(2,1)} %win_hbm.3, ...), custom_call_target="tpu_custom_call" | custom-call | flops 644245120 | bytes 800000 | tf_op jit(solution)/shard_map/in_sums/pallas_call | solution.py:423
  299.5 5.3 %all-to-all-start.5 = ((bf16[4,256,512]{2,1,0:T(8,128)(2,1)}), bf16[4,256,512]{2,1,0:T(8,128)(2,1)S(1)}, u32[]{:S(2)}, u32[]{:S(2)}) async-start(bf16[4,256,512]{2,1,0:T(8,128)(2,1)} %get-tuple-element.140), calls=%async_computation.5 | async-start | bytes 2097152 | tf_op jit(solution)/shard_map/all_to_all | solution.py:1142
  305.0 2.2 add_convert_fusion.6
  309.1 3.3 halve.3
  314.6 18.8 %in_sums.3 = (bf16[4,256,512]{2,1,0:T(8,128)(2,1)}, bf16[1024,512]{1,0:T(8,128)(2,1)}, bf16[2,1024,512]{2,1,0:T(8,128)(2,1)}) custom-call(s32[4]{0:T(128)} %pad_add_fusion.1.number_ref, bf16[1024,1024]{1,0:T(8,128)(2,1)} %bitcast.61, bf16[1024,4096]{1,0:T(8,128)(2,1)} %get-tuple-element.138.own_pre_ref, bf16[1,1024,4096]{2,1,0:T(8,128)(2,1)} %win_hbm.3, ...), custom_call_target="tpu_custom_call" | custom-call | flops 644245120 | bytes 800000 | tf_op jit(solution)/shard_map/in_sums/pallas_call | solution.py:423
  334.2 5.1 %all-to-all-start.6 = ((bf16[4,256,512]{2,1,0:T(8,128)(2,1)}), bf16[4,256,512]{2,1,0:T(8,128)(2,1)}, u32[]{:S(2)}, u32[]{:S(2)}) async-start(bf16[4,256,512]{2,1,0:T(8,128)(2,1)} %get-tuple-element.159), calls=%async_computation.6 | async-start | bytes 2097152 | tf_op jit(solution)/shard_map/all_to_all | solution.py:1142
  339.4 2.3 add_convert_fusion.5.prompt_ref
  341.6 10.6 %input_back.1 = (bf16[512,1024]{1,0:T(8,128)(2,1)}, f32[2,1024]{1,0:T(2,128)}) custom-call(bf16[2,128,1024]{2,1,0:T(8,128)(2,1)} %add_convert_fusion.5.prompt_ref, bf16[2,384,1024]{2,1,0:T(8,128)(2,1)} %get-tuple-element.125.refs_7_.own_ref, bf16[2,384,1024]{2,1,0:T(8,128)(2,1)} %collective-permute-done.9.near_ref, ...), custom_call_target="tpu_custom_call" | custom-call | flops 161061280 | bytes 524288 | tf_op jit(solution)/shard_map/input_back/pallas_call | solution.py:820
  352.3 2.7 turn.1
  355.0 2.0 collective-permute-start.19
  357.0 14.1 %out_sums.1 = f32[1,1024,1024]{2,1,0:T(8,128)} custom-call(f32[1024,1024]{1,0:T(8,128)} %own_out.1.own_ref, bf16[8,1,128,1024]{3,2,1,0:T(8,128)(2,1)} %all-to-all-done.2.near_hbm.near_ref, bf16[8,3,128,1024]{3,2,1,0:T(8,128)(2,1)} %all-to-all-done.4.far_hbm.far_ref, bf16[1024,512]{1,0:T(8,128)(2,1)} %get-tuple-element.172.refs_0_, ...), custom_call_target="tpu_custom_call" | custom-call | flops 322122560 | bytes 800000 | tf_op jit(solution)/shard_map/out_sums/pallas_call | solution.py:518
  371.7 2.1 collective-permute-start.20
  374.7 2.7 all-to-all-start.7
  377.4 4.2 %lay_out.1 = f32[1,256,4096]{2,1,0:T(8,128)} custom-call(bf16[4,256,512]{2,1,0:T(8,128)(2,1)} %copy-done.5, bf16[4,256,512]{2,1,0:T(8,128)(2,1)} %all-to-all-done.6.refs_1_), custom_call_target="tpu_custom_call" | custom-call | flops 52428 | bytes 314572 | tf_op jit(solution)/shard_map/lay_out/pallas_call | solution.py:549
  381.6 3.5 all-to-all-done.7
  (117 shorter events, 36.4 us)
Async XLA Ops:
  7.2 3.4 copy-start.6
  7.2 95.6 %all-gather.5.cloned.1.call-start = ((), (), s32[]{:S(2)}) async-start(), calls=%async_computation.8 | async-start | bytes 5898240 | tf_op jit(solution)/shard_map/all_gather | solution.py:1057
  10.5 6.6 %copy-start.15 = (s32[512,1]{0,1:T(1,128)S(1)}, s32[512,1]{0,1:T(1,128)}, u32[]{:S(2)}) copy-start(s32[512,1]{0,1:T(1,128)} %param.15) | copy-start | bytes 6148
  10.5 14.9 %copy-start.7 = (bf16[512,1024]{1,0:T(8,128)(2,1)S(1)}, bf16[512,1024]{1,0:T(8,128)(2,1)}, u32[]{:S(2)}) copy-start(bf16[512,1024]{1,0:T(8,128)(2,1)} %cot_ref.1) | copy-start | bytes 3145732
  10.6 17.3 %copy-start.8 = (bf16[384,1024]{1,0:T(8,128)(2,1)}, bf16[384,1024]{1,0:T(8,128)(2,1)S(1)}, u32[]{:S(2)}) copy-start(bf16[384,1024]{1,0:T(8,128)(2,1)S(1)} %slice.63.refs_9_) | copy-start | bytes 2359300
  10.6 12.3 %collective-permute-start.2 = (bf16[384,1024]{1,0:T(8,128)(2,1)S(1)}, bf16[384,1024]{1,0:T(8,128)(2,1)S(1)}, u32[]{:S(2)}, u32[]{:S(2)}) collective-permute-start(bf16[384,1024]{1,0:T(8,128)(2,1)S(1)} %slice.63.refs_9_), channel_id=1, source_target_pairs={{0,1},{2,3},{4,5},{6,7},{8,9},{10,11},{12,13},{14,15},{16,17},{18,... | collective-permute-start | bytes 2359304 | tf_op jit(solution)/shard_map/ppermute | solution.py:1050
  13.2 14.8 %copy-start.10 = (bf16[128,1024]{1,0:T(8,128)(2,1)}, bf16[128,1024]{1,0:T(8,128)(2,1)S(1)}, u32[]{:S(2)}) copy-start(bf16[128,1024]{1,0:T(8,128)(2,1)S(1)} %slice.62.refs_0_) | copy-start | bytes 786436
  13.2 8.3 %collective-permute-start = (bf16[128,1024]{1,0:T(8,128)(2,1)S(1)}, bf16[128,1024]{1,0:T(8,128)(2,1)}, u32[]{:S(2)}, u32[]{:S(2)}) collective-permute-start(bf16[128,1024]{1,0:T(8,128)(2,1)S(1)} %slice.62.refs_0_), channel_id=1, source_target_pairs={{0,2},{1,3},{2,0},{3,1},{4,6},{5,7},{6,4},{7,5},{8,10},{9,11},{10,... | collective-permute-start | bytes 786440 | tf_op jit(solution)/shard_map/ppermute | solution.py:25
  15.6 7.4 %collective-permute-start.1 = (bf16[128,1024]{1,0:T(8,128)(2,1)S(1)}, bf16[128,1024]{1,0:T(8,128)(2,1)}, u32[]{:S(2)}, u32[]{:S(2)}) collective-permute-start(bf16[128,1024]{1,0:T(8,128)(2,1)S(1)} %slice.62.refs_0_), channel_id=1, source_target_pairs={{0,4},{1,5},{2,6},{3,7},{4,0},{5,1},{6,2},{7,3},{8,12},{9,13},{10,... | collective-permute-start | bytes 786440 | tf_op jit(solution)/shard_map/ppermute | solution.py:25
  17.1 18.4 %collective-permute-start.4 = (bf16[128,1024]{1,0:T(8,128)(2,1)S(1)}, bf16[128,1024]{1,0:T(8,128)(2,1)}, u32[]{:S(2)}, u32[]{:S(2)}) collective-permute-start(bf16[128,1024]{1,0:T(8,128)(2,1)S(1)} %slice.62.refs_0_), channel_id=1, source_target_pairs={{0,1},{1,0},{2,3},{3,2},{4,5},{5,4},{6,7},{7,6},{8,9},{9,8},{10,11... | collective-permute-start | bytes 786440 | tf_op jit(solution)/shard_map/ppermute | solution.py:25
  23.9 6.7 %collective-permute-start.3 = (bf16[128,1024]{1,0:T(8,128)(2,1)}, bf16[128,1024]{1,0:T(8,128)(2,1)}, u32[]{:S(2)}, u32[]{:S(2)}) collective-permute-start(bf16[128,1024]{1,0:T(8,128)(2,1)} %collective-permute-done.refs_1_), channel_id=1, source_target_pairs={{0,4},{1,5},{2,6},{3,7},{4,0},{5,1},{6,2},{7,3},{8,12},{9,13},{10,... | collective-permute-start | bytes 786440 | tf_op jit(solution)/shard_map/ppermute | solution.py:25
  28.1 7.4 %collective-permute-start.5 = (bf16[128,1024]{1,0:T(8,128)(2,1)}, bf16[128,1024]{1,0:T(8,128)(2,1)}, u32[]{:S(2)}, u32[]{:S(2)}) collective-permute-start(bf16[128,1024]{1,0:T(8,128)(2,1)} %collective-permute-done.refs_1_), channel_id=1, source_target_pairs={{0,1},{1,0},{2,3},{3,2},{4,5},{5,4},{6,7},{7,6},{8,9},{9,8},{10,11... | collective-permute-start | bytes 786440 | tf_op jit(solution)/shard_map/ppermute | solution.py:25
  28.1 7.4 %collective-permute-start.6 = (bf16[128,1024]{1,0:T(8,128)(2,1)}, bf16[128,1024]{1,0:T(8,128)(2,1)}, u32[]{:S(2)}, u32[]{:S(2)}) collective-permute-start(bf16[128,1024]{1,0:T(8,128)(2,1)} %collective-permute-done.1.refs_2_), channel_id=1, source_target_pairs={{0,1},{1,0},{2,3},{3,2},{4,5},{5,4},{6,7},{7,6},{8,9},{9,8},{10,11... | collective-permute-start | bytes 786440 | tf_op jit(solution)/shard_map/ppermute | solution.py:25
  30.6 5.0 %collective-permute-start.7 = (bf16[128,1024]{1,0:T(8,128)(2,1)}, bf16[128,1024]{1,0:T(8,128)(2,1)}, u32[]{:S(2)}, u32[]{:S(2)}) collective-permute-start(bf16[128,1024]{1,0:T(8,128)(2,1)} %collective-permute-done.3.refs_3_), channel_id=1, source_target_pairs={{0,1},{1,0},{2,3},{3,2},{4,5},{5,4},{6,7},{7,6},{8,9},{9,8},{10,11... | collective-permute-start | bytes 786440 | tf_op jit(solution)/shard_map/ppermute | solution.py:25
  30.6 52.5 %all-to-all-start.1 = ((bf16[8,128,1024]{2,1,0:T(8,128)(2,1)}), bf16[8,128,1024]{2,1,0:T(8,128)(2,1)S(1)}, u32[]{:S(2)}, u32[]{:S(2)}) async-start(bf16[8,128,1024]{2,1,0:T(8,128)(2,1)} %bitcast.70), calls=%async_computation.1 | async-start | bytes 4194304 | tf_op jit(solution)/shard_map/all_to_all | solution.py:1044
  78.9 1.3 copy-start.2
  78.9 1.3 copy-start.18
  78.9 1.3 copy-start.19
  83.1 1.4 copy-start.1
  84.4 31.4 %all-to-all-start = ((bf16[8,128,1024]{2,1,0:T(8,128)(2,1)}), bf16[8,128,1024]{2,1,0:T(8,128)(2,1)S(1)}, u32[]{:S(2)}, u32[]{:S(2)}) async-start(bf16[8,128,1024]{2,1,0:T(8,128)(2,1)} %bitcast.71), calls=%async_computation | async-start | bytes 4194304 | tf_op jit(solution)/shard_map/all_to_all | solution.py:1044
  115.8 1.3 copy-start
  117.1 31.0 %all-to-all-start.2 = ((bf16[8,1,128,1024]{3,2,1,0:T(8,128)(2,1)}), bf16[8,1,128,1024]{3,2,1,0:T(8,128)(2,1)}, u32[]{:S(2)}, u32[]{:S(2)}) async-start(bf16[8,1,128,1024]{3,2,1,0:T(8,128)(2,1)} %spread_rows.2), calls=%async_computation.2 | async-start | bytes 4194304 | tf_op jit(solution)/shard_map/all_to_all | solution.py:1044
  121.5 159.3 %all-gather.7.cloned.1.call-start = ((), (), s32[]{:S(2)}) async-start(), calls=%async_computation.9 | async-start | bytes 10485760 | tf_op jit(solution)/shard_map/all_gather | solution.py:1094
  148.1 30.2 %all-to-all-start.3 = ((bf16[8,128,1024]{2,1,0:T(8,128)(2,1)}), bf16[8,128,1024]{2,1,0:T(8,128)(2,1)S(1)}, u32[]{:S(2)}, u32[]{:S(2)}) async-start(bf16[8,128,1024]{2,1,0:T(8,128)(2,1)} %bitcast.72), calls=%async_computation.3 | async-start | bytes 4194304 | tf_op jit(solution)/shard_map/all_to_all | solution.py:1044
  179.7 76.5 %all-to-all-start.4 = ((bf16[8,3,128,1024]{3,2,1,0:T(8,128)(2,1)}), bf16[8,3,128,1024]{3,2,1,0:T(8,128)(2,1)}, u32[]{:S(2)}, u32[]{:S(2)}) async-start(bf16[8,3,128,1024]{3,2,1,0:T(8,128)(2,1)} %spread_rows.3), calls=%async_computation.4 | async-start | bytes 12582912 | tf_op jit(solution)/shard_map/all_to_all | solution.py:1044
  228.1 26.1 %collective-permute-start.8 = (bf16[2,512,1024]{2,1,0:T(8,128)(2,1)}, bf16[2,512,1024]{2,1,0:T(8,128)(2,1)S(1)}, u32[]{:S(2)}, u32[]{:S(2)}) collective-permute-start(bf16[2,512,1024]{2,1,0:T(8,128)(2,1)} %get-tuple-element.123.refs_5_), channel_id=1, source_target_pairs={{0,1},{1,0},{2,3},{3,2},{4,5},{5,4},{6,7},{7,6},{8,9},{9,8},{10,11... | collective-permute-start | bytes 6291464 | tf_op jit(solution)/shard_map/ppermute | solution.py:25
  228.5 25.7 %collective-permute-start.9 = (bf16[2,384,1024]{2,1,0:T(8,128)(2,1)}, bf16[2,384,1024]{2,1,0:T(8,128)(2,1)}, u32[]{:S(2)}, u32[]{:S(2)}) collective-permute-start(bf16[2,384,1024]{2,1,0:T(8,128)(2,1)} %get-tuple-element.124.refs_6_), channel_id=1, source_target_pairs={{1,0},{3,2},{5,4},{7,6},{9,8},{11,10},{13,12},{15,14},{17,16},{19,... | collective-permute-start | bytes 4718600 | tf_op jit(solution)/shard_map/ppermute | solution.py:1113
  254.2 2.3 copy-start.9
  256.2 16.5 %collective-permute-start.10 = (bf16[4,4,4,32,1024]{4,3,2,1,0:T(8,128)(2,1)}, bf16[4,4,4,32,1024]{4,3,2,1,0:T(8,128)(2,1)}, u32[]{:S(2)}, u32[]{:S(2)}) collective-permute-start(bf16[4,4,4,32,1024]{4,3,2,1,0:T(8,128)(2,1)} %get-tuple-element.130), channel_id=1, source_target_pairs={{0,1},{1,0},{2,3},{3,2},{4,5},{5,4},{6,7},{7,6},{8,9},{9,8},{10,11... | collective-permute-start | bytes 12582920 | tf_op jit(solution)/shard_map/ppermute | solution.py:25
  258.4 6.6 %copy-start.3 = (f32[512,1024]{1,0:T(8,128)S(1)}, f32[512,1024]{1,0:T(8,128)}, u32[]{:S(2)}) copy-start(f32[512,1024]{1,0:T(8,128)} %copy-done.2) | copy-start | bytes 6291460
  261.8 8.9 %collective-permute-start.11 = (bf16[2,64,1024]{2,1,0:T(8,128)(2,1)S(1)}, bf16[2,64,1024]{2,1,0:T(8,128)(2,1)S(1)}, u32[]{:S(2)}, u32[]{:S(2)}) collective-permute-start(bf16[2,64,1024]{2,1,0:T(8,128)(2,1)S(1)} %get-tuple-element.189), channel_id=1, source_target_pairs={{0,4},{1,5},{2,6},{3,7},{4,0},{5,1},{6,2},{7,3},{8,12},{9,13},{10,... | collective-permute-start | bytes 786440 | tf_op jit(solution)/shard_map/ppermute | solution.py:25
  263.5 9.2 %collective-permute-start.12 = (bf16[2,64,1024]{2,1,0:T(8,128)(2,1)S(1)}, bf16[2,64,1024]{2,1,0:T(8,128)(2,1)S(1)}, u32[]{:S(2)}, u32[]{:S(2)}) collective-permute-start(bf16[2,64,1024]{2,1,0:T(8,128)(2,1)S(1)} %get-tuple-element.188), channel_id=1, source_target_pairs={{0,2},{1,3},{2,0},{3,1},{4,6},{5,7},{6,4},{7,5},{8,10},{9,11},{10,... | collective-permute-start | bytes 786440 | tf_op jit(solution)/shard_map/ppermute | solution.py:25
  272.7 5.4 %copy-start.14 = (bf16[2,64,1024]{2,1,0:T(8,128)(2,1)}, bf16[2,64,1024]{2,1,0:T(8,128)(2,1)S(1)}, u32[]{:S(2)}) copy-start(bf16[2,64,1024]{2,1,0:T(8,128)(2,1)S(1)} %collective-permute-done.12) | copy-start | bytes 786436
  278.1 26.7 %collective-permute-start.13 = (bf16[2,4,2,32,1024]{4,3,2,1,0:T(8,128)(2,1)}, bf16[2,4,2,32,1024]{4,3,2,1,0:T(8,128)(2,1)}, u32[]{:S(2)}, u32[]{:S(2)}) collective-permute-start(bf16[2,4,2,32,1024]{4,3,2,1,0:T(8,128)(2,1)} %get-tuple-element.141), channel_id=1, source_target_pairs={{0,2},{1,3},{2,0},{3,1},{4,6},{5,7},{6,4},{7,5},{8,10},{9,11},{10,... | collective-permute-start | bytes 3145736 | tf_op jit(solution)/shard_map/ppermute | solution.py:25
  279.7 25.3 %collective-permute-start.14 = (bf16[2,4,2,32,1024]{4,3,2,1,0:T(8,128)(2,1)}, bf16[2,4,2,32,1024]{4,3,2,1,0:T(8,128)(2,1)}, u32[]{:S(2)}, u32[]{:S(2)}) collective-permute-start(bf16[2,4,2,32,1024]{4,3,2,1,0:T(8,128)(2,1)} %get-tuple-element.142), channel_id=1, source_target_pairs={{0,4},{1,5},{2,6},{3,7},{4,0},{5,1},{6,2},{7,3},{8,12},{9,13},{10,... | collective-permute-start | bytes 3145736 | tf_op jit(solution)/shard_map/ppermute | solution.py:25
  299.5 34.7 %all-to-all-start.5 = ((bf16[4,256,512]{2,1,0:T(8,128)(2,1)}), bf16[4,256,512]{2,1,0:T(8,128)(2,1)S(1)}, u32[]{:S(2)}, u32[]{:S(2)}) async-start(bf16[4,256,512]{2,1,0:T(8,128)(2,1)} %get-tuple-element.140), calls=%async_computation.5 | async-start | bytes 2097152 | tf_op jit(solution)/shard_map/all_to_all | solution.py:1142
  307.2 26.2 %collective-permute-start.15 = (bf16[2,128,1024]{2,1,0:T(8,128)(2,1)}, bf16[2,128,1024]{2,1,0:T(8,128)(2,1)}, u32[]{:S(2)}, u32[]{:S(2)}) collective-permute-start(bf16[2,128,1024]{2,1,0:T(8,128)(2,1)} %get-tuple-element.187), channel_id=1, source_target_pairs={{0,2},{1,3},{2,0},{3,1},{4,6},{5,7},{6,4},{7,5},{8,10},{9,11},{10,... | collective-permute-start | bytes 1572872 | tf_op jit(solution)/shard_map/ppermute | solution.py:25
  307.8 25.6 %collective-permute-start.16 = (bf16[2,128,1024]{2,1,0:T(8,128)(2,1)}, bf16[2,128,1024]{2,1,0:T(8,128)(2,1)}, u32[]{:S(2)}, u32[]{:S(2)}) collective-permute-start(bf16[2,128,1024]{2,1,0:T(8,128)(2,1)} %get-tuple-element.186), channel_id=1, source_target_pairs={{0,4},{1,5},{2,6},{3,7},{4,0},{5,1},{6,2},{7,3},{8,12},{9,13},{10,... | collective-permute-start | bytes 1572872 | tf_op jit(solution)/shard_map/ppermute | solution.py:25
  312.5 21.0 %collective-permute-start.17 = (bf16[2,4,1,32,1024]{4,3,2,1,0:T(8,128)(2,1)}, bf16[2,4,1,32,1024]{4,3,2,1,0:T(8,128)(2,1)S(1)}, u32[]{:S(2)}, u32[]{:S(2)}) collective-permute-start(bf16[2,4,1,32,1024]{4,3,2,1,0:T(8,128)(2,1)} %get-tuple-element.153), channel_id=1, source_target_pairs={{0,4},{1,5},{2,6},{3,7},{4,0},{5,1},{6,2},{7,3},{8,12},{9,13},{10,... | collective-permute-start | bytes 1572872 | tf_op jit(solution)/shard_map/ppermute | solution.py:25
  313.1 21.1 %collective-permute-start.18 = (bf16[2,4,1,32,1024]{4,3,2,1,0:T(8,128)(2,1)}, bf16[2,4,1,32,1024]{4,3,2,1,0:T(8,128)(2,1)}, u32[]{:S(2)}, u32[]{:S(2)}) collective-permute-start(bf16[2,4,1,32,1024]{4,3,2,1,0:T(8,128)(2,1)} %get-tuple-element.154), channel_id=1, source_target_pairs={{0,2},{1,3},{2,0},{3,1},{4,6},{5,7},{6,4},{7,5},{8,10},{9,11},{10,... | collective-permute-start | bytes 1572872 | tf_op jit(solution)/shard_map/ppermute | solution.py:25
  334.2 7.4 %copy-start.5 = (bf16[4,256,512]{2,1,0:T(8,128)(2,1)}, bf16[4,256,512]{2,1,0:T(8,128)(2,1)S(1)}, u32[]{:S(2)}) copy-start(bf16[4,256,512]{2,1,0:T(8,128)(2,1)S(1)} %all-to-all-done.5.refs_0_) | copy-start | bytes 3145732
  334.2 37.3 %all-to-all-start.6 = ((bf16[4,256,512]{2,1,0:T(8,128)(2,1)}), bf16[4,256,512]{2,1,0:T(8,128)(2,1)}, u32[]{:S(2)}, u32[]{:S(2)}) async-start(bf16[4,256,512]{2,1,0:T(8,128)(2,1)} %get-tuple-element.159), calls=%async_computation.6 | async-start | bytes 2097152 | tf_op jit(solution)/shard_map/all_to_all | solution.py:1142
  355.0 16.5 %collective-permute-start.19 = (bf16[4,2,32,1024]{3,2,1,0:T(8,128)(2,1)}, bf16[4,2,32,1024]{3,2,1,0:T(8,128)(2,1)S(1)}, u32[]{:S(2)}, u32[]{:S(2)}) collective-permute-start(bf16[4,2,32,1024]{3,2,1,0:T(8,128)(2,1)} %get-tuple-element.179), channel_id=1, source_target_pairs={{0,8},{8,0},{16,24},{24,16},{1,9},{9,1},{17,25},{25,17},{2,10},{10... | collective-permute-start | bytes 1572872 | tf_op jit(solution)/shard_map/ppermute | solution.py:25
  357.0 14.1 %copy-start.16 = (f32[2,1024]{1,0:T(2,128)S(1)}, f32[2,1024]{1,0:T(2,128)}, u32[]{:S(2)}) copy-start(f32[2,1024]{1,0:T(2,128)} %get-tuple-element.170) | copy-start | bytes 24580
  357.0 14.1 %copy-start.17 = (f32[2,1024]{1,0:T(2,128)S(1)}, f32[2,1024]{1,0:T(2,128)}, u32[]{:S(2)}) copy-start(f32[2,1024]{1,0:T(2,128)} %get-tuple-element.169) | copy-start | bytes 24580
  357.0 14.5 %copy-start.13 = (bf16[4,2,32,1024]{3,2,1,0:T(8,128)(2,1)S(1)}, bf16[4,2,32,1024]{3,2,1,0:T(8,128)(2,1)}, u32[]{:S(2)}) copy-start(bf16[4,2,32,1024]{3,2,1,0:T(8,128)(2,1)} %get-tuple-element.181) | copy-start | bytes 1572868
  371.7 15.2 %collective-permute-start.20 = (bf16[4,32,1024]{2,1,0:T(8,128)(2,1)S(1)}, bf16[4,32,1024]{2,1,0:T(8,128)(2,1)S(1)}, u32[]{:S(2)}, u32[]{:S(2)}) collective-permute-start(bf16[4,32,1024]{2,1,0:T(8,128)(2,1)S(1)} %dynamic-slice_bitcast_fusion), channel_id=1, source_target_pairs={{0,16},{8,24},{16,0},{24,8},{1,17},{9,25},{17,1},{25,9},{2,18},{10... | collective-permute-start | bytes 786440 | tf_op jit(solution)/shard_map/ppermute | solution.py:25
  374.7 10.4 %all-to-all-start.7 = ((f32[32,1,128]{2,1,0:T(1,128)}), f32[32,1,128]{2,1,0:T(1,128)S(1)}, u32[]{:S(2)}, u32[]{:S(2)}) async-start(f32[32,1,128]{2,1,0:T(1,128)} %reshape.113), calls=%async_computation.7 | async-start | bytes 32768 | tf_op jit(solution)/shard_map/all_to_all | solution.py:243
  (3 other events, 3.0 us)
Sparse Core Ops, SparseCore 0:
  10.7 92.0 all-gather.4
  123.9 151.3 all-gather.6

commit v3 on v2

--- a/solution.py
+++ b/solution.py
@@ -81,13 +81,14 @@
     return [pieces[r] for r in order], order, more, last
 
 
-def scatter_relative(near, far, axis):
+def scatter_relative(near, far, axis, marks):
     size = lax.axis_size(axis)
     got = yield swapped(far, axis, 1)
     both = added(near, got)
     count = size // 2
     rows = both.shape[1] // count
     pieces = {2 * i: rounded(both[:, i * rows : (i + 1) * rows]) for i in range(count)}
+    marks.append(pieces)
     bits = list(outer_bits(size))
     for level in range(len(bits), 0, -1):
         sent, spans = [], []
@@ -1108,7 +1109,8 @@
         near_bias, queries, keys, values, bias, log_total, attended, grad_attended
     )
     backs = (back_first, back_second, back_near, back_own, grad_queries)
-    prompt_sums = scatter_relative(back_first, back_second, "expert")
+    prompt_marks = []
+    prompt_sums = scatter_relative(back_first, back_second, "expert", prompt_marks)
     prompt_sent = next(prompt_sums)
     near_back = lax.ppermute(
         back_near, "expert", [(i + 1, i) for i in range(0, experts, 2)]
@@ -1132,7 +1134,8 @@
     weight_sums = weight_chain(*weights, marks)
     weight_sent = next(weight_sums)
     prompt_sent, prompt_back = moved_on(prompt_sums, prompt_sent)
-    result_got = far_got[:, 0].reshape(slots, width)
+    far_late, _ = tied((far_got, list(prompt_marks[-1].values())))
+    result_got = far_late[:, 0].reshape(slots, width)
     result = rounded(residual + matmul_tn(spread, result_got))
     weight_sent, prompt_sent, result = tied((weight_sent, prompt_sent, result))
     weight_sent, _ = moved_on(weight_sums, weight_sent)

time: 399 us -> 399 us (level)
  no operation moved by 1% of the time
where the time goes in v3:
time: 399 us; the launch traced here: 395 us
  Pallas kernels  249 us (62%)
  starting transfers between devices  58.7 us (15%)
  waiting for transfers between devices  31.3 us (8%)
  other arithmetic  17.4 us (4%)
  between operations  14.7 us (4%)
  local copies, waits for them, and re-layouts  12.3 us (3%)
  matrix products  11.2 us (3%)
    pallas_call x2, Pallas kernels, in_sums(): pl.pallas_call(functools.partial(in_kernel, half), grid_spec=pltpu.Prefet...  37.5 us
    pallas_call x1, Pallas kernels, attend_back(): pl.pallas_call(functools.partial(attend_back_kernel, prompt_len), grid=(p...  34.1 us
    pallas_call x1, Pallas kernels, expert_front(): pl.pallas_call(functools.partial(front_kernel, 4), grid=(ff // block,), i...  25.4 us
    pallas_call x1, Pallas kernels, attend(): pl.pallas_call(functools.partial(attend_kernel, prompt_len), grid=(pairs,...  23.2 us
    all_to_all x5, starting transfers between devices, all_exchanged(): lax.all_to_all(values, 'expert', split_axis=0, concat_axis=0, tiled=True)  21.5 us
    ppermute x19, starting transfers between devices, swapped(): lax.ppermute(block, axis, [(i, i ^ mask) for i in range(lax.axis_size(axi...  20.1 us
    pallas_call x1, Pallas kernels, weight_parts(): pl.pallas_call(weights_kernel, grid=(groups,), in_specs=[pl.BlockSpec(mem...  18.6 us
    pallas_call x1, Pallas kernels, project(): pl.pallas_call(functools.partial(project_kernel, len(pieces)), grid=(widt...  16.9 us
  transfers between devices with their start and end apart: 31, of which 13 were waited for; matrix products, arithmetic and copies ran while one was open for 8% of the time, Pallas kernels for 63%

profile of v3, /device:TPU:0, one launch (start us, length us, event | category | flops | bytes accessed | tf_op | source)
XLA Modules:
  0.0 394.9 jit_solution(4734545895646434373)
XLA Ops:
  8.2 2.4 pad_maximum_fusion
  10.6 2.5 collective-permute-start.2
  13.2 2.4 collective-permute-start
  17.4 4.1 %collective-permute-done.refs_1_ = bf16[128,1024]{1,0:T(8,128)(2,1)} collective-permute-done((bf16[128,1024]{1,0:T(8,128)(2,1)S(1)}, bf16[128,1024]{1,0:T(8,128)(2,1)}, u32[]{:S(2)}, u32[]{:S(2)}) %collective-permute-start) | collective-permute-done | bytes 262176 | tf_op jit(solution)/shard_map/ppermute | solution.py:25
  25.4 2.6 fusion.5
  28.6 1.9 collective-permute-done.3.refs_3_
  30.6 3.9 all-to-all-start.1
  35.5 16.9 %project.1 = (bf16[1792,1024]{1,0:T(8,128)(2,1)}, bf16[512,1024]{1,0:T(8,128)(2,1)}, bf16[1792,1024]{1,0:T(8,128)(2,1)}, bf16[1792,1024]{1,0:T(8,128)(2,1)}) custom-call(f32[1,1024]{1,0:T(1,128)} %bitcast.75, f32[1,1024]{1,0:T(1,128)} %bitcast.79, bf16[1024,1024]{1,0:T(8,128)(2,1)} %wq_ref.3, bf16[1024,1024]{1,0:T(8,128)(2,1)} %wk_ref.3, ...), custom_call_target="tpu_custom_call" | custom-call | flops 375809632 | bytes 943718 | tf_op jit(solution)/shard_map/project/pallas_call | solution.py:654
  52.4 23.2 %attend.1 = (bf16[512,1024]{1,0:T(8,128)(2,1)}, f32[8,4,256]{2,1,0:T(4,128)}) custom-call(f32[1]{0:T(128)} %bitcast.1.near_ref, bf16[512,1024]{1,0:T(8,128)(2,1)} %get-tuple-element.105.q_ref, bf16[1792,1024]{1,0:T(8,128)(2,1)} %get-tuple-element.106.k_ref, bf16[1792,1024]{1,0:T(8,128)(2,1)} %get-tuple-element.107.v_ref, f32[1024,128]{1,0:T(8,128)} %compare_select_fusion.bias_ref), custom_call_target="tpu_custom_call" | custom-call | flops 751619264 | bytes 471859 | tf_op jit(solution)/shard_map/attend/pallas_call | solution.py:963
  75.6 3.3 fusion.17
  80.2 2.9 fusion.4
  84.4 4.8 %all-to-all-start = ((bf16[8,128,1024]{2,1,0:T(8,128)(2,1)}), bf16[8,128,1024]{2,1,0:T(8,128)(2,1)S(1)}, u32[]{:S(2)}, u32[]{:S(2)}) async-start(bf16[8,128,1024]{2,1,0:T(8,128)(2,1)} %bitcast.71), calls=%async_computation | async-start | bytes 4194304 | tf_op jit(solution)/shard_map/all_to_all | solution.py:1045
  89.2 13.2 %expert_back.1.gh_ref = bf16[1024,4096]{1,0:T(8,128)(2,1)} custom-call(bf16[1024,1024]{1,0:T(8,128)(2,1)} %bitcast.67, bf16[1,4096,1024]{2,1,0:T(8,128)(2,1)} %wout_hbm.3), custom_call_target="tpu_custom_call" | custom-call | flops 429496736 | bytes 838860 | tf_op jit(solution)/shard_map/expert_back/pallas_call | solution.py:270
  104.8 4.0 %spread_rows.2 = bf16[8,1,128,1024]{3,2,1,0:T(8,128)(2,1)} custom-call(s32[1]{0:T(128)} %bitcast.21._, s32[4,1,512]{2,1,0:T(1,128)} %reshape.110.ids_ref, bf16[4,512,1152]{2,1,0:T(8,128)(2,1)} %bitcast.65), custom_call_target="tpu_custom_call" | custom-call | flops 53687092 | bytes 400000 | tf_op jit(solution)/shard_map/spread_rows/pallas_call | solution.py:610
  108.9 7.0 %all-to-all-done = bf16[8,128,1024]{2,1,0:T(8,128)(2,1)S(1)} async-done(((bf16[8,128,1024]{2,1,0:T(8,128)(2,1)}), bf16[8,128,1024]{2,1,0:T(8,128)(2,1)S(1)}, u32[]{:S(2)}, u32[]{:S(2)}) %all-to-all-start) | async-done | bytes 2097184 | tf_op jit(solution)/shard_map/all_to_all | solution.py:1045
  117.1 4.3 %all-to-all-start.2 = ((bf16[8,1,128,1024]{3,2,1,0:T(8,128)(2,1)}), bf16[8,1,128,1024]{3,2,1,0:T(8,128)(2,1)}, u32[]{:S(2)}, u32[]{:S(2)}) async-start(bf16[8,1,128,1024]{3,2,1,0:T(8,128)(2,1)} %spread_rows.2), calls=%async_computation.2 | async-start | bytes 4194304 | tf_op jit(solution)/shard_map/all_to_all | solution.py:1045
  122.2 25.4 %expert_front.1 = (bf16[1024,4096]{1,0:T(8,128)(2,1)}, bf16[1024,4096]{1,0:T(8,128)(2,1)}, bf16[1024,1024]{1,0:T(8,128)(2,1)}) custom-call(bf16[1024,1024]{1,0:T(8,128)(2,1)} %bitcast.59, bf16[1024,4096]{1,0:T(8,128)(2,1)} %expert_back.1.gh_ref, bf16[1,1024,4096]{2,1,0:T(8,128)(2,1)} %win_hbm.3), custom_call_target="tpu_custom_call" | custom-call | flops 858993472 | bytes 1677721 | tf_op jit(solution)/shard_map/expert_front/pallas_call | solution.py:317
  148.1 3.6 all-to-all-start.3
  152.3 14.6 %expert_produce.1.refs_0_ = bf16[1024,1024]{1,0:T(8,128)(2,1)} custom-call(bf16[1024,4096]{1,0:T(8,128)(2,1)} %get-tuple-element.116.hidden_ref, bf16[1,4096,1024]{2,1,0:T(8,128)(2,1)} %wout_hbm.3), custom_call_target="tpu_custom_call" | custom-call | flops 429496736 | bytes 838860 | tf_op jit(solution)/shard_map/expert_produce/pallas_call | solution.py:355
  167.0 7.6 %spread_rows.3 = bf16[8,3,128,1024]{3,2,1,0:T(8,128)(2,1)} custom-call(s32[2]{0:T(128)} %pad_add_fusion._, s32[4,1,512]{2,1,0:T(1,128)} %reshape.110.ids_ref, bf16[4,512,1152]{2,1,0:T(8,128)(2,1)} %bitcast.66, bf16[1024,1024]{1,0:T(8,128)(2,1)} %expert_produce.1.refs_0_), custom_call_target="tpu_custom_call" | custom-call | flops 161061280 | bytes 400000 | tf_op jit(solution)/shard_map/spread_rows/pallas_call | solution.py:610
  174.6 3.8 all-to-all-done.3
  179.7 4.9 %all-to-all-start.4 = ((bf16[8,3,128,1024]{3,2,1,0:T(8,128)(2,1)}), bf16[8,3,128,1024]{3,2,1,0:T(8,128)(2,1)}, u32[]{:S(2)}, u32[]{:S(2)}) async-start(bf16[8,3,128,1024]{3,2,1,0:T(8,128)(2,1)} %spread_rows.3), calls=%async_computation.4 | async-start | bytes 12582912 | tf_op jit(solution)/shard_map/all_to_all | solution.py:1045
  186.0 8.0 %resid_back.1 = (f32[512,1024]{1,0:T(8,128)}, bf16[512,1024]{1,0:T(8,128)(2,1)}, bf16[512,1024]{1,0:T(8,128)(2,1)}, f32[2,1024]{1,0:T(2,128)}) custom-call(bf16[1024,1024]{1,0:T(8,128)(2,1)} %bitcast.69, bf16[1024,512]{1,0:T(8,128)(2,1)} %fusion.1.spread_ref, f32[512,1024]{1,0:T(8,128)} %copy-done.2, f32[1,1024]{1,0:T(1,128)} %bitcast.80, ...), custom_call_target="tpu_custom_call" | custom-call | flops 107374184 | bytes 419430 | tf_op jit(solution)/shard_map/resid_back/pallas_call | solution.py:754
  194.0 34.1 %attend_back.1 = (bf16[512,1024]{1,0:T(8,128)(2,1)}, bf16[2,512,1024]{2,1,0:T(8,128)(2,1)}, bf16[2,512,1024]{2,1,0:T(8,128)(2,1)}, bf16[2,384,1024]{2,1,0:T(8,128)(2,1)}, bf16[2,384,1024]{2,1,0:T(8,128)(2,1)}) custom-call(f32[1]{0:T(128)} %bitcast.1.near_ref, bf16[512,1024]{1,0:T(8,128)(2,1)} %get-tuple-element.105.q_ref, ...), custom_call_target="tpu_custom_call" | custom-call | flops 1879048192 | bytes 943718 | tf_op jit(solution)/shard_map/attend_back/pallas_call | solution.py:996
  229.8 18.6 %weight_parts.1 = (bf16[4,4,4,32,1024]{4,3,2,1,0:T(8,128)(2,1)}, bf16[4,4,4,32,1024]{4,3,2,1,0:T(8,128)(2,1)}) custom-call(s32[1]{0:T(128)} %bitcast.odd_ref, bf16[512,1024]{1,0:T(8,128)(2,1)} %get-tuple-element.108.out_ref.refs_0_, bf16[1792,1024]{1,0:T(8,128)(2,1)} %get-tuple-element.109.refs_1_, bf16[512,1024]{1,0:T(8,128)(2,1)} %get-tuple-element.119.refs_2_, ...), custom_call_target="tpu_custom_call" | custom-call | flops 500000000 | bytes 1500000 | tf_op jit(solution)/shard_map/weight_parts/pallas_call | solution.py:711
  248.4 5.8 %own_out.1.own_ref = f32[1024,1024]{1,0:T(8,128)} custom-call(s32[1]{0:T(128)} %bitcast.25._.own_ref, bf16[1024,4096]{1,0:T(8,128)(2,1)} %get-tuple-element.116.hidden_ref, bf16[1024,1024]{1,0:T(8,128)(2,1)} %bitcast.68), custom_call_target="tpu_custom_call" | custom-call | flops 107374184 | bytes 400000 | tf_op jit(solution)/shard_map/own_out/pallas_call | solution.py:470
  254.2 2.0 all-to-all-done.4.far_hbm.far_ref
  256.5 1.9 slice.71
  258.4 3.3 add_convert_fusion
  265.0 2.3 add_convert_fusion.1
  267.3 3.5 collective-permute-done.11
  270.8 1.9 collective-permute-done.12
  272.7 5.4 %halve.2 = (bf16[2,4,2,32,1024]{4,3,2,1,0:T(8,128)(2,1)}, bf16[2,4,2,32,1024]{4,3,2,1,0:T(8,128)(2,1)}, bf16[2,4,2,32,1024]{4,3,2,1,0:T(8,128)(2,1)}, bf16[2,4,2,32,1024]{4,3,2,1,0:T(8,128)(2,1)}) custom-call(s32[1]{0:T(128)} %bitcast.27.own_ref, bf16[4,4,4,32,1024]{4,3,2,1,0:T(8,128)(2,1)} %get-tuple-element.136.refs_0_.refs_2_, ...), custom_call_target="tpu_custom_call" | custom-call | flops 104857 | bytes 629145 | tf_op jit(solution)/shard_map/halve/pallas_call | solution.py:160
  280.8 18.7 %in_sums.2 = (bf16[4,256,512]{2,1,0:T(8,128)(2,1)}, bf16[1024,512]{1,0:T(8,128)(2,1)}, bf16[2,1024,512]{2,1,0:T(8,128)(2,1)}) custom-call(s32[4]{0:T(128)} %pad_add_fusion.1.number_ref, bf16[1024,1024]{1,0:T(8,128)(2,1)} %bitcast.60, bf16[1024,4096]{1,0:T(8,128)(2,1)} %get-tuple-element.140.own_pre_ref, bf16[1,1024,4096]{2,1,0:T(8,128)(2,1)} %win_hbm.3, ...), custom_call_target="tpu_custom_call" | custom-call | flops 644245120 | bytes 800000 | tf_op jit(solution)/shard_map/in_sums/pallas_call | solution.py:424
  299.5 5.3 %all-to-all-start.5 = ((bf16[4,256,512]{2,1,0:T(8,128)(2,1)}), bf16[4,256,512]{2,1,0:T(8,128)(2,1)S(1)}, u32[]{:S(2)}, u32[]{:S(2)}) async-start(bf16[4,256,512]{2,1,0:T(8,128)(2,1)} %get-tuple-element.142), calls=%async_computation.5 | async-start | bytes 2097152 | tf_op jit(solution)/shard_map/all_to_all | solution.py:1145
  305.0 2.2 add_convert_fusion.6
  309.1 3.3 halve.3
  314.6 18.8 %in_sums.3 = (bf16[4,256,512]{2,1,0:T(8,128)(2,1)}, bf16[1024,512]{1,0:T(8,128)(2,1)}, bf16[2,1024,512]{2,1,0:T(8,128)(2,1)}) custom-call(s32[4]{0:T(128)} %pad_add_fusion.1.number_ref, bf16[1024,1024]{1,0:T(8,128)(2,1)} %bitcast.61, bf16[1024,4096]{1,0:T(8,128)(2,1)} %get-tuple-element.140.own_pre_ref, bf16[1,1024,4096]{2,1,0:T(8,128)(2,1)} %win_hbm.3, ...), custom_call_target="tpu_custom_call" | custom-call | flops 644245120 | bytes 800000 | tf_op jit(solution)/shard_map/in_sums/pallas_call | solution.py:424
  334.2 5.1 %all-to-all-start.6 = ((bf16[4,256,512]{2,1,0:T(8,128)(2,1)}), bf16[4,256,512]{2,1,0:T(8,128)(2,1)}, u32[]{:S(2)}, u32[]{:S(2)}) async-start(bf16[4,256,512]{2,1,0:T(8,128)(2,1)} %get-tuple-element.161), calls=%async_computation.6 | async-start | bytes 2097152 | tf_op jit(solution)/shard_map/all_to_all | solution.py:1145
  339.4 2.3 add_convert_fusion.5.prompt_ref
  341.6 10.6 %input_back.1 = (bf16[512,1024]{1,0:T(8,128)(2,1)}, f32[2,1024]{1,0:T(2,128)}) custom-call(bf16[2,128,1024]{2,1,0:T(8,128)(2,1)} %add_convert_fusion.5.prompt_ref, bf16[2,384,1024]{2,1,0:T(8,128)(2,1)} %get-tuple-element.126.refs_7_.own_ref, bf16[2,384,1024]{2,1,0:T(8,128)(2,1)} %collective-permute-done.9.near_ref, ...), custom_call_target="tpu_custom_call" | custom-call | flops 161061280 | bytes 524288 | tf_op jit(solution)/shard_map/input_back/pallas_call | solution.py:821
  352.3 2.7 turn.1
  355.0 2.0 collective-permute-start.19
  357.0 14.1 %out_sums.1 = f32[1,1024,1024]{2,1,0:T(8,128)} custom-call(f32[1024,1024]{1,0:T(8,128)} %own_out.1.own_ref, bf16[8,1,128,1024]{3,2,1,0:T(8,128)(2,1)} %all-to-all-done.2.near_hbm.near_ref, bf16[8,3,128,1024]{3,2,1,0:T(8,128)(2,1)} %all-to-all-done.4.far_hbm.far_ref, bf16[1024,512]{1,0:T(8,128)(2,1)} %get-tuple-element.174.refs_0_, ...), custom_call_target="tpu_custom_call" | custom-call | flops 322122560 | bytes 800000 | tf_op jit(solution)/shard_map/out_sums/pallas_call | solution.py:519
  371.7 2.1 collective-permute-start.20
  374.7 2.7 all-to-all-start.7
  377.4 4.2 %lay_out.1 = f32[1,256,4096]{2,1,0:T(8,128)} custom-call(bf16[4,256,512]{2,1,0:T(8,128)(2,1)} %copy-done.5, bf16[4,256,512]{2,1,0:T(8,128)(2,1)} %all-to-all-done.6.refs_1_), custom_call_target="tpu_custom_call" | custom-call | flops 52428 | bytes 314572 | tf_op jit(solution)/shard_map/lay_out/pallas_call | solution.py:550
  381.6 3.5 all-to-all-done.7
  (117 shorter events, 36.4 us)
Async XLA Ops:
  7.2 3.4 copy-start.6
  7.2 95.6 %all-gather.5.cloned.1.call-start = ((), (), s32[]{:S(2)}) async-start(), calls=%async_computation.8 | async-start | bytes 5898240 | tf_op jit(solution)/shard_map/all_gather | solution.py:1058
  10.5 6.6 %copy-start.15 = (s32[512,1]{0,1:T(1,128)S(1)}, s32[512,1]{0,1:T(1,128)}, u32[]{:S(2)}) copy-start(s32[512,1]{0,1:T(1,128)} %param.15) | copy-start | bytes 6148
  10.5 14.9 %copy-start.7 = (bf16[512,1024]{1,0:T(8,128)(2,1)S(1)}, bf16[512,1024]{1,0:T(8,128)(2,1)}, u32[]{:S(2)}) copy-start(bf16[512,1024]{1,0:T(8,128)(2,1)} %cot_ref.1) | copy-start | bytes 3145732
  10.6 17.3 %copy-start.8 = (bf16[384,1024]{1,0:T(8,128)(2,1)}, bf16[384,1024]{1,0:T(8,128)(2,1)S(1)}, u32[]{:S(2)}) copy-start(bf16[384,1024]{1,0:T(8,128)(2,1)S(1)} %slice.63.refs_9_) | copy-start | bytes 2359300
  10.6 12.3 %collective-permute-start.2 = (bf16[384,1024]{1,0:T(8,128)(2,1)S(1)}, bf16[384,1024]{1,0:T(8,128)(2,1)S(1)}, u32[]{:S(2)}, u32[]{:S(2)}) collective-permute-start(bf16[384,1024]{1,0:T(8,128)(2,1)S(1)} %slice.63.refs_9_), channel_id=1, source_target_pairs={{0,1},{2,3},{4,5},{6,7},{8,9},{10,11},{12,13},{14,15},{16,17},{18,... | collective-permute-start | bytes 2359304 | tf_op jit(solution)/shard_map/ppermute | solution.py:1051
  13.2 14.8 %copy-start.10 = (bf16[128,1024]{1,0:T(8,128)(2,1)}, bf16[128,1024]{1,0:T(8,128)(2,1)S(1)}, u32[]{:S(2)}) copy-start(bf16[128,1024]{1,0:T(8,128)(2,1)S(1)} %slice.62.refs_0_) | copy-start | bytes 786436
  13.2 8.3 %collective-permute-start = (bf16[128,1024]{1,0:T(8,128)(2,1)S(1)}, bf16[128,1024]{1,0:T(8,128)(2,1)}, u32[]{:S(2)}, u32[]{:S(2)}) collective-permute-start(bf16[128,1024]{1,0:T(8,128)(2,1)S(1)} %slice.62.refs_0_), channel_id=1, source_target_pairs={{0,2},{1,3},{2,0},{3,1},{4,6},{5,7},{6,4},{7,5},{8,10},{9,11},{10,... | collective-permute-start | bytes 786440 | tf_op jit(solution)/shard_map/ppermute | solution.py:25
  15.6 7.4 %collective-permute-start.1 = (bf16[128,1024]{1,0:T(8,128)(2,1)S(1)}, bf16[128,1024]{1,0:T(8,128)(2,1)}, u32[]{:S(2)}, u32[]{:S(2)}) collective-permute-start(bf16[128,1024]{1,0:T(8,128)(2,1)S(1)} %slice.62.refs_0_), channel_id=1, source_target_pairs={{0,4},{1,5},{2,6},{3,7},{4,0},{5,1},{6,2},{7,3},{8,12},{9,13},{10,... | collective-permute-start | bytes 786440 | tf_op jit(solution)/shard_map/ppermute | solution.py:25
  17.1 18.4 %collective-permute-start.4 = (bf16[128,1024]{1,0:T(8,128)(2,1)S(1)}, bf16[128,1024]{1,0:T(8,128)(2,1)}, u32[]{:S(2)}, u32[]{:S(2)}) collective-permute-start(bf16[128,1024]{1,0:T(8,128)(2,1)S(1)} %slice.62.refs_0_), channel_id=1, source_target_pairs={{0,1},{1,0},{2,3},{3,2},{4,5},{5,4},{6,7},{7,6},{8,9},{9,8},{10,11... | collective-permute-start | bytes 786440 | tf_op jit(solution)/shard_map/ppermute | solution.py:25
  23.9 6.7 %collective-permute-start.3 = (bf16[128,1024]{1,0:T(8,128)(2,1)}, bf16[128,1024]{1,0:T(8,128)(2,1)}, u32[]{:S(2)}, u32[]{:S(2)}) collective-permute-start(bf16[128,1024]{1,0:T(8,128)(2,1)} %collective-permute-done.refs_1_), channel_id=1, source_target_pairs={{0,4},{1,5},{2,6},{3,7},{4,0},{5,1},{6,2},{7,3},{8,12},{9,13},{10,... | collective-permute-start | bytes 786440 | tf_op jit(solution)/shard_map/ppermute | solution.py:25
  28.1 7.4 %collective-permute-start.5 = (bf16[128,1024]{1,0:T(8,128)(2,1)}, bf16[128,1024]{1,0:T(8,128)(2,1)}, u32[]{:S(2)}, u32[]{:S(2)}) collective-permute-start(bf16[128,1024]{1,0:T(8,128)(2,1)} %collective-permute-done.refs_1_), channel_id=1, source_target_pairs={{0,1},{1,0},{2,3},{3,2},{4,5},{5,4},{6,7},{7,6},{8,9},{9,8},{10,11... | collective-permute-start | bytes 786440 | tf_op jit(solution)/shard_map/ppermute | solution.py:25
  28.1 7.4 %collective-permute-start.6 = (bf16[128,1024]{1,0:T(8,128)(2,1)}, bf16[128,1024]{1,0:T(8,128)(2,1)}, u32[]{:S(2)}, u32[]{:S(2)}) collective-permute-start(bf16[128,1024]{1,0:T(8,128)(2,1)} %collective-permute-done.1.refs_2_), channel_id=1, source_target_pairs={{0,1},{1,0},{2,3},{3,2},{4,5},{5,4},{6,7},{7,6},{8,9},{9,8},{10,11... | collective-permute-start | bytes 786440 | tf_op jit(solution)/shard_map/ppermute | solution.py:25
  30.6 5.0 %collective-permute-start.7 = (bf16[128,1024]{1,0:T(8,128)(2,1)}, bf16[128,1024]{1,0:T(8,128)(2,1)}, u32[]{:S(2)}, u32[]{:S(2)}) collective-permute-start(bf16[128,1024]{1,0:T(8,128)(2,1)} %collective-permute-done.3.refs_3_), channel_id=1, source_target_pairs={{0,1},{1,0},{2,3},{3,2},{4,5},{5,4},{6,7},{7,6},{8,9},{9,8},{10,11... | collective-permute-start | bytes 786440 | tf_op jit(solution)/shard_map/ppermute | solution.py:25
  30.6 52.5 %all-to-all-start.1 = ((bf16[8,128,1024]{2,1,0:T(8,128)(2,1)}), bf16[8,128,1024]{2,1,0:T(8,128)(2,1)S(1)}, u32[]{:S(2)}, u32[]{:S(2)}) async-start(bf16[8,128,1024]{2,1,0:T(8,128)(2,1)} %bitcast.70), calls=%async_computation.1 | async-start | bytes 4194304 | tf_op jit(solution)/shard_map/all_to_all | solution.py:1045
  78.9 1.3 copy-start.2
  78.9 1.3 copy-start.18
  78.9 1.3 copy-start.19
  83.1 1.4 copy-start.1
  84.4 31.4 %all-to-all-start = ((bf16[8,128,1024]{2,1,0:T(8,128)(2,1)}), bf16[8,128,1024]{2,1,0:T(8,128)(2,1)S(1)}, u32[]{:S(2)}, u32[]{:S(2)}) async-start(bf16[8,128,1024]{2,1,0:T(8,128)(2,1)} %bitcast.71), calls=%async_computation | async-start | bytes 4194304 | tf_op jit(solution)/shard_map/all_to_all | solution.py:1045
  115.8 1.3 copy-start
  117.1 31.0 %all-to-all-start.2 = ((bf16[8,1,128,1024]{3,2,1,0:T(8,128)(2,1)}), bf16[8,1,128,1024]{3,2,1,0:T(8,128)(2,1)}, u32[]{:S(2)}, u32[]{:S(2)}) async-start(bf16[8,1,128,1024]{3,2,1,0:T(8,128)(2,1)} %spread_rows.2), calls=%async_computation.2 | async-start | bytes 4194304 | tf_op jit(solution)/shard_map/all_to_all | solution.py:1045
  121.5 159.3 %all-gather.7.cloned.1.call-start = ((), (), s32[]{:S(2)}) async-start(), calls=%async_computation.9 | async-start | bytes 10485760 | tf_op jit(solution)/shard_map/all_gather | solution.py:1095
  148.1 30.2 %all-to-all-start.3 = ((bf16[8,128,1024]{2,1,0:T(8,128)(2,1)}), bf16[8,128,1024]{2,1,0:T(8,128)(2,1)S(1)}, u32[]{:S(2)}, u32[]{:S(2)}) async-start(bf16[8,128,1024]{2,1,0:T(8,128)(2,1)} %bitcast.72), calls=%async_computation.3 | async-start | bytes 4194304 | tf_op jit(solution)/shard_map/all_to_all | solution.py:1045
  179.7 76.5 %all-to-all-start.4 = ((bf16[8,3,128,1024]{3,2,1,0:T(8,128)(2,1)}), bf16[8,3,128,1024]{3,2,1,0:T(8,128)(2,1)}, u32[]{:S(2)}, u32[]{:S(2)}) async-start(bf16[8,3,128,1024]{3,2,1,0:T(8,128)(2,1)} %spread_rows.3), calls=%async_computation.4 | async-start | bytes 12582912 | tf_op jit(solution)/shard_map/all_to_all | solution.py:1045
  228.1 26.1 %collective-permute-start.8 = (bf16[2,512,1024]{2,1,0:T(8,128)(2,1)}, bf16[2,512,1024]{2,1,0:T(8,128)(2,1)S(1)}, u32[]{:S(2)}, u32[]{:S(2)}) collective-permute-start(bf16[2,512,1024]{2,1,0:T(8,128)(2,1)} %get-tuple-element.124.refs_5_), channel_id=1, source_target_pairs={{0,1},{1,0},{2,3},{3,2},{4,5},{5,4},{6,7},{7,6},{8,9},{9,8},{10,11... | collective-permute-start | bytes 6291464 | tf_op jit(solution)/shard_map/ppermute | solution.py:25
  228.5 25.7 %collective-permute-start.9 = (bf16[2,384,1024]{2,1,0:T(8,128)(2,1)}, bf16[2,384,1024]{2,1,0:T(8,128)(2,1)}, u32[]{:S(2)}, u32[]{:S(2)}) collective-permute-start(bf16[2,384,1024]{2,1,0:T(8,128)(2,1)} %get-tuple-element.125.refs_6_), channel_id=1, source_target_pairs={{1,0},{3,2},{5,4},{7,6},{9,8},{11,10},{13,12},{15,14},{17,16},{19,... | collective-permute-start | bytes 4718600 | tf_op jit(solution)/shard_map/ppermute | solution.py:1115
  254.2 2.3 copy-start.9
  256.2 16.5 %collective-permute-start.10 = (bf16[4,4,4,32,1024]{4,3,2,1,0:T(8,128)(2,1)}, bf16[4,4,4,32,1024]{4,3,2,1,0:T(8,128)(2,1)}, u32[]{:S(2)}, u32[]{:S(2)}) collective-permute-start(bf16[4,4,4,32,1024]{4,3,2,1,0:T(8,128)(2,1)} %get-tuple-element.131), channel_id=1, source_target_pairs={{0,1},{1,0},{2,3},{3,2},{4,5},{5,4},{6,7},{7,6},{8,9},{9,8},{10,11... | collective-permute-start | bytes 12582920 | tf_op jit(solution)/shard_map/ppermute | solution.py:25
  258.4 6.6 %copy-start.3 = (f32[512,1024]{1,0:T(8,128)S(1)}, f32[512,1024]{1,0:T(8,128)}, u32[]{:S(2)}) copy-start(f32[512,1024]{1,0:T(8,128)} %copy-done.2) | copy-start | bytes 6291460
  261.8 8.9 %collective-permute-start.11 = (bf16[2,64,1024]{2,1,0:T(8,128)(2,1)S(1)}, bf16[2,64,1024]{2,1,0:T(8,128)(2,1)S(1)}, u32[]{:S(2)}, u32[]{:S(2)}) collective-permute-start(bf16[2,64,1024]{2,1,0:T(8,128)(2,1)S(1)} %get-tuple-element.191), channel_id=1, source_target_pairs={{0,4},{1,5},{2,6},{3,7},{4,0},{5,1},{6,2},{7,3},{8,12},{9,13},{10,... | collective-permute-start | bytes 786440 | tf_op jit(solution)/shard_map/ppermute | solution.py:25
  263.5 9.2 %collective-permute-start.12 = (bf16[2,64,1024]{2,1,0:T(8,128)(2,1)S(1)}, bf16[2,64,1024]{2,1,0:T(8,128)(2,1)S(1)}, u32[]{:S(2)}, u32[]{:S(2)}) collective-permute-start(bf16[2,64,1024]{2,1,0:T(8,128)(2,1)S(1)} %get-tuple-element.190), channel_id=1, source_target_pairs={{0,2},{1,3},{2,0},{3,1},{4,6},{5,7},{6,4},{7,5},{8,10},{9,11},{10,... | collective-permute-start | bytes 786440 | tf_op jit(solution)/shard_map/ppermute | solution.py:25
  272.7 5.4 %copy-start.14 = (bf16[2,64,1024]{2,1,0:T(8,128)(2,1)}, bf16[2,64,1024]{2,1,0:T(8,128)(2,1)S(1)}, u32[]{:S(2)}) copy-start(bf16[2,64,1024]{2,1,0:T(8,128)(2,1)S(1)} %collective-permute-done.12) | copy-start | bytes 786436
  278.1 26.7 %collective-permute-start.13 = (bf16[2,4,2,32,1024]{4,3,2,1,0:T(8,128)(2,1)}, bf16[2,4,2,32,1024]{4,3,2,1,0:T(8,128)(2,1)}, u32[]{:S(2)}, u32[]{:S(2)}) collective-permute-start(bf16[2,4,2,32,1024]{4,3,2,1,0:T(8,128)(2,1)} %get-tuple-element.143), channel_id=1, source_target_pairs={{0,2},{1,3},{2,0},{3,1},{4,6},{5,7},{6,4},{7,5},{8,10},{9,11},{10,... | collective-permute-start | bytes 3145736 | tf_op jit(solution)/shard_map/ppermute | solution.py:25
  279.7 25.3 %collective-permute-start.14 = (bf16[2,4,2,32,1024]{4,3,2,1,0:T(8,128)(2,1)}, bf16[2,4,2,32,1024]{4,3,2,1,0:T(8,128)(2,1)}, u32[]{:S(2)}, u32[]{:S(2)}) collective-permute-start(bf16[2,4,2,32,1024]{4,3,2,1,0:T(8,128)(2,1)} %get-tuple-element.144), channel_id=1, source_target_pairs={{0,4},{1,5},{2,6},{3,7},{4,0},{5,1},{6,2},{7,3},{8,12},{9,13},{10,... | collective-permute-start | bytes 3145736 | tf_op jit(solution)/shard_map/ppermute | solution.py:25
  299.5 34.7 %all-to-all-start.5 = ((bf16[4,256,512]{2,1,0:T(8,128)(2,1)}), bf16[4,256,512]{2,1,0:T(8,128)(2,1)S(1)}, u32[]{:S(2)}, u32[]{:S(2)}) async-start(bf16[4,256,512]{2,1,0:T(8,128)(2,1)} %get-tuple-element.142), calls=%async_computation.5 | async-start | bytes 2097152 | tf_op jit(solution)/shard_map/all_to_all | solution.py:1145
  307.2 26.2 %collective-permute-start.15 = (bf16[2,128,1024]{2,1,0:T(8,128)(2,1)}, bf16[2,128,1024]{2,1,0:T(8,128)(2,1)}, u32[]{:S(2)}, u32[]{:S(2)}) collective-permute-start(bf16[2,128,1024]{2,1,0:T(8,128)(2,1)} %get-tuple-element.189), channel_id=1, source_target_pairs={{0,2},{1,3},{2,0},{3,1},{4,6},{5,7},{6,4},{7,5},{8,10},{9,11},{10,... | collective-permute-start | bytes 1572872 | tf_op jit(solution)/shard_map/ppermute | solution.py:25
  307.8 25.6 %collective-permute-start.16 = (bf16[2,128,1024]{2,1,0:T(8,128)(2,1)}, bf16[2,128,1024]{2,1,0:T(8,128)(2,1)}, u32[]{:S(2)}, u32[]{:S(2)}) collective-permute-start(bf16[2,128,1024]{2,1,0:T(8,128)(2,1)} %get-tuple-element.188), channel_id=1, source_target_pairs={{0,4},{1,5},{2,6},{3,7},{4,0},{5,1},{6,2},{7,3},{8,12},{9,13},{10,... | collective-permute-start | bytes 1572872 | tf_op jit(solution)/shard_map/ppermute | solution.py:25
  312.5 21.0 %collective-permute-start.17 = (bf16[2,4,1,32,1024]{4,3,2,1,0:T(8,128)(2,1)}, bf16[2,4,1,32,1024]{4,3,2,1,0:T(8,128)(2,1)S(1)}, u32[]{:S(2)}, u32[]{:S(2)}) collective-permute-start(bf16[2,4,1,32,1024]{4,3,2,1,0:T(8,128)(2,1)} %get-tuple-element.155), channel_id=1, source_target_pairs={{0,4},{1,5},{2,6},{3,7},{4,0},{5,1},{6,2},{7,3},{8,12},{9,13},{10,... | collective-permute-start | bytes 1572872 | tf_op jit(solution)/shard_map/ppermute | solution.py:25
  313.1 21.1 %collective-permute-start.18 = (bf16[2,4,1,32,1024]{4,3,2,1,0:T(8,128)(2,1)}, bf16[2,4,1,32,1024]{4,3,2,1,0:T(8,128)(2,1)}, u32[]{:S(2)}, u32[]{:S(2)}) collective-permute-start(bf16[2,4,1,32,1024]{4,3,2,1,0:T(8,128)(2,1)} %get-tuple-element.156), channel_id=1, source_target_pairs={{0,2},{1,3},{2,0},{3,1},{4,6},{5,7},{6,4},{7,5},{8,10},{9,11},{10,... | collective-permute-start | bytes 1572872 | tf_op jit(solution)/shard_map/ppermute | solution.py:25
  334.2 7.4 %copy-start.5 = (bf16[4,256,512]{2,1,0:T(8,128)(2,1)}, bf16[4,256,512]{2,1,0:T(8,128)(2,1)S(1)}, u32[]{:S(2)}) copy-start(bf16[4,256,512]{2,1,0:T(8,128)(2,1)S(1)} %all-to-all-done.5.refs_0_) | copy-start | bytes 3145732
  334.2 37.3 %all-to-all-start.6 = ((bf16[4,256,512]{2,1,0:T(8,128)(2,1)}), bf16[4,256,512]{2,1,0:T(8,128)(2,1)}, u32[]{:S(2)}, u32[]{:S(2)}) async-start(bf16[4,256,512]{2,1,0:T(8,128)(2,1)} %get-tuple-element.161), calls=%async_computation.6 | async-start | bytes 2097152 | tf_op jit(solution)/shard_map/all_to_all | solution.py:1145
  355.0 16.5 %collective-permute-start.19 = (bf16[4,2,32,1024]{3,2,1,0:T(8,128)(2,1)}, bf16[4,2,32,1024]{3,2,1,0:T(8,128)(2,1)S(1)}, u32[]{:S(2)}, u32[]{:S(2)}) collective-permute-start(bf16[4,2,32,1024]{3,2,1,0:T(8,128)(2,1)} %get-tuple-element.181), channel_id=1, source_target_pairs={{0,8},{8,0},{16,24},{24,16},{1,9},{9,1},{17,25},{25,17},{2,10},{10... | collective-permute-start | bytes 1572872 | tf_op jit(solution)/shard_map/ppermute | solution.py:25
  357.0 14.1 %copy-start.16 = (f32[2,1024]{1,0:T(2,128)S(1)}, f32[2,1024]{1,0:T(2,128)}, u32[]{:S(2)}) copy-start(f32[2,1024]{1,0:T(2,128)} %get-tuple-element.172) | copy-start | bytes 24580
  357.0 14.1 %copy-start.17 = (f32[2,1024]{1,0:T(2,128)S(1)}, f32[2,1024]{1,0:T(2,128)}, u32[]{:S(2)}) copy-start(f32[2,1024]{1,0:T(2,128)} %get-tuple-element.171) | copy-start | bytes 24580
  357.0 14.5 %copy-start.13 = (bf16[4,2,32,1024]{3,2,1,0:T(8,128)(2,1)S(1)}, bf16[4,2,32,1024]{3,2,1,0:T(8,128)(2,1)}, u32[]{:S(2)}) copy-start(bf16[4,2,32,1024]{3,2,1,0:T(8,128)(2,1)} %get-tuple-element.183) | copy-start | bytes 1572868
  371.7 15.2 %collective-permute-start.20 = (bf16[4,32,1024]{2,1,0:T(8,128)(2,1)S(1)}, bf16[4,32,1024]{2,1,0:T(8,128)(2,1)S(1)}, u32[]{:S(2)}, u32[]{:S(2)}) collective-permute-start(bf16[4,32,1024]{2,1,0:T(8,128)(2,1)S(1)} %dynamic-slice_bitcast_fusion), channel_id=1, source_target_pairs={{0,16},{8,24},{16,0},{24,8},{1,17},{9,25},{17,1},{25,9},{2,18},{10... | collective-permute-start | bytes 786440 | tf_op jit(solution)/shard_map/ppermute | solution.py:25
  374.7 10.4 %all-to-all-start.7 = ((f32[32,1,128]{2,1,0:T(1,128)}), f32[32,1,128]{2,1,0:T(1,128)S(1)}, u32[]{:S(2)}, u32[]{:S(2)}) async-start(f32[32,1,128]{2,1,0:T(1,128)} %reshape.113), calls=%async_computation.7 | async-start | bytes 32768 | tf_op jit(solution)/shard_map/all_to_all | solution.py:244
  (3 other events, 3.0 us)
Sparse Core Ops, SparseCore 0:
  10.7 92.0 all-gather.4
  123.9 151.3 all-gather.6

commit v4 on v2

--- a/solution.py
+++ b/solution.py
@@ -646,7 +646,7 @@
     width = gain.shape[0]
     size = sum(p.shape[0] for p in pieces)
     own = pieces[0].shape[0] + pieces[-1].shape[0]
-    block = 512
+    block = 256
     whole = lambda rows: pl.BlockSpec((rows, width), lambda j: (0, 0))
     weights = pl.BlockSpec((width, block), lambda j: (0, j))
     columns = lambda rows: pl.BlockSpec((rows, block), lambda j: (0, j))

time: 399 us -> 399 us (level)
  no operation moved by 1% of the time
where the time goes in v4:
time: 399 us; the launch traced here: 395 us
  Pallas kernels  249 us (62%)
  starting transfers between devices  58.6 us (15%)
  waiting for transfers between devices  31.3 us (8%)
  other arithmetic  17.4 us (4%)
  between operations  14.7 us (4%)
  local copies, waits for them, and re-layouts  12.3 us (3%)
  matrix products  11.2 us (3%)
    pallas_call x2, Pallas kernels, in_sums(): pl.pallas_call(functools.partial(in_kernel, half), grid_spec=pltpu.Prefet...  37.5 us
    pallas_call x1, Pallas kernels, attend_back(): pl.pallas_call(functools.partial(attend_back_kernel, prompt_len), grid=(p...  34.1 us
    pallas_call x1, Pallas kernels, expert_front(): pl.pallas_call(functools.partial(front_kernel, 4), grid=(ff // block,), i...  25.4 us
    pallas_call x1, Pallas kernels, attend(): pl.pallas_call(functools.partial(attend_kernel, prompt_len), grid=(pairs,...  23.2 us
    all_to_all x5, starting transfers between devices, all_exchanged(): lax.all_to_all(values, 'expert', split_axis=0, concat_axis=0, tiled=True)  21.5 us
    ppermute x19, starting transfers between devices, swapped(): lax.ppermute(block, axis, [(i, i ^ mask) for i in range(lax.axis_size(axi...  20.1 us
    pallas_call x1, Pallas kernels, weight_parts(): pl.pallas_call(weights_kernel, grid=(groups,), in_specs=[pl.BlockSpec(mem...  18.6 us
    pallas_call x1, Pallas kernels, project(): pl.pallas_call(functools.partial(project_kernel, len(pieces)), grid=(widt...  16.9 us
  transfers between devices with their start and end apart: 31, of which 13 were waited for; matrix products, arithmetic and copies ran while one was open for 8% of the time, Pallas kernels for 63%

profile of v4, /device:TPU:0, one launch (start us, length us, event | category | flops | bytes accessed | tf_op | source)
XLA Modules:
  0.0 394.8 jit_solution(17130684847575240798)
XLA Ops:
  8.2 2.4 pad_maximum_fusion
  10.6 2.5 collective-permute-start.2
  13.2 2.4 collective-permute-start
  17.4 4.1 %collective-permute-done.refs_1_ = bf16[128,1024]{1,0:T(8,128)(2,1)} collective-permute-done((bf16[128,1024]{1,0:T(8,128)(2,1)S(1)}, bf16[128,1024]{1,0:T(8,128)(2,1)}, u32[]{:S(2)}, u32[]{:S(2)}) %collective-permute-start) | collective-permute-done | bytes 262176 | tf_op jit(solution)/shard_map/ppermute | solution.py:25
  25.4 2.6 fusion.5
  28.6 1.9 collective-permute-done.3.refs_3_
  30.6 3.9 all-to-all-start.1
  35.5 16.9 %project.1 = (bf16[1792,1024]{1,0:T(8,128)(2,1)}, bf16[512,1024]{1,0:T(8,128)(2,1)}, bf16[1792,1024]{1,0:T(8,128)(2,1)}, bf16[1792,1024]{1,0:T(8,128)(2,1)}) custom-call(f32[1,1024]{1,0:T(1,128)} %bitcast.75, f32[1,1024]{1,0:T(1,128)} %bitcast.79, bf16[1024,1024]{1,0:T(8,128)(2,1)} %wq_ref.3, bf16[1024,1024]{1,0:T(8,128)(2,1)} %wk_ref.3, ...), custom_call_target="tpu_custom_call" | custom-call | flops 375809632 | bytes 943718 | tf_op jit(solution)/shard_map/project/pallas_call | solution.py:653
  52.4 23.2 %attend.1 = (bf16[512,1024]{1,0:T(8,128)(2,1)}, f32[8,4,256]{2,1,0:T(4,128)}) custom-call(f32[1]{0:T(128)} %bitcast.1.near_ref, bf16[512,1024]{1,0:T(8,128)(2,1)} %get-tuple-element.104.q_ref, bf16[1792,1024]{1,0:T(8,128)(2,1)} %get-tuple-element.105.k_ref, bf16[1792,1024]{1,0:T(8,128)(2,1)} %get-tuple-element.106.v_ref, f32[1024,128]{1,0:T(8,128)} %compare_select_fusion.bias_ref), custom_call_target="tpu_custom_call" | custom-call | flops 751619264 | bytes 471859 | tf_op jit(solution)/shard_map/attend/pallas_call | solution.py:962
  75.7 3.3 fusion.17
  80.3 2.9 fusion.4
  84.5 4.7 %all-to-all-start = ((bf16[8,128,1024]{2,1,0:T(8,128)(2,1)}), bf16[8,128,1024]{2,1,0:T(8,128)(2,1)S(1)}, u32[]{:S(2)}, u32[]{:S(2)}) async-start(bf16[8,128,1024]{2,1,0:T(8,128)(2,1)} %bitcast.71), calls=%async_computation | async-start | bytes 4194304 | tf_op jit(solution)/shard_map/all_to_all | solution.py:1044
  89.2 13.2 %expert_back.1.gh_ref = bf16[1024,4096]{1,0:T(8,128)(2,1)} custom-call(bf16[1024,1024]{1,0:T(8,128)(2,1)} %bitcast.67, bf16[1,4096,1024]{2,1,0:T(8,128)(2,1)} %wout_hbm.3), custom_call_target="tpu_custom_call" | custom-call | flops 429496736 | bytes 838860 | tf_op jit(solution)/shard_map/expert_back/pallas_call | solution.py:269
  104.8 4.0 %spread_rows.2 = bf16[8,1,128,1024]{3,2,1,0:T(8,128)(2,1)} custom-call(s32[1]{0:T(128)} %bitcast.21._, s32[4,1,512]{2,1,0:T(1,128)} %reshape.110.ids_ref, bf16[4,512,1152]{2,1,0:T(8,128)(2,1)} %bitcast.65), custom_call_target="tpu_custom_call" | custom-call | flops 53687092 | bytes 400000 | tf_op jit(solution)/shard_map/spread_rows/pallas_call | solution.py:609
  108.9 6.9 %all-to-all-done = bf16[8,128,1024]{2,1,0:T(8,128)(2,1)S(1)} async-done(((bf16[8,128,1024]{2,1,0:T(8,128)(2,1)}), bf16[8,128,1024]{2,1,0:T(8,128)(2,1)S(1)}, u32[]{:S(2)}, u32[]{:S(2)}) %all-to-all-start) | async-done | bytes 2097184 | tf_op jit(solution)/shard_map/all_to_all | solution.py:1044
  117.1 4.3 %all-to-all-start.2 = ((bf16[8,1,128,1024]{3,2,1,0:T(8,128)(2,1)}), bf16[8,1,128,1024]{3,2,1,0:T(8,128)(2,1)}, u32[]{:S(2)}, u32[]{:S(2)}) async-start(bf16[8,1,128,1024]{3,2,1,0:T(8,128)(2,1)} %spread_rows.2), calls=%async_computation.2 | async-start | bytes 4194304 | tf_op jit(solution)/shard_map/all_to_all | solution.py:1044
  122.2 25.4 %expert_front.1 = (bf16[1024,4096]{1,0:T(8,128)(2,1)}, bf16[1024,4096]{1,0:T(8,128)(2,1)}, bf16[1024,1024]{1,0:T(8,128)(2,1)}) custom-call(bf16[1024,1024]{1,0:T(8,128)(2,1)} %bitcast.59, bf16[1024,4096]{1,0:T(8,128)(2,1)} %expert_back.1.gh_ref, bf16[1,1024,4096]{2,1,0:T(8,128)(2,1)} %win_hbm.3), custom_call_target="tpu_custom_call" | custom-call | flops 858993472 | bytes 1677721 | tf_op jit(solution)/shard_map/expert_front/pallas_call | solution.py:316
  148.1 3.6 all-to-all-start.3
  152.3 14.6 %expert_produce.1.refs_0_ = bf16[1024,1024]{1,0:T(8,128)(2,1)} custom-call(bf16[1024,4096]{1,0:T(8,128)(2,1)} %get-tuple-element.115.hidden_ref, bf16[1,4096,1024]{2,1,0:T(8,128)(2,1)} %wout_hbm.3), custom_call_target="tpu_custom_call" | custom-call | flops 429496736 | bytes 838860 | tf_op jit(solution)/shard_map/expert_produce/pallas_call | solution.py:354
  167.0 7.6 %spread_rows.3 = bf16[8,3,128,1024]{3,2,1,0:T(8,128)(2,1)} custom-call(s32[2]{0:T(128)} %pad_add_fusion._, s32[4,1,512]{2,1,0:T(1,128)} %reshape.110.ids_ref, bf16[4,512,1152]{2,1,0:T(8,128)(2,1)} %bitcast.66, bf16[1024,1024]{1,0:T(8,128)(2,1)} %expert_produce.1.refs_0_), custom_call_target="tpu_custom_call" | custom-call | flops 161061280 | bytes 400000 | tf_op jit(solution)/shard_map/spread_rows/pallas_call | solution.py:609
  174.6 3.8 all-to-all-done.3
  179.7 4.9 %all-to-all-start.4 = ((bf16[8,3,128,1024]{3,2,1,0:T(8,128)(2,1)}), bf16[8,3,128,1024]{3,2,1,0:T(8,128)(2,1)}, u32[]{:S(2)}, u32[]{:S(2)}) async-start(bf16[8,3,128,1024]{3,2,1,0:T(8,128)(2,1)} %spread_rows.3), calls=%async_computation.4 | async-start | bytes 12582912 | tf_op jit(solution)/shard_map/all_to_all | solution.py:1044
  186.0 8.0 %resid_back.1 = (f32[512,1024]{1,0:T(8,128)}, bf16[512,1024]{1,0:T(8,128)(2,1)}, bf16[512,1024]{1,0:T(8,128)(2,1)}, f32[2,1024]{1,0:T(2,128)}) custom-call(bf16[1024,1024]{1,0:T(8,128)(2,1)} %bitcast.69, bf16[1024,512]{1,0:T(8,128)(2,1)} %fusion.1.spread_ref, f32[512,1024]{1,0:T(8,128)} %copy-done.2, f32[1,1024]{1,0:T(1,128)} %bitcast.80, ...), custom_call_target="tpu_custom_call" | custom-call | flops 107374184 | bytes 419430 | tf_op jit(solution)/shard_map/resid_back/pallas_call | solution.py:753
  194.0 34.1 %attend_back.1 = (bf16[512,1024]{1,0:T(8,128)(2,1)}, bf16[2,512,1024]{2,1,0:T(8,128)(2,1)}, bf16[2,512,1024]{2,1,0:T(8,128)(2,1)}, bf16[2,384,1024]{2,1,0:T(8,128)(2,1)}, bf16[2,384,1024]{2,1,0:T(8,128)(2,1)}) custom-call(f32[1]{0:T(128)} %bitcast.1.near_ref, bf16[512,1024]{1,0:T(8,128)(2,1)} %get-tuple-element.104.q_ref, ...), custom_call_target="tpu_custom_call" | custom-call | flops 1879048192 | bytes 943718 | tf_op jit(solution)/shard_map/attend_back/pallas_call | solution.py:995
  229.8 18.6 %weight_parts.1 = (bf16[4,4,4,32,1024]{4,3,2,1,0:T(8,128)(2,1)}, bf16[4,4,4,32,1024]{4,3,2,1,0:T(8,128)(2,1)}) custom-call(s32[1]{0:T(128)} %bitcast.odd_ref, bf16[512,1024]{1,0:T(8,128)(2,1)} %get-tuple-element.107.out_ref.refs_0_, bf16[1792,1024]{1,0:T(8,128)(2,1)} %get-tuple-element.108.refs_1_, bf16[512,1024]{1,0:T(8,128)(2,1)} %get-tuple-element.118.refs_2_, ...), custom_call_target="tpu_custom_call" | custom-call | flops 500000000 | bytes 1500000 | tf_op jit(solution)/shard_map/weight_parts/pallas_call | solution.py:710
  248.4 5.8 %own_out.1.own_ref = f32[1024,1024]{1,0:T(8,128)} custom-call(s32[1]{0:T(128)} %bitcast.25._.own_ref, bf16[1024,4096]{1,0:T(8,128)(2,1)} %get-tuple-element.115.hidden_ref, bf16[1024,1024]{1,0:T(8,128)(2,1)} %bitcast.68), custom_call_target="tpu_custom_call" | custom-call | flops 107374184 | bytes 400000 | tf_op jit(solution)/shard_map/own_out/pallas_call | solution.py:469
  254.2 2.0 all-to-all-done.4.far_hbm.far_ref
  256.5 1.9 slice.68
  258.4 3.3 add_convert_fusion
  265.0 2.3 add_convert_fusion.1
  267.3 3.5 collective-permute-done.11
  270.7 2.0 collective-permute-done.12
  272.7 5.4 %halve.2 = (bf16[2,4,2,32,1024]{4,3,2,1,0:T(8,128)(2,1)}, bf16[2,4,2,32,1024]{4,3,2,1,0:T(8,128)(2,1)}, bf16[2,4,2,32,1024]{4,3,2,1,0:T(8,128)(2,1)}, bf16[2,4,2,32,1024]{4,3,2,1,0:T(8,128)(2,1)}) custom-call(s32[1]{0:T(128)} %bitcast.27.own_ref, bf16[4,4,4,32,1024]{4,3,2,1,0:T(8,128)(2,1)} %get-tuple-element.134.refs_0_.refs_2_, ...), custom_call_target="tpu_custom_call" | custom-call | flops 104857 | bytes 629145 | tf_op jit(solution)/shard_map/halve/pallas_call | solution.py:159
  280.8 18.7 %in_sums.2 = (bf16[4,256,512]{2,1,0:T(8,128)(2,1)}, bf16[1024,512]{1,0:T(8,128)(2,1)}, bf16[2,1024,512]{2,1,0:T(8,128)(2,1)}) custom-call(s32[4]{0:T(128)} %pad_add_fusion.1.number_ref, bf16[1024,1024]{1,0:T(8,128)(2,1)} %bitcast.60, bf16[1024,4096]{1,0:T(8,128)(2,1)} %get-tuple-element.138.own_pre_ref, bf16[1,1024,4096]{2,1,0:T(8,128)(2,1)} %win_hbm.3, ...), custom_call_target="tpu_custom_call" | custom-call | flops 644245120 | bytes 800000 | tf_op jit(solution)/shard_map/in_sums/pallas_call | solution.py:423
  299.5 5.3 %all-to-all-start.5 = ((bf16[4,256,512]{2,1,0:T(8,128)(2,1)}), bf16[4,256,512]{2,1,0:T(8,128)(2,1)S(1)}, u32[]{:S(2)}, u32[]{:S(2)}) async-start(bf16[4,256,512]{2,1,0:T(8,128)(2,1)} %get-tuple-element.140), calls=%async_computation.5 | async-start | bytes 2097152 | tf_op jit(solution)/shard_map/all_to_all | solution.py:1142
  305.0 2.2 add_convert_fusion.6
  309.1 3.3 halve.3
  314.6 18.8 %in_sums.3 = (bf16[4,256,512]{2,1,0:T(8,128)(2,1)}, bf16[1024,512]{1,0:T(8,128)(2,1)}, bf16[2,1024,512]{2,1,0:T(8,128)(2,1)}) custom-call(s32[4]{0:T(128)} %pad_add_fusion.1.number_ref, bf16[1024,1024]{1,0:T(8,128)(2,1)} %bitcast.61, bf16[1024,4096]{1,0:T(8,128)(2,1)} %get-tuple-element.138.own_pre_ref, bf16[1,1024,4096]{2,1,0:T(8,128)(2,1)} %win_hbm.3, ...), custom_call_target="tpu_custom_call" | custom-call | flops 644245120 | bytes 800000 | tf_op jit(solution)/shard_map/in_sums/pallas_call | solution.py:423
  334.2 5.1 %all-to-all-start.6 = ((bf16[4,256,512]{2,1,0:T(8,128)(2,1)}), bf16[4,256,512]{2,1,0:T(8,128)(2,1)}, u32[]{:S(2)}, u32[]{:S(2)}) async-start(bf16[4,256,512]{2,1,0:T(8,128)(2,1)} %get-tuple-element.159), calls=%async_computation.6 | async-start | bytes 2097152 | tf_op jit(solution)/shard_map/all_to_all | solution.py:1142
  339.4 2.3 add_convert_fusion.5.prompt_ref
  341.6 10.6 %input_back.1 = (bf16[512,1024]{1,0:T(8,128)(2,1)}, f32[2,1024]{1,0:T(2,128)}) custom-call(bf16[2,128,1024]{2,1,0:T(8,128)(2,1)} %add_convert_fusion.5.prompt_ref, bf16[2,384,1024]{2,1,0:T(8,128)(2,1)} %get-tuple-element.125.refs_7_.own_ref, bf16[2,384,1024]{2,1,0:T(8,128)(2,1)} %collective-permute-done.9.near_ref, ...), custom_call_target="tpu_custom_call" | custom-call | flops 161061280 | bytes 524288 | tf_op jit(solution)/shard_map/input_back/pallas_call | solution.py:820
  352.3 2.7 turn.1
  355.0 2.0 collective-permute-start.19
  357.0 14.1 %out_sums.1 = f32[1,1024,1024]{2,1,0:T(8,128)} custom-call(f32[1024,1024]{1,0:T(8,128)} %own_out.1.own_ref, bf16[8,1,128,1024]{3,2,1,0:T(8,128)(2,1)} %all-to-all-done.2.near_hbm.near_ref, bf16[8,3,128,1024]{3,2,1,0:T(8,128)(2,1)} %all-to-all-done.4.far_hbm.far_ref, bf16[1024,512]{1,0:T(8,128)(2,1)} %get-tuple-element.172.refs_0_, ...), custom_call_target="tpu_custom_call" | custom-call | flops 322122560 | bytes 800000 | tf_op jit(solution)/shard_map/out_sums/pallas_call | solution.py:518
  371.7 2.1 collective-permute-start.20
  374.7 2.7 all-to-all-start.7
  377.4 4.2 %lay_out.1 = f32[1,256,4096]{2,1,0:T(8,128)} custom-call(bf16[4,256,512]{2,1,0:T(8,128)(2,1)} %copy-done.5, bf16[4,256,512]{2,1,0:T(8,128)(2,1)} %all-to-all-done.6.refs_1_), custom_call_target="tpu_custom_call" | custom-call | flops 52428 | bytes 314572 | tf_op jit(solution)/shard_map/lay_out/pallas_call | solution.py:549
  381.6 3.5 all-to-all-done.7
  (117 shorter events, 36.4 us)
Async XLA Ops:
  7.2 3.4 copy-start.6
  7.2 95.6 %all-gather.5.cloned.1.call-start = ((), (), s32[]{:S(2)}) async-start(), calls=%async_computation.8 | async-start | bytes 5898240 | tf_op jit(solution)/shard_map/all_gather | solution.py:1057
  10.5 6.6 %copy-start.15 = (s32[512,1]{0,1:T(1,128)S(1)}, s32[512,1]{0,1:T(1,128)}, u32[]{:S(2)}) copy-start(s32[512,1]{0,1:T(1,128)} %param.15) | copy-start | bytes 6148
  10.5 14.9 %copy-start.7 = (bf16[512,1024]{1,0:T(8,128)(2,1)S(1)}, bf16[512,1024]{1,0:T(8,128)(2,1)}, u32[]{:S(2)}) copy-start(bf16[512,1024]{1,0:T(8,128)(2,1)} %cot_ref.1) | copy-start | bytes 3145732
  10.6 17.3 %copy-start.8 = (bf16[384,1024]{1,0:T(8,128)(2,1)}, bf16[384,1024]{1,0:T(8,128)(2,1)S(1)}, u32[]{:S(2)}) copy-start(bf16[384,1024]{1,0:T(8,128)(2,1)S(1)} %slice.63.refs_9_) | copy-start | bytes 2359300
  10.6 12.3 %collective-permute-start.2 = (bf16[384,1024]{1,0:T(8,128)(2,1)S(1)}, bf16[384,1024]{1,0:T(8,128)(2,1)S(1)}, u32[]{:S(2)}, u32[]{:S(2)}) collective-permute-start(bf16[384,1024]{1,0:T(8,128)(2,1)S(1)} %slice.63.refs_9_), channel_id=1, source_target_pairs={{0,1},{2,3},{4,5},{6,7},{8,9},{10,11},{12,13},{14,15},{16,17},{18,... | collective-permute-start | bytes 2359304 | tf_op jit(solution)/shard_map/ppermute | solution.py:1050
  13.2 14.8 %copy-start.10 = (bf16[128,1024]{1,0:T(8,128)(2,1)}, bf16[128,1024]{1,0:T(8,128)(2,1)S(1)}, u32[]{:S(2)}) copy-start(bf16[128,1024]{1,0:T(8,128)(2,1)S(1)} %slice.62.refs_0_) | copy-start | bytes 786436
  13.2 8.3 %collective-permute-start = (bf16[128,1024]{1,0:T(8,128)(2,1)S(1)}, bf16[128,1024]{1,0:T(8,128)(2,1)}, u32[]{:S(2)}, u32[]{:S(2)}) collective-permute-start(bf16[128,1024]{1,0:T(8,128)(2,1)S(1)} %slice.62.refs_0_), channel_id=1, source_target_pairs={{0,2},{1,3},{2,0},{3,1},{4,6},{5,7},{6,4},{7,5},{8,10},{9,11},{10,... | collective-permute-start | bytes 786440 | tf_op jit(solution)/shard_map/ppermute | solution.py:25
  15.6 7.4 %collective-permute-start.1 = (bf16[128,1024]{1,0:T(8,128)(2,1)S(1)}, bf16[128,1024]{1,0:T(8,128)(2,1)}, u32[]{:S(2)}, u32[]{:S(2)}) collective-permute-start(bf16[128,1024]{1,0:T(8,128)(2,1)S(1)} %slice.62.refs_0_), channel_id=1, source_target_pairs={{0,4},{1,5},{2,6},{3,7},{4,0},{5,1},{6,2},{7,3},{8,12},{9,13},{10,... | collective-permute-start | bytes 786440 | tf_op jit(solution)/shard_map/ppermute | solution.py:25
  17.1 18.4 %collective-permute-start.4 = (bf16[128,1024]{1,0:T(8,128)(2,1)S(1)}, bf16[128,1024]{1,0:T(8,128)(2,1)}, u32[]{:S(2)}, u32[]{:S(2)}) collective-permute-start(bf16[128,1024]{1,0:T(8,128)(2,1)S(1)} %slice.62.refs_0_), channel_id=1, source_target_pairs={{0,1},{1,0},{2,3},{3,2},{4,5},{5,4},{6,7},{7,6},{8,9},{9,8},{10,11... | collective-permute-start | bytes 786440 | tf_op jit(solution)/shard_map/ppermute | solution.py:25
  23.9 6.7 %collective-permute-start.3 = (bf16[128,1024]{1,0:T(8,128)(2,1)}, bf16[128,1024]{1,0:T(8,128)(2,1)}, u32[]{:S(2)}, u32[]{:S(2)}) collective-permute-start(bf16[128,1024]{1,0:T(8,128)(2,1)} %collective-permute-done.refs_1_), channel_id=1, source_target_pairs={{0,4},{1,5},{2,6},{3,7},{4,0},{5,1},{6,2},{7,3},{8,12},{9,13},{10,... | collective-permute-start | bytes 786440 | tf_op jit(solution)/shard_map/ppermute | solution.py:25
  28.1 7.4 %collective-permute-start.5 = (bf16[128,1024]{1,0:T(8,128)(2,1)}, bf16[128,1024]{1,0:T(8,128)(2,1)}, u32[]{:S(2)}, u32[]{:S(2)}) collective-permute-start(bf16[128,1024]{1,0:T(8,128)(2,1)} %collective-permute-done.refs_1_), channel_id=1, source_target_pairs={{0,1},{1,0},{2,3},{3,2},{4,5},{5,4},{6,7},{7,6},{8,9},{9,8},{10,11... | collective-permute-start | bytes 786440 | tf_op jit(solution)/shard_map/ppermute | solution.py:25
  28.1 7.4 %collective-permute-start.6 = (bf16[128,1024]{1,0:T(8,128)(2,1)}, bf16[128,1024]{1,0:T(8,128)(2,1)}, u32[]{:S(2)}, u32[]{:S(2)}) collective-permute-start(bf16[128,1024]{1,0:T(8,128)(2,1)} %collective-permute-done.1.refs_2_), channel_id=1, source_target_pairs={{0,1},{1,0},{2,3},{3,2},{4,5},{5,4},{6,7},{7,6},{8,9},{9,8},{10,11... | collective-permute-start | bytes 786440 | tf_op jit(solution)/shard_map/ppermute | solution.py:25
  30.6 5.0 %collective-permute-start.7 = (bf16[128,1024]{1,0:T(8,128)(2,1)}, bf16[128,1024]{1,0:T(8,128)(2,1)}, u32[]{:S(2)}, u32[]{:S(2)}) collective-permute-start(bf16[128,1024]{1,0:T(8,128)(2,1)} %collective-permute-done.3.refs_3_), channel_id=1, source_target_pairs={{0,1},{1,0},{2,3},{3,2},{4,5},{5,4},{6,7},{7,6},{8,9},{9,8},{10,11... | collective-permute-start | bytes 786440 | tf_op jit(solution)/shard_map/ppermute | solution.py:25
  30.6 52.6 %all-to-all-start.1 = ((bf16[8,128,1024]{2,1,0:T(8,128)(2,1)}), bf16[8,128,1024]{2,1,0:T(8,128)(2,1)S(1)}, u32[]{:S(2)}, u32[]{:S(2)}) async-start(bf16[8,128,1024]{2,1,0:T(8,128)(2,1)} %bitcast.70), calls=%async_computation.1 | async-start | bytes 4194304 | tf_op jit(solution)/shard_map/all_to_all | solution.py:1044
  78.9 1.3 copy-start.2
  78.9 1.3 copy-start.18
  78.9 1.3 copy-start.19
  83.1 1.4 copy-start.1
  84.5 31.3 %all-to-all-start = ((bf16[8,128,1024]{2,1,0:T(8,128)(2,1)}), bf16[8,128,1024]{2,1,0:T(8,128)(2,1)S(1)}, u32[]{:S(2)}, u32[]{:S(2)}) async-start(bf16[8,128,1024]{2,1,0:T(8,128)(2,1)} %bitcast.71), calls=%async_computation | async-start | bytes 4194304 | tf_op jit(solution)/shard_map/all_to_all | solution.py:1044
  115.8 1.3 copy-start
  117.1 31.0 %all-to-all-start.2 = ((bf16[8,1,128,1024]{3,2,1,0:T(8,128)(2,1)}), bf16[8,1,128,1024]{3,2,1,0:T(8,128)(2,1)}, u32[]{:S(2)}, u32[]{:S(2)}) async-start(bf16[8,1,128,1024]{3,2,1,0:T(8,128)(2,1)} %spread_rows.2), calls=%async_computation.2 | async-start | bytes 4194304 | tf_op jit(solution)/shard_map/all_to_all | solution.py:1044
  121.5 159.3 %all-gather.7.cloned.1.call-start = ((), (), s32[]{:S(2)}) async-start(), calls=%async_computation.9 | async-start | bytes 10485760 | tf_op jit(solution)/shard_map/all_gather | solution.py:1094
  148.1 30.2 %all-to-all-start.3 = ((bf16[8,128,1024]{2,1,0:T(8,128)(2,1)}), bf16[8,128,1024]{2,1,0:T(8,128)(2,1)S(1)}, u32[]{:S(2)}, u32[]{:S(2)}) async-start(bf16[8,128,1024]{2,1,0:T(8,128)(2,1)} %bitcast.72), calls=%async_computation.3 | async-start | bytes 4194304 | tf_op jit(solution)/shard_map/all_to_all | solution.py:1044
  179.7 76.5 %all-to-all-start.4 = ((bf16[8,3,128,1024]{3,2,1,0:T(8,128)(2,1)}), bf16[8,3,128,1024]{3,2,1,0:T(8,128)(2,1)}, u32[]{:S(2)}, u32[]{:S(2)}) async-start(bf16[8,3,128,1024]{3,2,1,0:T(8,128)(2,1)} %spread_rows.3), calls=%async_computation.4 | async-start | bytes 12582912 | tf_op jit(solution)/shard_map/all_to_all | solution.py:1044
  228.0 26.1 %collective-permute-start.8 = (bf16[2,512,1024]{2,1,0:T(8,128)(2,1)}, bf16[2,512,1024]{2,1,0:T(8,128)(2,1)S(1)}, u32[]{:S(2)}, u32[]{:S(2)}) collective-permute-start(bf16[2,512,1024]{2,1,0:T(8,128)(2,1)} %get-tuple-element.123.refs_5_), channel_id=1, source_target_pairs={{0,1},{1,0},{2,3},{3,2},{4,5},{5,4},{6,7},{7,6},{8,9},{9,8},{10,11... | collective-permute-start | bytes 6291464 | tf_op jit(solution)/shard_map/ppermute | solution.py:25
  228.5 25.7 %collective-permute-start.9 = (bf16[2,384,1024]{2,1,0:T(8,128)(2,1)}, bf16[2,384,1024]{2,1,0:T(8,128)(2,1)}, u32[]{:S(2)}, u32[]{:S(2)}) collective-permute-start(bf16[2,384,1024]{2,1,0:T(8,128)(2,1)} %get-tuple-element.124.refs_6_), channel_id=1, source_target_pairs={{1,0},{3,2},{5,4},{7,6},{9,8},{11,10},{13,12},{15,14},{17,16},{19,... | collective-permute-start | bytes 4718600 | tf_op jit(solution)/shard_map/ppermute | solution.py:1113
  254.2 2.3 copy-start.9
  256.2 16.5 %collective-permute-start.10 = (bf16[4,4,4,32,1024]{4,3,2,1,0:T(8,128)(2,1)}, bf16[4,4,4,32,1024]{4,3,2,1,0:T(8,128)(2,1)}, u32[]{:S(2)}, u32[]{:S(2)}) collective-permute-start(bf16[4,4,4,32,1024]{4,3,2,1,0:T(8,128)(2,1)} %get-tuple-element.130), channel_id=1, source_target_pairs={{0,1},{1,0},{2,3},{3,2},{4,5},{5,4},{6,7},{7,6},{8,9},{9,8},{10,11... | collective-permute-start | bytes 12582920 | tf_op jit(solution)/shard_map/ppermute | solution.py:25
  258.4 6.6 %copy-start.3 = (f32[512,1024]{1,0:T(8,128)S(1)}, f32[512,1024]{1,0:T(8,128)}, u32[]{:S(2)}) copy-start(f32[512,1024]{1,0:T(8,128)} %copy-done.2) | copy-start | bytes 6291460
  261.8 8.9 %collective-permute-start.11 = (bf16[2,64,1024]{2,1,0:T(8,128)(2,1)S(1)}, bf16[2,64,1024]{2,1,0:T(8,128)(2,1)S(1)}, u32[]{:S(2)}, u32[]{:S(2)}) collective-permute-start(bf16[2,64,1024]{2,1,0:T(8,128)(2,1)S(1)} %get-tuple-element.189), channel_id=1, source_target_pairs={{0,4},{1,5},{2,6},{3,7},{4,0},{5,1},{6,2},{7,3},{8,12},{9,13},{10,... | collective-permute-start | bytes 786440 | tf_op jit(solution)/shard_map/ppermute | solution.py:25
  263.5 9.2 %collective-permute-start.12 = (bf16[2,64,1024]{2,1,0:T(8,128)(2,1)S(1)}, bf16[2,64,1024]{2,1,0:T(8,128)(2,1)S(1)}, u32[]{:S(2)}, u32[]{:S(2)}) collective-permute-start(bf16[2,64,1024]{2,1,0:T(8,128)(2,1)S(1)} %get-tuple-element.188), channel_id=1, source_target_pairs={{0,2},{1,3},{2,0},{3,1},{4,6},{5,7},{6,4},{7,5},{8,10},{9,11},{10,... | collective-permute-start | bytes 786440 | tf_op jit(solution)/shard_map/ppermute | solution.py:25
  272.7 5.4 %copy-start.14 = (bf16[2,64,1024]{2,1,0:T(8,128)(2,1)}, bf16[2,64,1024]{2,1,0:T(8,128)(2,1)S(1)}, u32[]{:S(2)}) copy-start(bf16[2,64,1024]{2,1,0:T(8,128)(2,1)S(1)} %collective-permute-done.12) | copy-start | bytes 786436
  278.1 26.7 %collective-permute-start.13 = (bf16[2,4,2,32,1024]{4,3,2,1,0:T(8,128)(2,1)}, bf16[2,4,2,32,1024]{4,3,2,1,0:T(8,128)(2,1)}, u32[]{:S(2)}, u32[]{:S(2)}) collective-permute-start(bf16[2,4,2,32,1024]{4,3,2,1,0:T(8,128)(2,1)} %get-tuple-element.141), channel_id=1, source_target_pairs={{0,2},{1,3},{2,0},{3,1},{4,6},{5,7},{6,4},{7,5},{8,10},{9,11},{10,... | collective-permute-start | bytes 3145736 | tf_op jit(solution)/shard_map/ppermute | solution.py:25
  279.7 25.3 %collective-permute-start.14 = (bf16[2,4,2,32,1024]{4,3,2,1,0:T(8,128)(2,1)}, bf16[2,4,2,32,1024]{4,3,2,1,0:T(8,128)(2,1)}, u32[]{:S(2)}, u32[]{:S(2)}) collective-permute-start(bf16[2,4,2,32,1024]{4,3,2,1,0:T(8,128)(2,1)} %get-tuple-element.142), channel_id=1, source_target_pairs={{0,4},{1,5},{2,6},{3,7},{4,0},{5,1},{6,2},{7,3},{8,12},{9,13},{10,... | collective-permute-start | bytes 3145736 | tf_op jit(solution)/shard_map/ppermute | solution.py:25
  299.5 34.7 %all-to-all-start.5 = ((bf16[4,256,512]{2,1,0:T(8,128)(2,1)}), bf16[4,256,512]{2,1,0:T(8,128)(2,1)S(1)}, u32[]{:S(2)}, u32[]{:S(2)}) async-start(bf16[4,256,512]{2,1,0:T(8,128)(2,1)} %get-tuple-element.140), calls=%async_computation.5 | async-start | bytes 2097152 | tf_op jit(solution)/shard_map/all_to_all | solution.py:1142
  307.2 26.2 %collective-permute-start.15 = (bf16[2,128,1024]{2,1,0:T(8,128)(2,1)}, bf16[2,128,1024]{2,1,0:T(8,128)(2,1)}, u32[]{:S(2)}, u32[]{:S(2)}) collective-permute-start(bf16[2,128,1024]{2,1,0:T(8,128)(2,1)} %get-tuple-element.187), channel_id=1, source_target_pairs={{0,2},{1,3},{2,0},{3,1},{4,6},{5,7},{6,4},{7,5},{8,10},{9,11},{10,... | collective-permute-start | bytes 1572872 | tf_op jit(solution)/shard_map/ppermute | solution.py:25
  307.8 25.6 %collective-permute-start.16 = (bf16[2,128,1024]{2,1,0:T(8,128)(2,1)}, bf16[2,128,1024]{2,1,0:T(8,128)(2,1)}, u32[]{:S(2)}, u32[]{:S(2)}) collective-permute-start(bf16[2,128,1024]{2,1,0:T(8,128)(2,1)} %get-tuple-element.186), channel_id=1, source_target_pairs={{0,4},{1,5},{2,6},{3,7},{4,0},{5,1},{6,2},{7,3},{8,12},{9,13},{10,... | collective-permute-start | bytes 1572872 | tf_op jit(solution)/shard_map/ppermute | solution.py:25
  312.4 21.0 %collective-permute-start.17 = (bf16[2,4,1,32,1024]{4,3,2,1,0:T(8,128)(2,1)}, bf16[2,4,1,32,1024]{4,3,2,1,0:T(8,128)(2,1)S(1)}, u32[]{:S(2)}, u32[]{:S(2)}) collective-permute-start(bf16[2,4,1,32,1024]{4,3,2,1,0:T(8,128)(2,1)} %get-tuple-element.153), channel_id=1, source_target_pairs={{0,4},{1,5},{2,6},{3,7},{4,0},{5,1},{6,2},{7,3},{8,12},{9,13},{10,... | collective-permute-start | bytes 1572872 | tf_op jit(solution)/shard_map/ppermute | solution.py:25
  313.1 21.1 %collective-permute-start.18 = (bf16[2,4,1,32,1024]{4,3,2,1,0:T(8,128)(2,1)}, bf16[2,4,1,32,1024]{4,3,2,1,0:T(8,128)(2,1)}, u32[]{:S(2)}, u32[]{:S(2)}) collective-permute-start(bf16[2,4,1,32,1024]{4,3,2,1,0:T(8,128)(2,1)} %get-tuple-element.154), channel_id=1, source_target_pairs={{0,2},{1,3},{2,0},{3,1},{4,6},{5,7},{6,4},{7,5},{8,10},{9,11},{10,... | collective-permute-start | bytes 1572872 | tf_op jit(solution)/shard_map/ppermute | solution.py:25
  334.2 7.4 %copy-start.5 = (bf16[4,256,512]{2,1,0:T(8,128)(2,1)}, bf16[4,256,512]{2,1,0:T(8,128)(2,1)S(1)}, u32[]{:S(2)}) copy-start(bf16[4,256,512]{2,1,0:T(8,128)(2,1)S(1)} %all-to-all-done.5.refs_0_) | copy-start | bytes 3145732
  334.2 37.3 %all-to-all-start.6 = ((bf16[4,256,512]{2,1,0:T(8,128)(2,1)}), bf16[4,256,512]{2,1,0:T(8,128)(2,1)}, u32[]{:S(2)}, u32[]{:S(2)}) async-start(bf16[4,256,512]{2,1,0:T(8,128)(2,1)} %get-tuple-element.159), calls=%async_computation.6 | async-start | bytes 2097152 | tf_op jit(solution)/shard_map/all_to_all | solution.py:1142
  355.0 16.5 %collective-permute-start.19 = (bf16[4,2,32,1024]{3,2,1,0:T(8,128)(2,1)}, bf16[4,2,32,1024]{3,2,1,0:T(8,128)(2,1)S(1)}, u32[]{:S(2)}, u32[]{:S(2)}) collective-permute-start(bf16[4,2,32,1024]{3,2,1,0:T(8,128)(2,1)} %get-tuple-element.179), channel_id=1, source_target_pairs={{0,8},{8,0},{16,24},{24,16},{1,9},{9,1},{17,25},{25,17},{2,10},{10... | collective-permute-start | bytes 1572872 | tf_op jit(solution)/shard_map/ppermute | solution.py:25
  357.0 14.1 %copy-start.16 = (f32[2,1024]{1,0:T(2,128)S(1)}, f32[2,1024]{1,0:T(2,128)}, u32[]{:S(2)}) copy-start(f32[2,1024]{1,0:T(2,128)} %get-tuple-element.170) | copy-start | bytes 24580
  357.0 14.1 %copy-start.17 = (f32[2,1024]{1,0:T(2,128)S(1)}, f32[2,1024]{1,0:T(2,128)}, u32[]{:S(2)}) copy-start(f32[2,1024]{1,0:T(2,128)} %get-tuple-element.169) | copy-start | bytes 24580
  357.0 14.5 %copy-start.13 = (bf16[4,2,32,1024]{3,2,1,0:T(8,128)(2,1)S(1)}, bf16[4,2,32,1024]{3,2,1,0:T(8,128)(2,1)}, u32[]{:S(2)}) copy-start(bf16[4,2,32,1024]{3,2,1,0:T(8,128)(2,1)} %get-tuple-element.181) | copy-start | bytes 1572868
  371.7 15.2 %collective-permute-start.20 = (bf16[4,32,1024]{2,1,0:T(8,128)(2,1)S(1)}, bf16[4,32,1024]{2,1,0:T(8,128)(2,1)S(1)}, u32[]{:S(2)}, u32[]{:S(2)}) collective-permute-start(bf16[4,32,1024]{2,1,0:T(8,128)(2,1)S(1)} %dynamic-slice_bitcast_fusion), channel_id=1, source_target_pairs={{0,16},{8,24},{16,0},{24,8},{1,17},{9,25},{17,1},{25,9},{2,18},{10... | collective-permute-start | bytes 786440 | tf_op jit(solution)/shard_map/ppermute | solution.py:25
  374.7 10.4 %all-to-all-start.7 = ((f32[32,1,128]{2,1,0:T(1,128)}), f32[32,1,128]{2,1,0:T(1,128)S(1)}, u32[]{:S(2)}, u32[]{:S(2)}) async-start(f32[32,1,128]{2,1,0:T(1,128)} %reshape.113), calls=%async_computation.7 | async-start | bytes 32768 | tf_op jit(solution)/shard_map/all_to_all | solution.py:243
  (3 other events, 3.0 us)
Sparse Core Ops, SparseCore 0:
  10.7 92.0 all-gather.4
  123.9 151.2 all-gather.6
